TPU v7x, 256 devices: a whole 4x4x8 slice. The times are simulated.
256 devices in a mesh: dp: 16 (over z_lo, x), shard: 16 (over z_hi, y, core).
Axes of the slice: x: 4, y: 4, z: 8 (z_hi: 2, z_lo: 4; z = z_hi * 4 + z_lo), core: 2. Of those that a mesh axis runs over, the one named last changes fastest.
Arguments:
- hidden_in: bfloat16 [65536, 5120], P(('dp', 'shard')), may hold values from -24 to 24
- teacher: bfloat16 [65536, 768], P(('dp', 'shard')), may hold values from -6 to 6
- norm_gain: bfloat16 [5120], P('shard'), may hold values from 0.5 to 1.5
- w_key: bfloat16 [5120, 768], P('shard'), may hold values from -0.078125 to 0.078125
- group_rows: int32 [16], P('dp'), may hold values from 64 to 256
- member: int32 [16, 16], P('dp', 'shard'), may hold values from 0 to 1, as said below
Outputs:
- loss: float32 [], replicated
- grad_gain: float32 [5120], P('shard')
- grad_key: float32 [5120, 768], P('shard')
Inputs may be any that keep to these rules, and one draw needn't show every extreme that they name: The first group_rows[p] token slots of each surviving device of group p hold valid tokens. `member`: 1 marks a surviving device; the first device of every group survives.
All inputs are finite; a program needn't handle non-finite values.
Results may differ from a plain program's by a relative error of at most 0.0023.
Values may be sent and summed in bfloat16 or wider, within the bound.
No kernel may reach another device: no remote copies, remote signals or barrier semaphores. Data moves between devices by JAX's collectives and lax.ppermute only.
A program may use at most 128 MiB of HBM per device.

v0:
```python
import jax
import jax.numpy as jnp
from jax import lax
from jax.sharding import Mesh
from jax.sharding import PartitionSpec as P

ZL, X, ZH, Y, C = "dp_0", "dp_1", "shard_0", "shard_1", "shard_2"
SHARD = (ZH, Y, C)
DP_SHARD = (ZL, X, ZH, Y, C)
DP = (ZL, X)

EPSILON = 1e-06
SCALE = 1024.0


def fetch(value, axis, step):
    n = lax.axis_size(axis)
    return lax.ppermute(value, axis, [((i + step) % n, i) for i in range(n)])


def ring_blocks(value, axis):
    one, three, two = (fetch(value, axis, step) for step in (1, 3, 2))
    return [value, one, two, three]


def from_everyone(value, axes):
    copies = jnp.broadcast_to(value, (lax.axis_size(axes), *value.shape))
    return lax.all_to_all(copies, axes, split_axis=0, concat_axis=0, tiled=True)


def summed(value, axes):
    tile = jnp.broadcast_to(value, (8, 128))
    return from_everyone(tile, axes)[:, 0, 0].sum()


def block(value, *places):
    starts = [0 if at is None else at for at in places] + [0] * (value.ndim - len(places))
    sizes = [size if at is None else 1 for at, size in zip(places, value.shape)] + list(value.shape[len(places) :])
    kept = [size for at, size in zip(places, value.shape) if at is None] + list(value.shape[len(places) :])
    return lax.dynamic_slice(value, starts, sizes).reshape(kept)


def rows_by(left, right):
    return lax.dot_general(left, right, (((0,), (0,)), ((), ())), preferred_element_type=jnp.float32)


def body(hidden_in, teacher, norm_gain, w_key, group_rows, member):
    rows, width = hidden_in.shape
    own, features = w_key.shape
    part = own // 4
    x, y, zh, core = (lax.axis_index(name) for name in (X, Y, ZH, C))

    other = fetch(lax.dynamic_slice_in_dim(w_key, x * part, part), ZH, 1)
    near = ring_blocks(w_key, Y)
    quarter = jnp.zeros((4, part, features), w_key.dtype)
    for step, piece in enumerate(ring_blocks(other, Y)):
        quarter = lax.dynamic_update_index_in_dim(quarter, piece, (y + step) & 3, 0)
    far = [block.reshape(own, features) for block in ring_blocks(quarter, X)]

    live_rows = group_rows[0]
    alive = member[0, 0]
    own_count = (alive * live_rows).astype(jnp.float32)
    gain_rows = jnp.pad(norm_gain.astype(jnp.float32), (0, 384 - own)).reshape(3, 128)
    tile = jnp.concatenate([gain_rows, jnp.broadcast_to(own_count, (5, 128))])
    tiles = from_everyone(tile, SHARD)
    gains = tiles[:, :3].reshape(-1, 384)[:, :own].reshape(width)
    total_count = summed(tiles[:, 3, 0].sum(), DP)

    values = hidden_in.astype(jnp.float32)
    inverse_rms = lax.rsqrt(jnp.mean(values * values, axis=1, keepdims=True) + EPSILON)
    normed = (values * inverse_rms * gains).astype(jnp.bfloat16)

    turned = normed.T.reshape(2, 4, 2, 4, part, rows)
    theirs = fetch(block(turned, None, None, 1 - core), C, 1)
    pair = jnp.concatenate([block(turned, None, None, core), theirs], axis=-1)
    near_half = [block(pair, zh, (y + s) & 3).reshape(own, -1) for s in range(4)]
    far_half = [block(pair, 1 - zh, None, (x + s) & 3).reshape(own, -1) for s in range(4)]
    near_cols = [block(turned, zh, (y + s) & 3).reshape(2 * own, rows) for s in range(4)]
    far_cols = [block(turned, 1 - zh, None, None, (x + s) & 3).reshape(2 * own, rows) for s in range(4)]

    halves = rows_by(jnp.concatenate(near_half), jnp.concatenate(near)) + rows_by(far_half[0], far[0])
    halves += sum(rows_by(far_half[i], far[i]) for i in (1, 3, 2))
    keys = halves[:rows] + fetch(halves[rows:], C, 1)

    position = lax.broadcasted_iota(jnp.int32, (rows, 1), 0)
    valid = jnp.where((position < live_rows) & (alive == 1), 1.0, 0.0).astype(jnp.float32)
    diff = keys - teacher.astype(jnp.float32)
    own_sum = jnp.sum(valid * diff * diff)
    upstream = (SCALE / total_count * valid * diff).astype(jnp.bfloat16)

    near_in = [near_cols[0]] + [fetch(near_cols[4 - s], Y, s) for s in (1, 2, 3)]
    far_in = [far_cols[0]] + [fetch(far_cols[4 - s], X, s) for s in (1, 2, 3)]
    near_up = ring_blocks(upstream, Y)
    far_up = ring_blocks(upstream, X)

    def pooled(left, up):
        first = jnp.dot(
            jnp.concatenate([left[i] for i in (0, 1, 3)], axis=1),
            jnp.concatenate([up[i] for i in (0, 1, 3)]),
            preferred_element_type=jnp.float32,
        )
        return first + jnp.dot(left[2], up[2], preferred_element_type=jnp.float32)

    near_out = pooled(near_in, near_up).reshape(2, 4, part, features)
    near_out = block(near_out, core) + fetch(block(near_out, 1 - core), C, 1)
    far_out = pooled(far_in, far_up).reshape(4, 2, part, features)
    far_out = block(far_out, None, core) + fetch(block(far_out, None, 1 - core), C, 1)
    near_sum = block(near_out, x) + sum(fetch(block(near_out, (x - s) & 3), X, s) for s in (1, 2, 3))
    far_sum = block(far_out, y) + sum(fetch(block(far_out, (y - s) & 3), Y, s) for s in (1, 2, 3))
    both = jnp.where(zh == 0, jnp.stack([near_sum, far_sum]), jnp.stack([far_sum, near_sum]))

    tall, wide = part // 16, features // 256
    pieces = both.reshape(2, 2, tall, 8, 2, wide, 128).transpose(0, 1, 4, 2, 5, 3, 6).reshape(8, -1, 128)
    pieces = lax.all_to_all(pieces, (ZH, ZL), split_axis=0, concat_axis=0, tiled=True)
    group_sum = summed(own_sum, SHARD)
    piece = jnp.concatenate([pieces.sum(axis=0), jnp.broadcast_to(group_sum, (8, 128))])
    whole = from_everyone(piece, DP)
    loss = whole[:, -8, 0].sum() / (2.0 * features * total_count)
    whole = whole[:, :-8].reshape(2, 2, 4, tall, wide, 8, 128)
    grad_key = whole.transpose(2, 0, 3, 5, 1, 4, 6).reshape(own, features)
    grad_gain = jnp.sum(w_key.astype(jnp.float32) * grad_key, axis=1) / norm_gain.astype(jnp.float32)
    return (loss, grad_gain, grad_key)


def solution(mesh):
    split = Mesh(mesh.devices.reshape(4, 4, 2, 4, 2), DP_SHARD)
    return jax.shard_map(
        body,
        mesh=split,
        in_specs=(
            P(DP_SHARD, None),
            P(DP_SHARD, None),
            P(SHARD),
            P(SHARD, None),
            P(DP),
            P(DP, SHARD),
        ),
        out_specs=(P(), P(SHARD), P(SHARD, None)),
        check_vma=False,
    )
```

profile of v0, /device:TPU:32, one launch (start us, length us, event | category | flops | bytes accessed | tf_op | source)
XLA Modules:
  0.0 232.7 jit_solution(4113142368576541671)
XLA Ops:
  3.3 10.3 %all-to-all-start = ((f32[16,8,128]{2,1,0:T(8,128)}), f32[16,8,128]{2,1,0:T(8,128)S(1)}, u32[]{:S(2)}, u32[]{:S(2)}) async-start(f32[16,8,128]{2,1,0:T(8,128)} %broadcast_in_dim.33), calls=%async_computation | async-start | bytes 131072 | tf_op jit(solution)/shard_map/all_to_all | solution.py:28
  14.5 5.9 %collective-permute-start.6 = (bf16[80,768]{1,0:T(8,128)(2,1)S(1)}, bf16[80,768]{1,0:T(8,128)(2,1)S(1)}, u32[]{:S(2)}, u32[]{:S(2)}) collective-permute-start(bf16[80,768]{1,0:T(8,128)(2,1)S(1)} %constant_dynamic-slice_fusion.5), channel_id=1, source_target_pairs={{8,0},{0,8},{9,1},{1,9},{10,2},{2,10},{11,3},{3,11},{12,4},{4,12},... | collective-permute-start | bytes 368648 | tf_op jit(solution)/shard_map/ppermute | solution.py:18
  20.4 3.0 %copy.16 = bf16[256,5120]{0,1:T(8,128)(2,1)S(1)} copy(bf16[256,5120]{1,0:T(8,128)(2,1)} %param.6) | data formatting | bytes 5242880 | tf_op args[0]
  28.2 2.7 %collective-permute-start.7 = (bf16[80,768]{1,0:T(8,128)(2,1)S(1)}, bf16[80,768]{1,0:T(8,128)(2,1)S(1)}, u32[]{:S(2)}, u32[]{:S(2)}) collective-permute-start(bf16[80,768]{1,0:T(8,128)(2,1)S(1)} %collective-permute-done.6), channel_id=1, source_target_pairs={{2,0},{4,2},{6,4},{0,6},{3,1},{5,3},{7,5},{1,7},{10,8},{12,10},{14... | collective-permute-start | bytes 368648 | tf_op jit(solution)/shard_map/ppermute | solution.py:18
  32.7 4.1 %collective-permute-done.7 = bf16[80,768]{1,0:T(8,128)(2,1)S(1)} collective-permute-done((bf16[80,768]{1,0:T(8,128)(2,1)S(1)}, bf16[80,768]{1,0:T(8,128)(2,1)S(1)}, u32[]{:S(2)}, u32[]{:S(2)}) %collective-permute-start.7) | collective-permute-done | bytes 122912 | tf_op jit(solution)/shard_map/ppermute | solution.py:18
  40.5 2.8 %collective-permute-start.10 = (bf16[4,80,768]{2,1,0:T(8,128)(2,1)S(1)}, bf16[4,80,768]{2,1,0:T(8,128)(2,1)}, u32[]{:S(2)}, u32[]{:S(2)}) collective-permute-start(bf16[4,80,768]{2,1,0:T(8,128)(2,1)S(1)} %bitcast_dynamic-update-slice_fusion), channel_id=1, source_target_pairs={{16,0},{32,16},{48,32},{0,48},{17,1},{33,17},{49,33},{1,49},{18,2}... | collective-permute-start | bytes 1474568 | tf_op jit(solution)/shard_map/ppermute | solution.py:18
  45.8 8.3 %collective-permute-done.10 = bf16[4,80,768]{2,1,0:T(8,128)(2,1)} collective-permute-done((bf16[4,80,768]{2,1,0:T(8,128)(2,1)S(1)}, bf16[4,80,768]{2,1,0:T(8,128)(2,1)}, u32[]{:S(2)}, u32[]{:S(2)}) %collective-permute-start.10) | collective-permute-done | bytes 491552 | tf_op jit(solution)/shard_map/ppermute | solution.py:18
  54.0 2.9 %collective-permute-start.12 = (bf16[4,80,768]{2,1,0:T(8,128)(2,1)S(1)}, bf16[4,80,768]{2,1,0:T(8,128)(2,1)S(1)}, u32[]{:S(2)}, u32[]{:S(2)}) collective-permute-start(bf16[4,80,768]{2,1,0:T(8,128)(2,1)S(1)} %bitcast_dynamic-update-slice_fusion), channel_id=1, source_target_pairs={{32,0},{48,16},{0,32},{16,48},{33,1},{49,17},{1,33},{17,49},{34,2}... | collective-permute-start | bytes 1474568 | tf_op jit(solution)/shard_map/ppermute | solution.py:18
  58.5 9.6 %collective-permute-done.11 = bf16[4,80,768]{2,1,0:T(8,128)(2,1)} collective-permute-done((bf16[4,80,768]{2,1,0:T(8,128)(2,1)S(1)}, bf16[4,80,768]{2,1,0:T(8,128)(2,1)}, u32[]{:S(2)}, u32[]{:S(2)}) %collective-permute-start.11) | collective-permute-done | bytes 491552 | tf_op jit(solution)/shard_map/ppermute | solution.py:18
  77.2 5.0 %all-to-all-start.1 = ((f32[16,8,128]{2,1,0:T(8,128)}), f32[16,8,128]{2,1,0:T(8,128)S(1)}, u32[]{:S(2)}, u32[]{:S(2)}) async-start(f32[16,8,128]{2,1,0:T(8,128)} %broadcast_in_dim_broadcast_in_dim.6), calls=%async_computation.1 | async-start | bytes 131072 | tf_op jit(solution)/shard_map/all_to_all | solution.py:28
  84.2 4.7 %all-to-all-done.1 = f32[16,8,128]{2,1,0:T(8,128)S(1)} async-done(((f32[16,8,128]{2,1,0:T(8,128)}), f32[16,8,128]{2,1,0:T(8,128)S(1)}, u32[]{:S(2)}, u32[]{:S(2)}) %all-to-all-start.1) | async-done | bytes 65568 | tf_op jit(solution)/shard_map/all_to_all | solution.py:28
  90.2 2.5 %fusion.36 = (f32[]{:T(128)}, bf16[256,768]{1,0:T(8,128)(2,1)S(1)}) fusion(f32[256]{0:T(256)S(1)} %get-tuple-element.29, bf16[256,768]{1,0:T(8,128)(2,1)} %param.7, f32[256,768]{1,0:T(8,128)} %collective-permute-done.13, f32[512,768]{1,0:T(8,128)} %copy-done.2, f32[256]{0:T(256)S(1)} %get-tuple-element.30), kind=kLoop, calls=%fused_computation.65 | loop fusion | flops 1572863 | bytes 2361348 | tf_op jit(solution)/shard_map/reduce_sum | solution.py:88
  97.7 8.5 %collective-permute-done.17 = bf16[256,768]{1,0:T(8,128)(2,1)S(1)} collective-permute-done((bf16[256,768]{1,0:T(8,128)(2,1)S(1)}, bf16[256,768]{1,0:T(8,128)(2,1)S(1)}, u32[]{:S(2)}, u32[]{:S(2)}) %collective-permute-start.17) | collective-permute-done | bytes 393248 | tf_op jit(solution)/shard_map/ppermute | solution.py:18
  113.0 4.7 %collective-permute-done.14 = bf16[256,768]{1,0:T(8,128)(2,1)S(1)} collective-permute-done((bf16[256,768]{1,0:T(8,128)(2,1)S(1)}, bf16[256,768]{1,0:T(8,128)(2,1)S(1)}, u32[]{:S(2)}, u32[]{:S(2)}) %collective-permute-start.14) | collective-permute-done | bytes 393248 | tf_op jit(solution)/shard_map/ppermute | solution.py:18
  123.0 8.3 %collective-permute-done.27 = bf16[256,768]{1,0:T(8,128)(2,1)S(1)} collective-permute-done((bf16[256,768]{1,0:T(8,128)(2,1)S(1)}, bf16[256,768]{1,0:T(8,128)(2,1)S(1)}, u32[]{:S(2)}, u32[]{:S(2)}) %collective-permute-start.27) | collective-permute-done | bytes 393248 | tf_op jit(solution)/shard_map/ppermute | solution.py:18
  131.8 5.5 %collective-permute-done.24 = bf16[256,768]{1,0:T(8,128)(2,1)S(1)} collective-permute-done((bf16[256,768]{1,0:T(8,128)(2,1)S(1)}, bf16[256,768]{1,0:T(8,128)(2,1)S(1)}, u32[]{:S(2)}, u32[]{:S(2)}) %collective-permute-start.24) | collective-permute-done | bytes 393248 | tf_op jit(solution)/shard_map/ppermute | solution.py:18
  143.7 4.0 %all-to-all-start.3 = ((f32[16,8,128]{2,1,0:T(8,128)}), f32[16,8,128]{2,1,0:T(8,128)S(1)}, u32[]{:S(2)}, u32[]{:S(2)}) async-start(f32[16,8,128]{2,1,0:T(8,128)} %broadcast_in_dim_broadcast_in_dim.7), calls=%async_computation.3 | async-start | bytes 131072 | tf_op jit(solution)/shard_map/all_to_all | solution.py:28
  154.3 3.2 %collective-permute-start.29 = (f32[80,768]{1,0:T(8,128)S(1)}, f32[80,768]{1,0:T(8,128)S(1)}, u32[]{:S(2)}, u32[]{:S(2)}) collective-permute-start(f32[80,768]{1,0:T(8,128)S(1)} %get-tuple-element.28), channel_id=1, source_target_pairs={{2,0},{4,2},{6,4},{0,6},{3,1},{5,3},{7,5},{1,7},{10,8},{12,10},{14... | collective-permute-start | bytes 737288 | tf_op jit(solution)/shard_map/ppermute | solution.py:18
  158.3 3.9 %collective-permute-done.19 = f32[80,768]{1,0:T(8,128)S(1)} collective-permute-done((f32[80,768]{1,0:T(8,128)S(1)}, f32[80,768]{1,0:T(8,128)S(1)}, u32[]{:S(2)}, u32[]{:S(2)}) %collective-permute-start.19) | collective-permute-done | bytes 245792 | tf_op jit(solution)/shard_map/ppermute | solution.py:18
  167.8 3.3 %collective-permute-done.31 = f32[80,768]{1,0:T(8,128)S(1)} collective-permute-done((f32[80,768]{1,0:T(8,128)S(1)}, f32[80,768]{1,0:T(8,128)S(1)}, u32[]{:S(2)}, u32[]{:S(2)}) %collective-permute-start.31) | collective-permute-done | bytes 245792 | tf_op jit(solution)/shard_map/ppermute | solution.py:18
  172.0 7.4 %all-to-all-start.2 = ((f32[8,120,128]{2,1,0:T(8,128)}), f32[8,120,128]{2,1,0:T(8,128)S(1)}, u32[]{:S(2)}, u32[]{:S(2)}) async-start(f32[8,120,128]{2,1,0:T(8,128)} %bitcast.49), calls=%async_computation.2 | async-start | bytes 983040 | tf_op jit(solution)/shard_map/all_to_all | solution.py:114
  180.1 14.8 %all-to-all-done.2 = f32[8,120,128]{2,1,0:T(8,128)S(1)} async-done(((f32[8,120,128]{2,1,0:T(8,128)}), f32[8,120,128]{2,1,0:T(8,128)S(1)}, u32[]{:S(2)}, u32[]{:S(2)}) %all-to-all-start.2) | async-done | bytes 491552 | tf_op jit(solution)/shard_map/all_to_all | solution.py:114
  196.6 6.4 %all-to-all-start.4 = ((f32[16,128,128]{2,1,0:T(8,128)}), f32[16,128,128]{2,1,0:T(8,128)S(1)}, u32[]{:S(2)}, u32[]{:S(2)}) async-start(f32[16,128,128]{2,1,0:T(8,128)} %broadcast_in_dim.41), calls=%async_computation.4 | async-start | bytes 2097152 | tf_op jit(solution)/shard_map/all_to_all | solution.py:28
  203.7 25.2 %all-to-all-done.4 = f32[16,128,128]{2,1,0:T(8,128)S(1)} async-done(((f32[16,128,128]{2,1,0:T(8,128)}), f32[16,128,128]{2,1,0:T(8,128)S(1)}, u32[]{:S(2)}, u32[]{:S(2)}) %all-to-all-start.4) | async-done | bytes 1048608 | tf_op jit(solution)/shard_map/all_to_all | solution.py:28
  (131 shorter events, 70.3 us)
Async XLA Ops:
  3.3 20.8 %all-to-all-start = ((f32[16,8,128]{2,1,0:T(8,128)}), f32[16,8,128]{2,1,0:T(8,128)S(1)}, u32[]{:S(2)}, u32[]{:S(2)}) async-start(f32[16,8,128]{2,1,0:T(8,128)} %broadcast_in_dim.33), calls=%async_computation | async-start | bytes 131072 | tf_op jit(solution)/shard_map/all_to_all | solution.py:28
  14.5 13.8 %collective-permute-start.6 = (bf16[80,768]{1,0:T(8,128)(2,1)S(1)}, bf16[80,768]{1,0:T(8,128)(2,1)S(1)}, u32[]{:S(2)}, u32[]{:S(2)}) collective-permute-start(bf16[80,768]{1,0:T(8,128)(2,1)S(1)} %constant_dynamic-slice_fusion.5), channel_id=1, source_target_pairs={{8,0},{0,8},{9,1},{1,9},{10,2},{2,10},{11,3},{3,11},{12,4},{4,12},... | collective-permute-start | bytes 368648 | tf_op jit(solution)/shard_map/ppermute | solution.py:18
  28.2 16.6 %collective-permute-start.2 = (bf16[2,4,4,80,256]{4,3,2,1,0:T(8,128)(2,1)}, bf16[2,4,4,80,256]{4,3,2,1,0:T(8,128)(2,1)S(1)}, u32[]{:S(2)}, u32[]{:S(2)}) collective-permute-start(bf16[2,4,4,80,256]{4,3,2,1,0:T(8,128)(2,1)} %get-tuple-element.21), channel_id=1, source_target_pairs={{1,0},{0,1},{3,2},{2,3},{5,4},{4,5},{7,6},{6,7},{9,8},{8,9},{11,10... | collective-permute-start | bytes 3932168 | tf_op jit(solution)/shard_map/ppermute | solution.py:18
  43.4 24.7 %collective-permute-start.11 = (bf16[4,80,768]{2,1,0:T(8,128)(2,1)S(1)}, bf16[4,80,768]{2,1,0:T(8,128)(2,1)}, u32[]{:S(2)}, u32[]{:S(2)}) collective-permute-start(bf16[4,80,768]{2,1,0:T(8,128)(2,1)S(1)} %bitcast_dynamic-update-slice_fusion), channel_id=1, source_target_pairs={{48,0},{0,16},{16,32},{32,48},{49,1},{1,17},{17,33},{33,49},{50,2}... | collective-permute-start | bytes 1474568 | tf_op jit(solution)/shard_map/ppermute | solution.py:18
  43.4 27.1 %collective-permute-start.3 = (bf16[320,768]{1,0:T(8,128)(2,1)}, bf16[320,768]{1,0:T(8,128)(2,1)}, u32[]{:S(2)}, u32[]{:S(2)}) collective-permute-start(bf16[320,768]{1,0:T(8,128)(2,1)} %param.9), channel_id=1, source_target_pairs={{2,0},{4,2},{6,4},{0,6},{3,1},{5,3},{7,5},{1,7},{10,8},{12,10},{14... | collective-permute-start | bytes 1474568 | tf_op jit(solution)/shard_map/ppermute | solution.py:18
  43.9 26.6 %collective-permute-start.4 = (bf16[320,768]{1,0:T(8,128)(2,1)}, bf16[320,768]{1,0:T(8,128)(2,1)}, u32[]{:S(2)}, u32[]{:S(2)}) collective-permute-start(bf16[320,768]{1,0:T(8,128)(2,1)} %param.9), channel_id=1, source_target_pairs={{4,0},{6,2},{0,4},{2,6},{5,1},{7,3},{1,5},{3,7},{12,8},{14,10},{8,... | collective-permute-start | bytes 1474568 | tf_op jit(solution)/shard_map/ppermute | solution.py:18
  44.8 25.7 %collective-permute-start.5 = (bf16[320,768]{1,0:T(8,128)(2,1)}, bf16[320,768]{1,0:T(8,128)(2,1)S(1)}, u32[]{:S(2)}, u32[]{:S(2)}) collective-permute-start(bf16[320,768]{1,0:T(8,128)(2,1)} %param.9), channel_id=1, source_target_pairs={{6,0},{0,2},{2,4},{4,6},{7,1},{1,3},{3,5},{5,7},{14,8},{8,10},{10,... | collective-permute-start | bytes 1474568 | tf_op jit(solution)/shard_map/ppermute | solution.py:18
  54.0 15.9 %collective-permute-start.12 = (bf16[4,80,768]{2,1,0:T(8,128)(2,1)S(1)}, bf16[4,80,768]{2,1,0:T(8,128)(2,1)S(1)}, u32[]{:S(2)}, u32[]{:S(2)}) collective-permute-start(bf16[4,80,768]{2,1,0:T(8,128)(2,1)S(1)} %bitcast_dynamic-update-slice_fusion), channel_id=1, source_target_pairs={{32,0},{48,16},{0,32},{16,48},{33,1},{49,17},{1,33},{17,49},{34,2}... | collective-permute-start | bytes 1474568 | tf_op jit(solution)/shard_map/ppermute | solution.py:18
  75.2 15.0 %collective-permute-start.13 = (f32[256,768]{1,0:T(8,128)S(1)}, f32[256,768]{1,0:T(8,128)}, u32[]{:S(2)}, u32[]{:S(2)}) collective-permute-start(f32[256,768]{1,0:T(8,128)S(1)} %slice.41), channel_id=1, source_target_pairs={{1,0},{0,1},{3,2},{2,3},{5,4},{4,5},{7,6},{6,7},{9,8},{8,9},{11,10... | collective-permute-start | bytes 2359304 | tf_op jit(solution)/shard_map/ppermute | solution.py:18
  83.4 13.8 %collective-permute-start.16 = (bf16[640,256]{1,0:T(8,128)(2,1)}, bf16[640,256]{1,0:T(8,128)(2,1)}, u32[]{:S(2)}, u32[]{:S(2)}) collective-permute-start(bf16[640,256]{1,0:T(8,128)(2,1)} %bitcast.27), channel_id=1, source_target_pairs={{4,0},{6,2},{0,4},{2,6},{5,1},{7,3},{1,5},{3,7},{12,8},{14,10},{8,... | collective-permute-start | bytes 983048 | tf_op jit(solution)/shard_map/ppermute | solution.py:18
  93.5 17.5 %collective-permute-start = (bf16[640,256]{1,0:T(8,128)(2,1)S(1)}, bf16[640,256]{1,0:T(8,128)(2,1)S(1)}, u32[]{:S(2)}, u32[]{:S(2)}) collective-permute-start(bf16[640,256]{1,0:T(8,128)(2,1)S(1)} %bitcast.116), channel_id=1, source_target_pairs={{2,0},{4,2},{6,4},{0,6},{3,1},{5,3},{7,5},{1,7},{10,8},{12,10},{14... | collective-permute-start | bytes 983048 | tf_op jit(solution)/shard_map/ppermute | solution.py:18
  93.9 18.3 %collective-permute-start.1 = (bf16[640,256]{1,0:T(8,128)(2,1)S(1)}, bf16[640,256]{1,0:T(8,128)(2,1)S(1)}, u32[]{:S(2)}, u32[]{:S(2)}) collective-permute-start(bf16[640,256]{1,0:T(8,128)(2,1)S(1)} %bitcast.114), channel_id=1, source_target_pairs={{6,0},{0,2},{2,4},{4,6},{7,1},{1,3},{3,5},{5,7},{14,8},{8,10},{10,... | collective-permute-start | bytes 983048 | tf_op jit(solution)/shard_map/ppermute | solution.py:18
  95.5 22.2 %collective-permute-start.14 = (bf16[256,768]{1,0:T(8,128)(2,1)S(1)}, bf16[256,768]{1,0:T(8,128)(2,1)S(1)}, u32[]{:S(2)}, u32[]{:S(2)}) collective-permute-start(bf16[256,768]{1,0:T(8,128)(2,1)S(1)} %get-tuple-element.4), channel_id=1, source_target_pairs={{2,0},{4,2},{6,4},{0,6},{3,1},{5,3},{7,5},{1,7},{10,8},{12,10},{14... | collective-permute-start | bytes 1179656 | tf_op jit(solution)/shard_map/ppermute | solution.py:18
  97.2 22.7 %collective-permute-start.15 = (bf16[256,768]{1,0:T(8,128)(2,1)S(1)}, bf16[256,768]{1,0:T(8,128)(2,1)S(1)}, u32[]{:S(2)}, u32[]{:S(2)}) collective-permute-start(bf16[256,768]{1,0:T(8,128)(2,1)S(1)} %get-tuple-element.4), channel_id=1, source_target_pairs={{6,0},{0,2},{2,4},{4,6},{7,1},{1,3},{3,5},{5,7},{14,8},{8,10},{10,... | collective-permute-start | bytes 1179656 | tf_op jit(solution)/shard_map/ppermute | solution.py:18
  106.2 15.9 %collective-permute-start.26 = (bf16[640,256]{1,0:T(8,128)(2,1)S(1)}, bf16[640,256]{1,0:T(8,128)(2,1)S(1)}, u32[]{:S(2)}, u32[]{:S(2)}) collective-permute-start(bf16[640,256]{1,0:T(8,128)(2,1)S(1)} %bitcast.119), channel_id=1, source_target_pairs={{32,0},{48,16},{0,32},{16,48},{33,1},{49,17},{1,33},{17,49},{34,2}... | collective-permute-start | bytes 983048 | tf_op jit(solution)/shard_map/ppermute | solution.py:18
  111.0 20.8 %collective-permute-start.22 = (bf16[640,256]{1,0:T(8,128)(2,1)S(1)}, bf16[640,256]{1,0:T(8,128)(2,1)S(1)}, u32[]{:S(2)}, u32[]{:S(2)}) collective-permute-start(bf16[640,256]{1,0:T(8,128)(2,1)S(1)} %bitcast.118), channel_id=1, source_target_pairs={{16,0},{32,16},{48,32},{0,48},{17,1},{33,17},{49,33},{1,49},{18,2}... | collective-permute-start | bytes 983048 | tf_op jit(solution)/shard_map/ppermute | solution.py:18
  112.2 19.5 %collective-permute-start.23 = (bf16[640,256]{1,0:T(8,128)(2,1)S(1)}, bf16[640,256]{1,0:T(8,128)(2,1)S(1)}, u32[]{:S(2)}, u32[]{:S(2)}) collective-permute-start(bf16[640,256]{1,0:T(8,128)(2,1)S(1)} %bitcast.117), channel_id=1, source_target_pairs={{48,0},{0,16},{16,32},{32,48},{49,1},{1,17},{17,33},{33,49},{50,2}... | collective-permute-start | bytes 983048 | tf_op jit(solution)/shard_map/ppermute | solution.py:18
  119.9 17.4 %collective-permute-start.24 = (bf16[256,768]{1,0:T(8,128)(2,1)S(1)}, bf16[256,768]{1,0:T(8,128)(2,1)S(1)}, u32[]{:S(2)}, u32[]{:S(2)}) collective-permute-start(bf16[256,768]{1,0:T(8,128)(2,1)S(1)} %get-tuple-element.4), channel_id=1, source_target_pairs={{16,0},{32,16},{48,32},{0,48},{17,1},{33,17},{49,33},{1,49},{18,2}... | collective-permute-start | bytes 1179656 | tf_op jit(solution)/shard_map/ppermute | solution.py:18
  122.1 17.0 %collective-permute-start.25 = (bf16[256,768]{1,0:T(8,128)(2,1)S(1)}, bf16[256,768]{1,0:T(8,128)(2,1)S(1)}, u32[]{:S(2)}, u32[]{:S(2)}) collective-permute-start(bf16[256,768]{1,0:T(8,128)(2,1)S(1)} %get-tuple-element.4), channel_id=1, source_target_pairs={{48,0},{0,16},{16,32},{32,48},{49,1},{1,17},{17,33},{33,49},{50,2}... | collective-permute-start | bytes 1179656 | tf_op jit(solution)/shard_map/ppermute | solution.py:18
  131.3 16.4 %collective-permute-start.18 = (f32[4,80,768]{2,1,0:T(8,128)S(1)}, f32[4,80,768]{2,1,0:T(8,128)}, u32[]{:S(2)}, u32[]{:S(2)}) collective-permute-start(f32[4,80,768]{2,1,0:T(8,128)S(1)} %dynamic-slice_bitcast_fusion.3), channel_id=1, source_target_pairs={{1,0},{0,1},{3,2},{2,3},{5,4},{4,5},{7,6},{6,7},{9,8},{8,9},{11,10... | collective-permute-start | bytes 2949128 | tf_op jit(solution)/shard_map/ppermute | solution.py:18
  143.7 28.3 %all-to-all-start.3 = ((f32[16,8,128]{2,1,0:T(8,128)}), f32[16,8,128]{2,1,0:T(8,128)S(1)}, u32[]{:S(2)}, u32[]{:S(2)}) async-start(f32[16,8,128]{2,1,0:T(8,128)} %broadcast_in_dim_broadcast_in_dim.7), calls=%async_computation.3 | async-start | bytes 131072 | tf_op jit(solution)/shard_map/all_to_all | solution.py:28
  152.1 13.9 %collective-permute-start.21 = (f32[80,768]{1,0:T(8,128)S(1)}, f32[80,768]{1,0:T(8,128)S(1)}, u32[]{:S(2)}, u32[]{:S(2)}) collective-permute-start(f32[80,768]{1,0:T(8,128)S(1)} %get-tuple-element.24), channel_id=1, source_target_pairs={{48,0},{0,16},{16,32},{32,48},{49,1},{1,17},{17,33},{33,49},{50,2}... | collective-permute-start | bytes 737288 | tf_op jit(solution)/shard_map/ppermute | solution.py:18
  172.0 22.8 %all-to-all-start.2 = ((f32[8,120,128]{2,1,0:T(8,128)}), f32[8,120,128]{2,1,0:T(8,128)S(1)}, u32[]{:S(2)}, u32[]{:S(2)}) async-start(f32[8,120,128]{2,1,0:T(8,128)} %bitcast.49), calls=%async_computation.2 | async-start | bytes 983040 | tf_op jit(solution)/shard_map/all_to_all | solution.py:114
  196.6 32.3 %all-to-all-start.4 = ((f32[16,128,128]{2,1,0:T(8,128)}), f32[16,128,128]{2,1,0:T(8,128)S(1)}, u32[]{:S(2)}, u32[]{:S(2)}) async-start(f32[16,128,128]{2,1,0:T(8,128)} %broadcast_in_dim.41), calls=%async_computation.4 | async-start | bytes 2097152 | tf_op jit(solution)/shard_map/all_to_all | solution.py:28
  (25 other events, 224.6 us)
where the time goes:
time: 234 us; the launch traced here: 233 us
  waiting for transfers between devices  113 us (48%)
  starting transfers between devices  73.8 us (32%)
  local copies, waits for them, and re-layouts  17.5 us (7%)
  other arithmetic  12.5 us (5%)
  matrix products  10.6 us (5%)
  between operations  5.52 us (2%)
    ppermute x32, waiting for transfers between devices, fetch(): return lax.ppermute(value, axis, [((i + step) % n, i) for i in range(n)])  68.2 us
    ppermute x32, starting transfers between devices, fetch(): return lax.ppermute(value, axis, [((i + step) % n, i) for i in range(n)])  40.6 us
    all_to_all x4, waiting for transfers between devices, from_everyone(): return lax.all_to_all(copies, axes, split_axis=0, concat_axis=0, tiled=True)  29.9 us
    all_to_all x4, starting transfers between devices, from_everyone(): return lax.all_to_all(copies, axes, split_axis=0, concat_axis=0, tiled=True)  25.7 us
    all_to_all x1, waiting for transfers between devices, body(): lax.all_to_all(pieces, (ZH, ZL), split_axis=0, concat_axis=0, tiled=True)  14.8 us
    all_to_all x1, starting transfers between devices, body(): lax.all_to_all(pieces, (ZH, ZL), split_axis=0, concat_axis=0, tiled=True)  7.42 us
    dot_general x5, matrix products, rows_by(): lax.dot_general(left, right, (((0,), (0,)), ((), ())), preferred_element_...  6.95 us
    unnamed x26, local copies, waits for them, and re-layouts  6.65 us
  transfers between devices with their start and end apart: 37, of which 20 were waited for; matrix products, arithmetic and copies ran while one was open for 13% of the time, Pallas kernels for 0%

commit v1 on v0

--- a/solution.py
+++ b/solution.py
@@ -99,6 +99,7 @@
             jnp.concatenate([up[i] for i in (0, 1, 3)]),
             preferred_element_type=jnp.float32,
         )
+        first = lax.optimization_barrier(first)
         return first + jnp.dot(left[2], up[2], preferred_element_type=jnp.float32)
 
     near_out = pooled(near_in, near_up).reshape(2, 4, part, features)
@@ -110,13 +111,16 @@
     both = jnp.where(zh == 0, jnp.stack([near_sum, far_sum]), jnp.stack([far_sum, near_sum]))
 
     tall, wide = part // 16, features // 256
-    pieces = both.reshape(2, 2, tall, 8, 2, wide, 128).transpose(0, 1, 4, 2, 5, 3, 6).reshape(8, -1, 128)
-    pieces = lax.all_to_all(pieces, (ZH, ZL), split_axis=0, concat_axis=0, tiled=True)
-    group_sum = summed(own_sum, SHARD)
-    piece = jnp.concatenate([pieces.sum(axis=0), jnp.broadcast_to(group_sum, (8, 128))])
-    whole = from_everyone(piece, DP)
-    loss = whole[:, -8, 0].sum() / (2.0 * features * total_count)
-    whole = whole[:, :-8].reshape(2, 2, 4, tall, wide, 8, 128)
+
+    def tiled(value):
+        return value.reshape(-1, 2, tall, 8, 2, wide, 128).transpose(0, 1, 4, 2, 5, 3, 6)
+
+    plane_sum = summed(own_sum, (X, Y, C))
+    pieces = tiled(both).reshape(8, -1, 128)
+    pieces = jnp.concatenate([pieces, jnp.broadcast_to(plane_sum, (8, 8, 128))], axis=1)
+    pieces = lax.all_to_all(pieces, (ZH, ZL), split_axis=0, concat_axis=0, tiled=True).sum(axis=0)
+    loss = pieces[-1, 0] / (2.0 * features * total_count)
+    whole = from_everyone(pieces[:-8], DP).reshape(2, 2, 4, tall, wide, 8, 128)
     grad_key = whole.transpose(2, 0, 3, 5, 1, 4, 6).reshape(own, features)
     grad_gain = jnp.sum(w_key.astype(jnp.float32) * grad_key, axis=1) / norm_gain.astype(jnp.float32)
     return (loss, grad_gain, grad_key)

time: 234 us -> 246 us (1.051)
  blocking collectives: 0 us -> 19.7 us
  starting transfers between devices: 73.8 us -> 64.4 us
    all_to_all x0 -> x1, blocking collectives: none -> 19.7 us  [body(): lax.all_to_all(pieces, (ZH, ZL), split_axis=0, concat_axis=0, tiled=True)]
    all_to_all x1 -> x0, waiting for transfers between devices: 14.8 us -> none  [body(): lax.all_to_all(pieces, (ZH, ZL), split_axis=0, concat_axis=0, tiled=True)]
    ppermute x32, waiting for transfers between devices: 68.2 us -> 80.9 us  [fetch(): return lax.ppermute(value, axis, [((i + step) % n, i) for i in range(n)])]
    all_to_all x1 -> x0, starting transfers between devices: 7.42 us -> none  [body(): lax.all_to_all(pieces, (ZH, ZL), split_axis=0, concat_axis=0, tiled=True)]
    all_to_all x4, waiting for transfers between devices: 29.9 us -> 34.3 us  [from_everyone(): return lax.all_to_all(copies, axes, split_axis=0, concat_axis=0, tiled=True)]
  transfers between devices with their start and end apart: 37 -> 36, of which waited for: 20 -> 17; matrix products, arithmetic and copies ran while one was open for 13% -> 12% of each run, Pallas kernels for 0% -> 0%
where the time goes in v1:
time: 246 us; the launch traced here: 245 us
  waiting for transfers between devices  115 us (47%)
  starting transfers between devices  64.4 us (26%)
  blocking collectives  19.7 us (8%)
  local copies, waits for them, and re-layouts  16.9 us (7%)
  other arithmetic  12.4 us (5%)
  matrix products  10.6 us (4%)
  between operations  5.56 us (2%)
    ppermute x32, waiting for transfers between devices, fetch(): return lax.ppermute(value, axis, [((i + step) % n, i) for i in range(n)])  80.9 us
    ppermute x32, starting transfers between devices, fetch(): return lax.ppermute(value, axis, [((i + step) % n, i) for i in range(n)])  39 us
    all_to_all x4, waiting for transfers between devices, from_everyone(): return lax.all_to_all(copies, axes, split_axis=0, concat_axis=0, tiled=True)  34.3 us
    all_to_all x4, starting transfers between devices, from_everyone(): return lax.all_to_all(copies, axes, split_axis=0, concat_axis=0, tiled=True)  25.4 us
    all_to_all x1, blocking collectives, body(): lax.all_to_all(pieces, (ZH, ZL), split_axis=0, concat_axis=0, tiled=True)  19.7 us
    dot_general x5, matrix products, rows_by(): lax.dot_general(left, right, (((0,), (0,)), ((), ())), preferred_element_...  6.95 us
    unnamed x26, local copies, waits for them, and re-layouts  6.34 us
  transfers between devices with their start and end apart: 36, of which 17 were waited for; matrix products, arithmetic and copies ran while one was open for 12% of the time, Pallas kernels for 0%

profile of v1, /device:TPU:32, one launch (start us, length us, event | category | flops | bytes accessed | tf_op | source)
XLA Modules:
  0.0 244.8 jit_solution(7755516687592487387)
XLA Ops:
  3.3 10.3 %all-to-all-start = ((f32[16,8,128]{2,1,0:T(8,128)}), f32[16,8,128]{2,1,0:T(8,128)S(1)}, u32[]{:S(2)}, u32[]{:S(2)}) async-start(f32[16,8,128]{2,1,0:T(8,128)} %broadcast_in_dim.33), calls=%async_computation | async-start | bytes 131072 | tf_op jit(solution)/shard_map/all_to_all | solution.py:28
  14.5 5.9 %collective-permute-start.6 = (bf16[80,768]{1,0:T(8,128)(2,1)S(1)}, bf16[80,768]{1,0:T(8,128)(2,1)S(1)}, u32[]{:S(2)}, u32[]{:S(2)}) collective-permute-start(bf16[80,768]{1,0:T(8,128)(2,1)S(1)} %constant_dynamic-slice_fusion.5), channel_id=1, source_target_pairs={{8,0},{0,8},{9,1},{1,9},{10,2},{2,10},{11,3},{3,11},{12,4},{4,12},... | collective-permute-start | bytes 368648 | tf_op jit(solution)/shard_map/ppermute | solution.py:18
  20.4 3.0 %copy.16 = bf16[256,5120]{0,1:T(8,128)(2,1)S(1)} copy(bf16[256,5120]{1,0:T(8,128)(2,1)} %param.6) | data formatting | bytes 5242880 | tf_op args[0]
  28.2 2.7 %collective-permute-start.7 = (bf16[80,768]{1,0:T(8,128)(2,1)S(1)}, bf16[80,768]{1,0:T(8,128)(2,1)S(1)}, u32[]{:S(2)}, u32[]{:S(2)}) collective-permute-start(bf16[80,768]{1,0:T(8,128)(2,1)S(1)} %collective-permute-done.6), channel_id=1, source_target_pairs={{2,0},{4,2},{6,4},{0,6},{3,1},{5,3},{7,5},{1,7},{10,8},{12,10},{14... | collective-permute-start | bytes 368648 | tf_op jit(solution)/shard_map/ppermute | solution.py:18
  32.7 4.1 %collective-permute-done.7 = bf16[80,768]{1,0:T(8,128)(2,1)S(1)} collective-permute-done((bf16[80,768]{1,0:T(8,128)(2,1)S(1)}, bf16[80,768]{1,0:T(8,128)(2,1)S(1)}, u32[]{:S(2)}, u32[]{:S(2)}) %collective-permute-start.7) | collective-permute-done | bytes 122912 | tf_op jit(solution)/shard_map/ppermute | solution.py:18
  40.5 2.8 %collective-permute-start.10 = (bf16[4,80,768]{2,1,0:T(8,128)(2,1)S(1)}, bf16[4,80,768]{2,1,0:T(8,128)(2,1)}, u32[]{:S(2)}, u32[]{:S(2)}) collective-permute-start(bf16[4,80,768]{2,1,0:T(8,128)(2,1)S(1)} %bitcast_dynamic-update-slice_fusion), channel_id=1, source_target_pairs={{16,0},{32,16},{48,32},{0,48},{17,1},{33,17},{49,33},{1,49},{18,2}... | collective-permute-start | bytes 1474568 | tf_op jit(solution)/shard_map/ppermute | solution.py:18
  45.8 8.3 %collective-permute-done.10 = bf16[4,80,768]{2,1,0:T(8,128)(2,1)} collective-permute-done((bf16[4,80,768]{2,1,0:T(8,128)(2,1)S(1)}, bf16[4,80,768]{2,1,0:T(8,128)(2,1)}, u32[]{:S(2)}, u32[]{:S(2)}) %collective-permute-start.10) | collective-permute-done | bytes 491552 | tf_op jit(solution)/shard_map/ppermute | solution.py:18
  54.0 2.9 %collective-permute-start.12 = (bf16[4,80,768]{2,1,0:T(8,128)(2,1)S(1)}, bf16[4,80,768]{2,1,0:T(8,128)(2,1)S(1)}, u32[]{:S(2)}, u32[]{:S(2)}) collective-permute-start(bf16[4,80,768]{2,1,0:T(8,128)(2,1)S(1)} %bitcast_dynamic-update-slice_fusion), channel_id=1, source_target_pairs={{32,0},{48,16},{0,32},{16,48},{33,1},{49,17},{1,33},{17,49},{34,2}... | collective-permute-start | bytes 1474568 | tf_op jit(solution)/shard_map/ppermute | solution.py:18
  58.5 9.6 %collective-permute-done.11 = bf16[4,80,768]{2,1,0:T(8,128)(2,1)} collective-permute-done((bf16[4,80,768]{2,1,0:T(8,128)(2,1)S(1)}, bf16[4,80,768]{2,1,0:T(8,128)(2,1)}, u32[]{:S(2)}, u32[]{:S(2)}) %collective-permute-start.11) | collective-permute-done | bytes 491552 | tf_op jit(solution)/shard_map/ppermute | solution.py:18
  77.2 5.0 %all-to-all-start.1 = ((f32[16,8,128]{2,1,0:T(8,128)}), f32[16,8,128]{2,1,0:T(8,128)S(1)}, u32[]{:S(2)}, u32[]{:S(2)}) async-start(f32[16,8,128]{2,1,0:T(8,128)} %broadcast_in_dim_broadcast_in_dim.6), calls=%async_computation.1 | async-start | bytes 131072 | tf_op jit(solution)/shard_map/all_to_all | solution.py:28
  83.8 5.1 %all-to-all-done.1 = f32[16,8,128]{2,1,0:T(8,128)S(1)} async-done(((f32[16,8,128]{2,1,0:T(8,128)}), f32[16,8,128]{2,1,0:T(8,128)S(1)}, u32[]{:S(2)}, u32[]{:S(2)}) %all-to-all-start.1) | async-done | bytes 65568 | tf_op jit(solution)/shard_map/all_to_all | solution.py:28
  90.2 2.5 %fusion.38 = (f32[]{:T(128)}, bf16[256,768]{1,0:T(8,128)(2,1)S(1)}) fusion(f32[256]{0:T(256)S(1)} %get-tuple-element.29, bf16[256,768]{1,0:T(8,128)(2,1)} %param.7, f32[256,768]{1,0:T(8,128)} %collective-permute-done.13, f32[512,768]{1,0:T(8,128)} %copy-done.4, f32[256]{0:T(256)S(1)} %get-tuple-element.30), kind=kLoop, calls=%fused_computation.65 | loop fusion | flops 1572863 | bytes 2361348 | tf_op jit(solution)/shard_map/reduce_sum | solution.py:88
  96.3 2.5 %collective-permute-start.14 = (bf16[256,768]{1,0:T(8,128)(2,1)S(1)}, bf16[256,768]{1,0:T(8,128)(2,1)S(1)}, u32[]{:S(2)}, u32[]{:S(2)}) collective-permute-start(bf16[256,768]{1,0:T(8,128)(2,1)S(1)} %get-tuple-element.4), channel_id=1, source_target_pairs={{2,0},{4,2},{6,4},{0,6},{3,1},{5,3},{7,5},{1,7},{10,8},{12,10},{14... | collective-permute-start | bytes 1179656 | tf_op jit(solution)/shard_map/ppermute | solution.py:18
  99.0 14.3 %collective-permute-done.1 = bf16[640,256]{1,0:T(8,128)(2,1)S(1)} collective-permute-done((bf16[640,256]{1,0:T(8,128)(2,1)S(1)}, bf16[640,256]{1,0:T(8,128)(2,1)S(1)}, u32[]{:S(2)}, u32[]{:S(2)}) %collective-permute-start.1) | collective-permute-done | bytes 327712 | tf_op jit(solution)/shard_map/ppermute | solution.py:18
  114.5 5.8 %collective-permute-done.16 = bf16[640,256]{1,0:T(8,128)(2,1)S(1)} collective-permute-done((bf16[640,256]{1,0:T(8,128)(2,1)S(1)}, bf16[640,256]{1,0:T(8,128)(2,1)S(1)}, u32[]{:S(2)}, u32[]{:S(2)}) %collective-permute-start.16) | collective-permute-done | bytes 327712 | tf_op jit(solution)/shard_map/ppermute | solution.py:18
  123.4 3.5 %collective-permute-done.15 = bf16[256,768]{1,0:T(8,128)(2,1)S(1)} collective-permute-done((bf16[256,768]{1,0:T(8,128)(2,1)S(1)}, bf16[256,768]{1,0:T(8,128)(2,1)S(1)}, u32[]{:S(2)}, u32[]{:S(2)}) %collective-permute-start.15) | collective-permute-done | bytes 393248 | tf_op jit(solution)/shard_map/ppermute | solution.py:18
  132.8 19.7 %collective-permute-done.23 = bf16[640,256]{1,0:T(8,128)(2,1)S(1)} collective-permute-done((bf16[640,256]{1,0:T(8,128)(2,1)S(1)}, bf16[640,256]{1,0:T(8,128)(2,1)S(1)}, u32[]{:S(2)}, u32[]{:S(2)}) %collective-permute-start.23) | collective-permute-done | bytes 327712 | tf_op jit(solution)/shard_map/ppermute | solution.py:18
  158.3 3.8 %all-to-all-start.2 = ((f32[32,8,128]{2,1,0:T(8,128)}), f32[32,8,128]{2,1,0:T(8,128)S(1)}, u32[]{:S(2)}, u32[]{:S(2)}) async-start(f32[32,8,128]{2,1,0:T(8,128)} %broadcast_in_dim_broadcast_in_dim.7), calls=%async_computation.2 | async-start | bytes 262144 | tf_op jit(solution)/shard_map/all_to_all | solution.py:28
  162.2 7.8 %all-to-all-done.2 = f32[32,8,128]{2,1,0:T(8,128)S(1)} async-done(((f32[32,8,128]{2,1,0:T(8,128)}), f32[32,8,128]{2,1,0:T(8,128)S(1)}, u32[]{:S(2)}, u32[]{:S(2)}) %all-to-all-start.2) | async-done | bytes 131104 | tf_op jit(solution)/shard_map/all_to_all | solution.py:28
  183.6 4.1 %collective-permute-done.21 = f32[80,768]{1,0:T(8,128)S(1)} collective-permute-done((f32[80,768]{1,0:T(8,128)S(1)}, f32[80,768]{1,0:T(8,128)S(1)}, u32[]{:S(2)}, u32[]{:S(2)}) %collective-permute-start.21) | collective-permute-done | bytes 245792 | tf_op jit(solution)/shard_map/ppermute | solution.py:18
  187.9 3.5 %collective-permute-done.31 = f32[80,768]{1,0:T(8,128)S(1)} collective-permute-done((f32[80,768]{1,0:T(8,128)S(1)}, f32[80,768]{1,0:T(8,128)S(1)}, u32[]{:S(2)}, u32[]{:S(2)}) %collective-permute-start.31) | collective-permute-done | bytes 245792 | tf_op jit(solution)/shard_map/ppermute | solution.py:18
  192.3 19.7 %all_to_all.25 = f32[8,128,128]{2,1,0:T(8,128)S(1)} all-to-all(f32[8,128,128]{2,1,0:T(8,128)S(1)} %concatenate.37), channel_id=1, replica_groups=mesh['dp_0'=4,'dp_1'=4,'shard_0'=2,'shard_1'=4,'shard_2'=2] {'shard_0','..., dimensions={0} | all-to-all | bytes 1048576 | tf_op jit(solution)/shard_map/all_to_all | solution.py:121
  213.1 6.2 %all-to-all-start.4 = ((f32[16,120,128]{2,1,0:T(8,128)}), f32[16,120,128]{2,1,0:T(8,128)S(1)}, u32[]{:S(2)}, u32[]{:S(2)}) async-start(f32[16,120,128]{2,1,0:T(8,128)} %broadcast_in_dim.41), calls=%async_computation.4 | async-start | bytes 1966080 | tf_op jit(solution)/shard_map/all_to_all | solution.py:28
  221.1 21.5 %all-to-all-done.4 = f32[16,120,128]{2,1,0:T(8,128)S(1)} async-done(((f32[16,120,128]{2,1,0:T(8,128)}), f32[16,120,128]{2,1,0:T(8,128)S(1)}, u32[]{:S(2)}, u32[]{:S(2)}) %all-to-all-start.4) | async-done | bytes 983072 | tf_op jit(solution)/shard_map/all_to_all | solution.py:28
  (132 shorter events, 64.6 us)
Async XLA Ops:
  3.3 20.8 %all-to-all-start = ((f32[16,8,128]{2,1,0:T(8,128)}), f32[16,8,128]{2,1,0:T(8,128)S(1)}, u32[]{:S(2)}, u32[]{:S(2)}) async-start(f32[16,8,128]{2,1,0:T(8,128)} %broadcast_in_dim.33), calls=%async_computation | async-start | bytes 131072 | tf_op jit(solution)/shard_map/all_to_all | solution.py:28
  14.5 13.8 %collective-permute-start.6 = (bf16[80,768]{1,0:T(8,128)(2,1)S(1)}, bf16[80,768]{1,0:T(8,128)(2,1)S(1)}, u32[]{:S(2)}, u32[]{:S(2)}) collective-permute-start(bf16[80,768]{1,0:T(8,128)(2,1)S(1)} %constant_dynamic-slice_fusion.5), channel_id=1, source_target_pairs={{8,0},{0,8},{9,1},{1,9},{10,2},{2,10},{11,3},{3,11},{12,4},{4,12},... | collective-permute-start | bytes 368648 | tf_op jit(solution)/shard_map/ppermute | solution.py:18
  28.2 16.6 %collective-permute-start.2 = (bf16[2,4,4,80,256]{4,3,2,1,0:T(8,128)(2,1)}, bf16[2,4,4,80,256]{4,3,2,1,0:T(8,128)(2,1)S(1)}, u32[]{:S(2)}, u32[]{:S(2)}) collective-permute-start(bf16[2,4,4,80,256]{4,3,2,1,0:T(8,128)(2,1)} %get-tuple-element.21), channel_id=1, source_target_pairs={{1,0},{0,1},{3,2},{2,3},{5,4},{4,5},{7,6},{6,7},{9,8},{8,9},{11,10... | collective-permute-start | bytes 3932168 | tf_op jit(solution)/shard_map/ppermute | solution.py:18
  43.4 24.7 %collective-permute-start.11 = (bf16[4,80,768]{2,1,0:T(8,128)(2,1)S(1)}, bf16[4,80,768]{2,1,0:T(8,128)(2,1)}, u32[]{:S(2)}, u32[]{:S(2)}) collective-permute-start(bf16[4,80,768]{2,1,0:T(8,128)(2,1)S(1)} %bitcast_dynamic-update-slice_fusion), channel_id=1, source_target_pairs={{48,0},{0,16},{16,32},{32,48},{49,1},{1,17},{17,33},{33,49},{50,2}... | collective-permute-start | bytes 1474568 | tf_op jit(solution)/shard_map/ppermute | solution.py:18
  43.4 27.1 %collective-permute-start.3 = (bf16[320,768]{1,0:T(8,128)(2,1)}, bf16[320,768]{1,0:T(8,128)(2,1)}, u32[]{:S(2)}, u32[]{:S(2)}) collective-permute-start(bf16[320,768]{1,0:T(8,128)(2,1)} %param.9), channel_id=1, source_target_pairs={{2,0},{4,2},{6,4},{0,6},{3,1},{5,3},{7,5},{1,7},{10,8},{12,10},{14... | collective-permute-start | bytes 1474568 | tf_op jit(solution)/shard_map/ppermute | solution.py:18
  43.9 26.6 %collective-permute-start.4 = (bf16[320,768]{1,0:T(8,128)(2,1)}, bf16[320,768]{1,0:T(8,128)(2,1)}, u32[]{:S(2)}, u32[]{:S(2)}) collective-permute-start(bf16[320,768]{1,0:T(8,128)(2,1)} %param.9), channel_id=1, source_target_pairs={{4,0},{6,2},{0,4},{2,6},{5,1},{7,3},{1,5},{3,7},{12,8},{14,10},{8,... | collective-permute-start | bytes 1474568 | tf_op jit(solution)/shard_map/ppermute | solution.py:18
  44.8 25.7 %collective-permute-start.5 = (bf16[320,768]{1,0:T(8,128)(2,1)}, bf16[320,768]{1,0:T(8,128)(2,1)S(1)}, u32[]{:S(2)}, u32[]{:S(2)}) collective-permute-start(bf16[320,768]{1,0:T(8,128)(2,1)} %param.9), channel_id=1, source_target_pairs={{6,0},{0,2},{2,4},{4,6},{7,1},{1,3},{3,5},{5,7},{14,8},{8,10},{10,... | collective-permute-start | bytes 1474568 | tf_op jit(solution)/shard_map/ppermute | solution.py:18
  54.0 15.8 %collective-permute-start.12 = (bf16[4,80,768]{2,1,0:T(8,128)(2,1)S(1)}, bf16[4,80,768]{2,1,0:T(8,128)(2,1)S(1)}, u32[]{:S(2)}, u32[]{:S(2)}) collective-permute-start(bf16[4,80,768]{2,1,0:T(8,128)(2,1)S(1)} %bitcast_dynamic-update-slice_fusion), channel_id=1, source_target_pairs={{32,0},{48,16},{0,32},{16,48},{33,1},{49,17},{1,33},{17,49},{34,2}... | collective-permute-start | bytes 1474568 | tf_op jit(solution)/shard_map/ppermute | solution.py:18
  75.2 15.0 %collective-permute-start.13 = (f32[256,768]{1,0:T(8,128)S(1)}, f32[256,768]{1,0:T(8,128)}, u32[]{:S(2)}, u32[]{:S(2)}) collective-permute-start(f32[256,768]{1,0:T(8,128)S(1)} %slice.41), channel_id=1, source_target_pairs={{1,0},{0,1},{3,2},{2,3},{5,4},{4,5},{7,6},{6,7},{9,8},{8,9},{11,10... | collective-permute-start | bytes 2359304 | tf_op jit(solution)/shard_map/ppermute | solution.py:18
  83.4 15.5 %collective-permute-start = (bf16[640,256]{1,0:T(8,128)(2,1)}, bf16[640,256]{1,0:T(8,128)(2,1)}, u32[]{:S(2)}, u32[]{:S(2)}) collective-permute-start(bf16[640,256]{1,0:T(8,128)(2,1)} %bitcast.7), channel_id=1, source_target_pairs={{2,0},{4,2},{6,4},{0,6},{3,1},{5,3},{7,5},{1,7},{10,8},{12,10},{14... | collective-permute-start | bytes 983048 | tf_op jit(solution)/shard_map/ppermute | solution.py:18
  92.7 28.9 %collective-permute-start.17 = (bf16[256,768]{1,0:T(8,128)(2,1)S(1)}, bf16[256,768]{1,0:T(8,128)(2,1)S(1)}, u32[]{:S(2)}, u32[]{:S(2)}) collective-permute-start(bf16[256,768]{1,0:T(8,128)(2,1)S(1)} %get-tuple-element.4), channel_id=1, source_target_pairs={{4,0},{6,2},{0,4},{2,6},{5,1},{7,3},{1,5},{3,7},{12,8},{14,10},{8,... | collective-permute-start | bytes 1179656 | tf_op jit(solution)/shard_map/ppermute | solution.py:18
  93.5 19.8 %collective-permute-start.1 = (bf16[640,256]{1,0:T(8,128)(2,1)S(1)}, bf16[640,256]{1,0:T(8,128)(2,1)S(1)}, u32[]{:S(2)}, u32[]{:S(2)}) collective-permute-start(bf16[640,256]{1,0:T(8,128)(2,1)S(1)} %bitcast.119), channel_id=1, source_target_pairs={{6,0},{0,2},{2,4},{4,6},{7,1},{1,3},{3,5},{5,7},{14,8},{8,10},{10,... | collective-permute-start | bytes 983048 | tf_op jit(solution)/shard_map/ppermute | solution.py:18
  94.0 26.3 %collective-permute-start.16 = (bf16[640,256]{1,0:T(8,128)(2,1)S(1)}, bf16[640,256]{1,0:T(8,128)(2,1)S(1)}, u32[]{:S(2)}, u32[]{:S(2)}) collective-permute-start(bf16[640,256]{1,0:T(8,128)(2,1)S(1)} %bitcast.118), channel_id=1, source_target_pairs={{4,0},{6,2},{0,4},{2,6},{5,1},{7,3},{1,5},{3,7},{12,8},{14,10},{8,... | collective-permute-start | bytes 983048 | tf_op jit(solution)/shard_map/ppermute | solution.py:18
  96.3 26.4 %collective-permute-start.14 = (bf16[256,768]{1,0:T(8,128)(2,1)S(1)}, bf16[256,768]{1,0:T(8,128)(2,1)S(1)}, u32[]{:S(2)}, u32[]{:S(2)}) collective-permute-start(bf16[256,768]{1,0:T(8,128)(2,1)S(1)} %get-tuple-element.4), channel_id=1, source_target_pairs={{2,0},{4,2},{6,4},{0,6},{3,1},{5,3},{7,5},{1,7},{10,8},{12,10},{14... | collective-permute-start | bytes 1179656 | tf_op jit(solution)/shard_map/ppermute | solution.py:18
  98.9 28.1 %collective-permute-start.15 = (bf16[256,768]{1,0:T(8,128)(2,1)S(1)}, bf16[256,768]{1,0:T(8,128)(2,1)S(1)}, u32[]{:S(2)}, u32[]{:S(2)}) collective-permute-start(bf16[256,768]{1,0:T(8,128)(2,1)S(1)} %get-tuple-element.4), channel_id=1, source_target_pairs={{6,0},{0,2},{2,4},{4,6},{7,1},{1,3},{3,5},{5,7},{14,8},{8,10},{10,... | collective-permute-start | bytes 1179656 | tf_op jit(solution)/shard_map/ppermute | solution.py:18
  113.3 17.3 %collective-permute-start.22 = (bf16[640,256]{1,0:T(8,128)(2,1)S(1)}, bf16[640,256]{1,0:T(8,128)(2,1)S(1)}, u32[]{:S(2)}, u32[]{:S(2)}) collective-permute-start(bf16[640,256]{1,0:T(8,128)(2,1)S(1)} %bitcast.121), channel_id=1, source_target_pairs={{16,0},{32,16},{48,32},{0,48},{17,1},{33,17},{49,33},{1,49},{18,2}... | collective-permute-start | bytes 983048 | tf_op jit(solution)/shard_map/ppermute | solution.py:18
  120.3 32.2 %collective-permute-start.24 = (bf16[256,768]{1,0:T(8,128)(2,1)S(1)}, bf16[256,768]{1,0:T(8,128)(2,1)S(1)}, u32[]{:S(2)}, u32[]{:S(2)}) collective-permute-start(bf16[256,768]{1,0:T(8,128)(2,1)S(1)} %get-tuple-element.4), channel_id=1, source_target_pairs={{16,0},{32,16},{48,32},{0,48},{17,1},{33,17},{49,33},{1,49},{18,2}... | collective-permute-start | bytes 1179656 | tf_op jit(solution)/shard_map/ppermute | solution.py:18
  121.6 30.9 %collective-permute-start.25 = (bf16[256,768]{1,0:T(8,128)(2,1)S(1)}, bf16[256,768]{1,0:T(8,128)(2,1)S(1)}, u32[]{:S(2)}, u32[]{:S(2)}) collective-permute-start(bf16[256,768]{1,0:T(8,128)(2,1)S(1)} %get-tuple-element.4), channel_id=1, source_target_pairs={{48,0},{0,16},{16,32},{32,48},{49,1},{1,17},{17,33},{33,49},{50,2}... | collective-permute-start | bytes 1179656 | tf_op jit(solution)/shard_map/ppermute | solution.py:18
  122.8 29.7 %collective-permute-start.23 = (bf16[640,256]{1,0:T(8,128)(2,1)S(1)}, bf16[640,256]{1,0:T(8,128)(2,1)S(1)}, u32[]{:S(2)}, u32[]{:S(2)}) collective-permute-start(bf16[640,256]{1,0:T(8,128)(2,1)S(1)} %bitcast.120), channel_id=1, source_target_pairs={{48,0},{0,16},{16,32},{32,48},{49,1},{1,17},{17,33},{33,49},{50,2}... | collective-permute-start | bytes 983048 | tf_op jit(solution)/shard_map/ppermute | solution.py:18
  126.9 26.5 %collective-permute-start.27 = (bf16[256,768]{1,0:T(8,128)(2,1)S(1)}, bf16[256,768]{1,0:T(8,128)(2,1)S(1)}, u32[]{:S(2)}, u32[]{:S(2)}) collective-permute-start(bf16[256,768]{1,0:T(8,128)(2,1)S(1)} %get-tuple-element.4), channel_id=1, source_target_pairs={{32,0},{48,16},{0,32},{16,48},{33,1},{49,17},{1,33},{17,49},{34,2}... | collective-permute-start | bytes 1179656 | tf_op jit(solution)/shard_map/ppermute | solution.py:18
  130.6 22.8 %collective-permute-start.26 = (bf16[640,256]{1,0:T(8,128)(2,1)S(1)}, bf16[640,256]{1,0:T(8,128)(2,1)S(1)}, u32[]{:S(2)}, u32[]{:S(2)}) collective-permute-start(bf16[640,256]{1,0:T(8,128)(2,1)S(1)} %bitcast.116), channel_id=1, source_target_pairs={{32,0},{48,16},{0,32},{16,48},{33,1},{49,17},{1,33},{17,49},{34,2}... | collective-permute-start | bytes 983048 | tf_op jit(solution)/shard_map/ppermute | solution.py:18
  152.5 18.1 %collective-permute-start.18 = (f32[4,80,768]{2,1,0:T(8,128)S(1)}, f32[4,80,768]{2,1,0:T(8,128)}, u32[]{:S(2)}, u32[]{:S(2)}) collective-permute-start(f32[4,80,768]{2,1,0:T(8,128)S(1)} %dynamic-slice_bitcast_fusion.3), channel_id=1, source_target_pairs={{1,0},{0,1},{3,2},{2,3},{5,4},{4,5},{7,6},{6,7},{9,8},{8,9},{11,10... | collective-permute-start | bytes 2949128 | tf_op jit(solution)/shard_map/ppermute | solution.py:18
  156.5 18.4 %collective-permute-start.28 = (f32[4,80,768]{2,1,0:T(8,128)}, f32[4,80,768]{2,1,0:T(8,128)}, u32[]{:S(2)}, u32[]{:S(2)}) collective-permute-start(f32[4,80,768]{2,1,0:T(8,128)} %dynamic-slice_bitcast_fusion.2), channel_id=1, source_target_pairs={{1,0},{0,1},{3,2},{2,3},{5,4},{4,5},{7,6},{6,7},{9,8},{8,9},{11,10... | collective-permute-start | bytes 2949128 | tf_op jit(solution)/shard_map/ppermute | solution.py:18
  213.1 29.6 %all-to-all-start.4 = ((f32[16,120,128]{2,1,0:T(8,128)}), f32[16,120,128]{2,1,0:T(8,128)S(1)}, u32[]{:S(2)}, u32[]{:S(2)}) async-start(f32[16,120,128]{2,1,0:T(8,128)} %broadcast_in_dim.41), calls=%async_computation.4 | async-start | bytes 1966080 | tf_op jit(solution)/shard_map/all_to_all | solution.py:28
  (24 other events, 235.8 us)

commit v2 on v1

--- a/solution.py
+++ b/solution.py
@@ -120,9 +120,20 @@
     pieces = jnp.concatenate([pieces, jnp.broadcast_to(plane_sum, (8, 8, 128))], axis=1)
     pieces = lax.all_to_all(pieces, (ZH, ZL), split_axis=0, concat_axis=0, tiled=True).sum(axis=0)
     loss = pieces[-1, 0] / (2.0 * features * total_count)
-    whole = from_everyone(pieces[:-8], DP).reshape(2, 2, 4, tall, wide, 8, 128)
-    grad_key = whole.transpose(2, 0, 3, 5, 1, 4, 6).reshape(own, features)
-    grad_gain = jnp.sum(w_key.astype(jnp.float32) * grad_key, axis=1) / norm_gain.astype(jnp.float32)
+
+    piece = pieces[:-8]
+    mine = tiled(block(w_key.reshape(4, part, features), x)).reshape(4, -1, 128)
+    share = (piece * block(mine, lax.axis_index(ZL)).astype(jnp.float32)).sum(axis=1)
+    lines = []
+    for _ in range(3):
+        lines.append(lax.reduce_precision(share, 8, 7))
+        share = share - lines[-1]
+    lines = jnp.pad(jnp.stack(lines), ((0, 5), (0, 128 - share.size)))
+    whole = from_everyone(jnp.concatenate([piece, lines]).astype(jnp.bfloat16), DP)
+    shares = whole[:, -8:-5, : share.size].astype(jnp.float32).sum(axis=1).reshape(2, 2, 4, tall, wide, 8)
+    grad_gain = shares.sum(axis=(1, 4)).swapaxes(0, 1).reshape(own) / norm_gain.astype(jnp.float32)
+    whole = whole[:, :-8].reshape(2, 2, 4, tall, wide, 8, 128)
+    grad_key = whole.transpose(2, 0, 3, 5, 1, 4, 6).reshape(own, features).astype(jnp.float32)
     return (loss, grad_gain, grad_key)
 
 

time: 246 us -> 240 us (0.976)
  blocking collectives: 19.7 us -> 0 us
  waiting for transfers between devices: 115 us -> 122 us
  starting transfers between devices: 64.4 us -> 69 us
  local copies, waits for them, and re-layouts: 16.9 us -> 19.6 us
    all_to_all x1 -> x0, blocking collectives: 19.7 us -> none  [body(): lax.all_to_all(pieces, (ZH, ZL), split_axis=0, concat_axis=0, tiled=True)]
    all_to_all x0 -> x1, waiting for transfers between devices: none -> 15 us  [body(): lax.all_to_all(pieces, (ZH, ZL), split_axis=0, concat_axis=0, tiled=True)]
    all_to_all x4, waiting for transfers between devices: 34.3 us -> 26 us  [from_everyone(): return lax.all_to_all(copies, axes, split_axis=0, concat_axis=0, tiled=True)]
    all_to_all x0 -> x1, starting transfers between devices: none -> 4.77 us  [body(): lax.all_to_all(pieces, (ZH, ZL), split_axis=0, concat_axis=0, tiled=True)]
    unnamed x26 -> x22, local copies, waits for them, and re-layouts: 6.34 us -> 6.28 us
  transfers between devices with their start and end apart: 36 -> 37, of which waited for: 17 -> 18; matrix products, arithmetic and copies ran while one was open for 12% -> 13% of each run, Pallas kernels for 0% -> 0%
where the time goes in v2:
time: 240 us; the launch traced here: 239 us
  waiting for transfers between devices  122 us (51%)
  starting transfers between devices  69 us (29%)
  local copies, waits for them, and re-layouts  19.6 us (8%)
  other arithmetic  12.4 us (5%)
  matrix products  10.6 us (4%)
  between operations  5.6 us (2%)
    ppermute x32, waiting for transfers between devices, fetch(): return lax.ppermute(value, axis, [((i + step) % n, i) for i in range(n)])  80.9 us
    ppermute x32, starting transfers between devices, fetch(): return lax.ppermute(value, axis, [((i + step) % n, i) for i in range(n)])  39 us
    all_to_all x4, waiting for transfers between devices, from_everyone(): return lax.all_to_all(copies, axes, split_axis=0, concat_axis=0, tiled=True)  26 us
    all_to_all x4, starting transfers between devices, from_everyone(): return lax.all_to_all(copies, axes, split_axis=0, concat_axis=0, tiled=True)  25.3 us
    all_to_all x1, waiting for transfers between devices, body(): lax.all_to_all(pieces, (ZH, ZL), split_axis=0, concat_axis=0, tiled=True)  15 us
    dot_general x5, matrix products, rows_by(): lax.dot_general(left, right, (((0,), (0,)), ((), ())), preferred_element_...  6.95 us
    unnamed x22, local copies, waits for them, and re-layouts  6.28 us
  transfers between devices with their start and end apart: 37, of which 18 were waited for; matrix products, arithmetic and copies ran while one was open for 13% of the time, Pallas kernels for 0%

profile of v2, /device:TPU:32, one launch (start us, length us, event | category | flops | bytes accessed | tf_op | source)
XLA Modules:
  0.0 239.2 jit_solution(11114335453514316585)
XLA Ops:
  3.3 10.3 %all-to-all-start = ((f32[16,8,128]{2,1,0:T(8,128)}), f32[16,8,128]{2,1,0:T(8,128)S(1)}, u32[]{:S(2)}, u32[]{:S(2)}) async-start(f32[16,8,128]{2,1,0:T(8,128)} %broadcast_in_dim.33), calls=%async_computation | async-start | bytes 131072 | tf_op jit(solution)/shard_map/all_to_all | solution.py:28
  14.5 5.9 %collective-permute-start.6 = (bf16[80,768]{1,0:T(8,128)(2,1)S(1)}, bf16[80,768]{1,0:T(8,128)(2,1)S(1)}, u32[]{:S(2)}, u32[]{:S(2)}) collective-permute-start(bf16[80,768]{1,0:T(8,128)(2,1)S(1)} %constant_dynamic-slice_fusion.6), channel_id=1, source_target_pairs={{8,0},{0,8},{9,1},{1,9},{10,2},{2,10},{11,3},{3,11},{12,4},{4,12},... | collective-permute-start | bytes 368648 | tf_op jit(solution)/shard_map/ppermute | solution.py:18
  20.4 3.0 %copy.24 = bf16[256,5120]{0,1:T(8,128)(2,1)S(1)} copy(bf16[256,5120]{1,0:T(8,128)(2,1)} %param.6) | data formatting | bytes 5242880 | tf_op args[0]
  28.3 2.7 %collective-permute-start.7 = (bf16[80,768]{1,0:T(8,128)(2,1)S(1)}, bf16[80,768]{1,0:T(8,128)(2,1)S(1)}, u32[]{:S(2)}, u32[]{:S(2)}) collective-permute-start(bf16[80,768]{1,0:T(8,128)(2,1)S(1)} %collective-permute-done.6), channel_id=1, source_target_pairs={{2,0},{4,2},{6,4},{0,6},{3,1},{5,3},{7,5},{1,7},{10,8},{12,10},{14... | collective-permute-start | bytes 368648 | tf_op jit(solution)/shard_map/ppermute | solution.py:18
  32.7 4.1 %collective-permute-done.7 = bf16[80,768]{1,0:T(8,128)(2,1)S(1)} collective-permute-done((bf16[80,768]{1,0:T(8,128)(2,1)S(1)}, bf16[80,768]{1,0:T(8,128)(2,1)S(1)}, u32[]{:S(2)}, u32[]{:S(2)}) %collective-permute-start.7) | collective-permute-done | bytes 122912 | tf_op jit(solution)/shard_map/ppermute | solution.py:18
  40.6 2.8 %collective-permute-start.10 = (bf16[4,80,768]{2,1,0:T(8,128)(2,1)S(1)}, bf16[4,80,768]{2,1,0:T(8,128)(2,1)}, u32[]{:S(2)}, u32[]{:S(2)}) collective-permute-start(bf16[4,80,768]{2,1,0:T(8,128)(2,1)S(1)} %bitcast_dynamic-update-slice_fusion), channel_id=1, source_target_pairs={{16,0},{32,16},{48,32},{0,48},{17,1},{33,17},{49,33},{1,49},{18,2}... | collective-permute-start | bytes 1474568 | tf_op jit(solution)/shard_map/ppermute | solution.py:18
  45.8 8.3 %collective-permute-done.10 = bf16[4,80,768]{2,1,0:T(8,128)(2,1)} collective-permute-done((bf16[4,80,768]{2,1,0:T(8,128)(2,1)S(1)}, bf16[4,80,768]{2,1,0:T(8,128)(2,1)}, u32[]{:S(2)}, u32[]{:S(2)}) %collective-permute-start.10) | collective-permute-done | bytes 491552 | tf_op jit(solution)/shard_map/ppermute | solution.py:18
  54.1 2.9 %collective-permute-start.12 = (bf16[4,80,768]{2,1,0:T(8,128)(2,1)S(1)}, bf16[4,80,768]{2,1,0:T(8,128)(2,1)S(1)}, u32[]{:S(2)}, u32[]{:S(2)}) collective-permute-start(bf16[4,80,768]{2,1,0:T(8,128)(2,1)S(1)} %bitcast_dynamic-update-slice_fusion), channel_id=1, source_target_pairs={{32,0},{48,16},{0,32},{16,48},{33,1},{49,17},{1,33},{17,49},{34,2}... | collective-permute-start | bytes 1474568 | tf_op jit(solution)/shard_map/ppermute | solution.py:18
  58.5 9.6 %collective-permute-done.11 = bf16[4,80,768]{2,1,0:T(8,128)(2,1)} collective-permute-done((bf16[4,80,768]{2,1,0:T(8,128)(2,1)S(1)}, bf16[4,80,768]{2,1,0:T(8,128)(2,1)}, u32[]{:S(2)}, u32[]{:S(2)}) %collective-permute-start.11) | collective-permute-done | bytes 491552 | tf_op jit(solution)/shard_map/ppermute | solution.py:18
  77.2 5.0 %all-to-all-start.1 = ((f32[16,8,128]{2,1,0:T(8,128)}), f32[16,8,128]{2,1,0:T(8,128)S(1)}, u32[]{:S(2)}, u32[]{:S(2)}) async-start(f32[16,8,128]{2,1,0:T(8,128)} %broadcast_in_dim_broadcast_in_dim.6), calls=%async_computation.1 | async-start | bytes 131072 | tf_op jit(solution)/shard_map/all_to_all | solution.py:28
  83.8 5.1 %all-to-all-done.1 = f32[16,8,128]{2,1,0:T(8,128)S(1)} async-done(((f32[16,8,128]{2,1,0:T(8,128)}), f32[16,8,128]{2,1,0:T(8,128)S(1)}, u32[]{:S(2)}, u32[]{:S(2)}) %all-to-all-start.1) | async-done | bytes 65568 | tf_op jit(solution)/shard_map/all_to_all | solution.py:28
  96.3 2.5 %collective-permute-start.14 = (bf16[256,768]{1,0:T(8,128)(2,1)S(1)}, bf16[256,768]{1,0:T(8,128)(2,1)S(1)}, u32[]{:S(2)}, u32[]{:S(2)}) collective-permute-start(bf16[256,768]{1,0:T(8,128)(2,1)S(1)} %get-tuple-element.4), channel_id=1, source_target_pairs={{2,0},{4,2},{6,4},{0,6},{3,1},{5,3},{7,5},{1,7},{10,8},{12,10},{14... | collective-permute-start | bytes 1179656 | tf_op jit(solution)/shard_map/ppermute | solution.py:18
  99.0 14.3 %collective-permute-done.1 = bf16[640,256]{1,0:T(8,128)(2,1)S(1)} collective-permute-done((bf16[640,256]{1,0:T(8,128)(2,1)S(1)}, bf16[640,256]{1,0:T(8,128)(2,1)S(1)}, u32[]{:S(2)}, u32[]{:S(2)}) %collective-permute-start.1) | collective-permute-done | bytes 327712 | tf_op jit(solution)/shard_map/ppermute | solution.py:18
  114.5 5.8 %collective-permute-done.16 = bf16[640,256]{1,0:T(8,128)(2,1)S(1)} collective-permute-done((bf16[640,256]{1,0:T(8,128)(2,1)S(1)}, bf16[640,256]{1,0:T(8,128)(2,1)S(1)}, u32[]{:S(2)}, u32[]{:S(2)}) %collective-permute-start.16) | collective-permute-done | bytes 327712 | tf_op jit(solution)/shard_map/ppermute | solution.py:18
  123.4 3.5 %collective-permute-done.15 = bf16[256,768]{1,0:T(8,128)(2,1)S(1)} collective-permute-done((bf16[256,768]{1,0:T(8,128)(2,1)S(1)}, bf16[256,768]{1,0:T(8,128)(2,1)S(1)}, u32[]{:S(2)}, u32[]{:S(2)}) %collective-permute-start.15) | collective-permute-done | bytes 393248 | tf_op jit(solution)/shard_map/ppermute | solution.py:18
  132.8 19.7 %collective-permute-done.23 = bf16[640,256]{1,0:T(8,128)(2,1)S(1)} collective-permute-done((bf16[640,256]{1,0:T(8,128)(2,1)S(1)}, bf16[640,256]{1,0:T(8,128)(2,1)S(1)}, u32[]{:S(2)}, u32[]{:S(2)}) %collective-permute-start.23) | collective-permute-done | bytes 327712 | tf_op jit(solution)/shard_map/ppermute | solution.py:18
  158.2 3.8 %all-to-all-start.2 = ((f32[32,8,128]{2,1,0:T(8,128)}), f32[32,8,128]{2,1,0:T(8,128)S(1)}, u32[]{:S(2)}, u32[]{:S(2)}) async-start(f32[32,8,128]{2,1,0:T(8,128)} %broadcast_in_dim_broadcast_in_dim.7), calls=%async_computation.2 | async-start | bytes 262144 | tf_op jit(solution)/shard_map/all_to_all | solution.py:28
  162.1 7.8 %all-to-all-done.2 = f32[32,8,128]{2,1,0:T(8,128)S(1)} async-done(((f32[32,8,128]{2,1,0:T(8,128)}), f32[32,8,128]{2,1,0:T(8,128)S(1)}, u32[]{:S(2)}, u32[]{:S(2)}) %all-to-all-start.2) | async-done | bytes 131104 | tf_op jit(solution)/shard_map/all_to_all | solution.py:28
  183.6 4.1 %collective-permute-done.21 = f32[80,768]{1,0:T(8,128)S(1)} collective-permute-done((f32[80,768]{1,0:T(8,128)S(1)}, f32[80,768]{1,0:T(8,128)S(1)}, u32[]{:S(2)}, u32[]{:S(2)}) %collective-permute-start.21) | collective-permute-done | bytes 245792 | tf_op jit(solution)/shard_map/ppermute | solution.py:18
  187.9 3.5 %collective-permute-done.31 = f32[80,768]{1,0:T(8,128)S(1)} collective-permute-done((f32[80,768]{1,0:T(8,128)S(1)}, f32[80,768]{1,0:T(8,128)S(1)}, u32[]{:S(2)}, u32[]{:S(2)}) %collective-permute-start.31) | collective-permute-done | bytes 245792 | tf_op jit(solution)/shard_map/ppermute | solution.py:18
  193.1 4.8 %all-to-all-start.3 = ((f32[8,128,128]{2,1,0:T(8,128)}), f32[8,128,128]{2,1,0:T(8,128)S(1)}, u32[]{:S(2)}, u32[]{:S(2)}) async-start(f32[8,128,128]{2,1,0:T(8,128)} %concatenate.41), calls=%async_computation.3 | async-start | bytes 1048576 | tf_op jit(solution)/shard_map/all_to_all | solution.py:121
  198.8 15.0 %all-to-all-done.3 = f32[8,128,128]{2,1,0:T(8,128)S(1)} async-done(((f32[8,128,128]{2,1,0:T(8,128)}), f32[8,128,128]{2,1,0:T(8,128)S(1)}, u32[]{:S(2)}, u32[]{:S(2)}) %all-to-all-start.3) | async-done | bytes 524320 | tf_op jit(solution)/shard_map/all_to_all | solution.py:121
  214.9 6.1 %all-to-all-start.4 = ((bf16[16,128,128]{2,1,0:T(8,128)(2,1)}), bf16[16,128,128]{2,1,0:T(8,128)(2,1)S(1)}, u32[]{:S(2)}, u32[]{:S(2)}) async-start(bf16[16,128,128]{2,1,0:T(8,128)(2,1)} %broadcast_in_dim.41), calls=%async_computation.4 | async-start | bytes 1048576 | tf_op jit(solution)/shard_map/all_to_all | solution.py:28
  222.8 13.1 %all-to-all-done.4 = bf16[16,128,128]{2,1,0:T(8,128)(2,1)S(1)} async-done(((bf16[16,128,128]{2,1,0:T(8,128)(2,1)}), bf16[16,128,128]{2,1,0:T(8,128)(2,1)S(1)}, u32[]{:S(2)}, u32[]{:S(2)}) %all-to-all-start.4) | async-done | bytes 524320 | tf_op jit(solution)/shard_map/all_to_all | solution.py:28
  (141 shorter events, 69.8 us)
Async XLA Ops:
  3.3 20.8 %all-to-all-start = ((f32[16,8,128]{2,1,0:T(8,128)}), f32[16,8,128]{2,1,0:T(8,128)S(1)}, u32[]{:S(2)}, u32[]{:S(2)}) async-start(f32[16,8,128]{2,1,0:T(8,128)} %broadcast_in_dim.33), calls=%async_computation | async-start | bytes 131072 | tf_op jit(solution)/shard_map/all_to_all | solution.py:28
  28.3 16.6 %collective-permute-start.2 = (bf16[2,4,4,80,256]{4,3,2,1,0:T(8,128)(2,1)}, bf16[2,4,4,80,256]{4,3,2,1,0:T(8,128)(2,1)S(1)}, u32[]{:S(2)}, u32[]{:S(2)}) collective-permute-start(bf16[2,4,4,80,256]{4,3,2,1,0:T(8,128)(2,1)} %get-tuple-element.21), channel_id=1, source_target_pairs={{1,0},{0,1},{3,2},{2,3},{5,4},{4,5},{7,6},{6,7},{9,8},{8,9},{11,10... | collective-permute-start | bytes 3932168 | tf_op jit(solution)/shard_map/ppermute | solution.py:18
  43.4 24.7 %collective-permute-start.11 = (bf16[4,80,768]{2,1,0:T(8,128)(2,1)S(1)}, bf16[4,80,768]{2,1,0:T(8,128)(2,1)}, u32[]{:S(2)}, u32[]{:S(2)}) collective-permute-start(bf16[4,80,768]{2,1,0:T(8,128)(2,1)S(1)} %bitcast_dynamic-update-slice_fusion), channel_id=1, source_target_pairs={{48,0},{0,16},{16,32},{32,48},{49,1},{1,17},{17,33},{33,49},{50,2}... | collective-permute-start | bytes 1474568 | tf_op jit(solution)/shard_map/ppermute | solution.py:18
  43.4 27.1 %collective-permute-start.3 = (bf16[320,768]{1,0:T(8,128)(2,1)}, bf16[320,768]{1,0:T(8,128)(2,1)}, u32[]{:S(2)}, u32[]{:S(2)}) collective-permute-start(bf16[320,768]{1,0:T(8,128)(2,1)} %param.9), channel_id=1, source_target_pairs={{2,0},{4,2},{6,4},{0,6},{3,1},{5,3},{7,5},{1,7},{10,8},{12,10},{14... | collective-permute-start | bytes 1474568 | tf_op jit(solution)/shard_map/ppermute | solution.py:18
  44.0 26.6 %collective-permute-start.4 = (bf16[320,768]{1,0:T(8,128)(2,1)}, bf16[320,768]{1,0:T(8,128)(2,1)}, u32[]{:S(2)}, u32[]{:S(2)}) collective-permute-start(bf16[320,768]{1,0:T(8,128)(2,1)} %param.9), channel_id=1, source_target_pairs={{4,0},{6,2},{0,4},{2,6},{5,1},{7,3},{1,5},{3,7},{12,8},{14,10},{8,... | collective-permute-start | bytes 1474568 | tf_op jit(solution)/shard_map/ppermute | solution.py:18
  44.8 25.7 %collective-permute-start.5 = (bf16[320,768]{1,0:T(8,128)(2,1)}, bf16[320,768]{1,0:T(8,128)(2,1)S(1)}, u32[]{:S(2)}, u32[]{:S(2)}) collective-permute-start(bf16[320,768]{1,0:T(8,128)(2,1)} %param.9), channel_id=1, source_target_pairs={{6,0},{0,2},{2,4},{4,6},{7,1},{1,3},{3,5},{5,7},{14,8},{8,10},{10,... | collective-permute-start | bytes 1474568 | tf_op jit(solution)/shard_map/ppermute | solution.py:18
  54.1 15.9 %collective-permute-start.12 = (bf16[4,80,768]{2,1,0:T(8,128)(2,1)S(1)}, bf16[4,80,768]{2,1,0:T(8,128)(2,1)S(1)}, u32[]{:S(2)}, u32[]{:S(2)}) collective-permute-start(bf16[4,80,768]{2,1,0:T(8,128)(2,1)S(1)} %bitcast_dynamic-update-slice_fusion), channel_id=1, source_target_pairs={{32,0},{48,16},{0,32},{16,48},{33,1},{49,17},{1,33},{17,49},{34,2}... | collective-permute-start | bytes 1474568 | tf_op jit(solution)/shard_map/ppermute | solution.py:18
  75.3 15.0 %collective-permute-start.13 = (f32[256,768]{1,0:T(8,128)S(1)}, f32[256,768]{1,0:T(8,128)}, u32[]{:S(2)}, u32[]{:S(2)}) collective-permute-start(f32[256,768]{1,0:T(8,128)S(1)} %slice.49), channel_id=1, source_target_pairs={{1,0},{0,1},{3,2},{2,3},{5,4},{4,5},{7,6},{6,7},{9,8},{8,9},{11,10... | collective-permute-start | bytes 2359304 | tf_op jit(solution)/shard_map/ppermute | solution.py:18
  83.4 15.5 %collective-permute-start = (bf16[640,256]{1,0:T(8,128)(2,1)}, bf16[640,256]{1,0:T(8,128)(2,1)}, u32[]{:S(2)}, u32[]{:S(2)}) collective-permute-start(bf16[640,256]{1,0:T(8,128)(2,1)} %bitcast.7), channel_id=1, source_target_pairs={{2,0},{4,2},{6,4},{0,6},{3,1},{5,3},{7,5},{1,7},{10,8},{12,10},{14... | collective-permute-start | bytes 983048 | tf_op jit(solution)/shard_map/ppermute | solution.py:18
  92.7 28.9 %collective-permute-start.17 = (bf16[256,768]{1,0:T(8,128)(2,1)S(1)}, bf16[256,768]{1,0:T(8,128)(2,1)S(1)}, u32[]{:S(2)}, u32[]{:S(2)}) collective-permute-start(bf16[256,768]{1,0:T(8,128)(2,1)S(1)} %get-tuple-element.4), channel_id=1, source_target_pairs={{4,0},{6,2},{0,4},{2,6},{5,1},{7,3},{1,5},{3,7},{12,8},{14,10},{8,... | collective-permute-start | bytes 1179656 | tf_op jit(solution)/shard_map/ppermute | solution.py:18
  93.5 19.8 %collective-permute-start.1 = (bf16[640,256]{1,0:T(8,128)(2,1)S(1)}, bf16[640,256]{1,0:T(8,128)(2,1)S(1)}, u32[]{:S(2)}, u32[]{:S(2)}) collective-permute-start(bf16[640,256]{1,0:T(8,128)(2,1)S(1)} %bitcast.136), channel_id=1, source_target_pairs={{6,0},{0,2},{2,4},{4,6},{7,1},{1,3},{3,5},{5,7},{14,8},{8,10},{10,... | collective-permute-start | bytes 983048 | tf_op jit(solution)/shard_map/ppermute | solution.py:18
  94.0 26.3 %collective-permute-start.16 = (bf16[640,256]{1,0:T(8,128)(2,1)S(1)}, bf16[640,256]{1,0:T(8,128)(2,1)S(1)}, u32[]{:S(2)}, u32[]{:S(2)}) collective-permute-start(bf16[640,256]{1,0:T(8,128)(2,1)S(1)} %bitcast.135), channel_id=1, source_target_pairs={{4,0},{6,2},{0,4},{2,6},{5,1},{7,3},{1,5},{3,7},{12,8},{14,10},{8,... | collective-permute-start | bytes 983048 | tf_op jit(solution)/shard_map/ppermute | solution.py:18
  96.3 26.4 %collective-permute-start.14 = (bf16[256,768]{1,0:T(8,128)(2,1)S(1)}, bf16[256,768]{1,0:T(8,128)(2,1)S(1)}, u32[]{:S(2)}, u32[]{:S(2)}) collective-permute-start(bf16[256,768]{1,0:T(8,128)(2,1)S(1)} %get-tuple-element.4), channel_id=1, source_target_pairs={{2,0},{4,2},{6,4},{0,6},{3,1},{5,3},{7,5},{1,7},{10,8},{12,10},{14... | collective-permute-start | bytes 1179656 | tf_op jit(solution)/shard_map/ppermute | solution.py:18
  98.9 28.1 %collective-permute-start.15 = (bf16[256,768]{1,0:T(8,128)(2,1)S(1)}, bf16[256,768]{1,0:T(8,128)(2,1)S(1)}, u32[]{:S(2)}, u32[]{:S(2)}) collective-permute-start(bf16[256,768]{1,0:T(8,128)(2,1)S(1)} %get-tuple-element.4), channel_id=1, source_target_pairs={{6,0},{0,2},{2,4},{4,6},{7,1},{1,3},{3,5},{5,7},{14,8},{8,10},{10,... | collective-permute-start | bytes 1179656 | tf_op jit(solution)/shard_map/ppermute | solution.py:18
  113.3 17.3 %collective-permute-start.22 = (bf16[640,256]{1,0:T(8,128)(2,1)S(1)}, bf16[640,256]{1,0:T(8,128)(2,1)S(1)}, u32[]{:S(2)}, u32[]{:S(2)}) collective-permute-start(bf16[640,256]{1,0:T(8,128)(2,1)S(1)} %bitcast.138), channel_id=1, source_target_pairs={{16,0},{32,16},{48,32},{0,48},{17,1},{33,17},{49,33},{1,49},{18,2}... | collective-permute-start | bytes 983048 | tf_op jit(solution)/shard_map/ppermute | solution.py:18
  120.3 32.2 %collective-permute-start.24 = (bf16[256,768]{1,0:T(8,128)(2,1)S(1)}, bf16[256,768]{1,0:T(8,128)(2,1)S(1)}, u32[]{:S(2)}, u32[]{:S(2)}) collective-permute-start(bf16[256,768]{1,0:T(8,128)(2,1)S(1)} %get-tuple-element.4), channel_id=1, source_target_pairs={{16,0},{32,16},{48,32},{0,48},{17,1},{33,17},{49,33},{1,49},{18,2}... | collective-permute-start | bytes 1179656 | tf_op jit(solution)/shard_map/ppermute | solution.py:18
  121.6 30.9 %collective-permute-start.25 = (bf16[256,768]{1,0:T(8,128)(2,1)S(1)}, bf16[256,768]{1,0:T(8,128)(2,1)S(1)}, u32[]{:S(2)}, u32[]{:S(2)}) collective-permute-start(bf16[256,768]{1,0:T(8,128)(2,1)S(1)} %get-tuple-element.4), channel_id=1, source_target_pairs={{48,0},{0,16},{16,32},{32,48},{49,1},{1,17},{17,33},{33,49},{50,2}... | collective-permute-start | bytes 1179656 | tf_op jit(solution)/shard_map/ppermute | solution.py:18
  122.8 29.7 %collective-permute-start.23 = (bf16[640,256]{1,0:T(8,128)(2,1)S(1)}, bf16[640,256]{1,0:T(8,128)(2,1)S(1)}, u32[]{:S(2)}, u32[]{:S(2)}) collective-permute-start(bf16[640,256]{1,0:T(8,128)(2,1)S(1)} %bitcast.137), channel_id=1, source_target_pairs={{48,0},{0,16},{16,32},{32,48},{49,1},{1,17},{17,33},{33,49},{50,2}... | collective-permute-start | bytes 983048 | tf_op jit(solution)/shard_map/ppermute | solution.py:18
  126.9 26.5 %collective-permute-start.27 = (bf16[256,768]{1,0:T(8,128)(2,1)S(1)}, bf16[256,768]{1,0:T(8,128)(2,1)S(1)}, u32[]{:S(2)}, u32[]{:S(2)}) collective-permute-start(bf16[256,768]{1,0:T(8,128)(2,1)S(1)} %get-tuple-element.4), channel_id=1, source_target_pairs={{32,0},{48,16},{0,32},{16,48},{33,1},{49,17},{1,33},{17,49},{34,2}... | collective-permute-start | bytes 1179656 | tf_op jit(solution)/shard_map/ppermute | solution.py:18
  130.6 22.8 %collective-permute-start.26 = (bf16[640,256]{1,0:T(8,128)(2,1)S(1)}, bf16[640,256]{1,0:T(8,128)(2,1)S(1)}, u32[]{:S(2)}, u32[]{:S(2)}) collective-permute-start(bf16[640,256]{1,0:T(8,128)(2,1)S(1)} %bitcast.133), channel_id=1, source_target_pairs={{32,0},{48,16},{0,32},{16,48},{33,1},{49,17},{1,33},{17,49},{34,2}... | collective-permute-start | bytes 983048 | tf_op jit(solution)/shard_map/ppermute | solution.py:18
  152.5 18.1 %collective-permute-start.18 = (f32[4,80,768]{2,1,0:T(8,128)S(1)}, f32[4,80,768]{2,1,0:T(8,128)}, u32[]{:S(2)}, u32[]{:S(2)}) collective-permute-start(f32[4,80,768]{2,1,0:T(8,128)S(1)} %dynamic-slice_bitcast_fusion.3), channel_id=1, source_target_pairs={{1,0},{0,1},{3,2},{2,3},{5,4},{4,5},{7,6},{6,7},{9,8},{8,9},{11,10... | collective-permute-start | bytes 2949128 | tf_op jit(solution)/shard_map/ppermute | solution.py:18
  156.4 18.4 %collective-permute-start.28 = (f32[4,80,768]{2,1,0:T(8,128)}, f32[4,80,768]{2,1,0:T(8,128)}, u32[]{:S(2)}, u32[]{:S(2)}) collective-permute-start(f32[4,80,768]{2,1,0:T(8,128)} %dynamic-slice_bitcast_fusion.2), channel_id=1, source_target_pairs={{1,0},{0,1},{3,2},{2,3},{5,4},{4,5},{7,6},{6,7},{9,8},{8,9},{11,10... | collective-permute-start | bytes 2949128 | tf_op jit(solution)/shard_map/ppermute | solution.py:18
  193.1 20.7 %all-to-all-start.3 = ((f32[8,128,128]{2,1,0:T(8,128)}), f32[8,128,128]{2,1,0:T(8,128)S(1)}, u32[]{:S(2)}, u32[]{:S(2)}) async-start(f32[8,128,128]{2,1,0:T(8,128)} %concatenate.41), calls=%async_computation.3 | async-start | bytes 1048576 | tf_op jit(solution)/shard_map/all_to_all | solution.py:121
  214.9 21.1 %all-to-all-start.4 = ((bf16[16,128,128]{2,1,0:T(8,128)(2,1)}), bf16[16,128,128]{2,1,0:T(8,128)(2,1)S(1)}, u32[]{:S(2)}, u32[]{:S(2)}) async-start(bf16[16,128,128]{2,1,0:T(8,128)(2,1)} %broadcast_in_dim.41), calls=%async_computation.4 | async-start | bytes 1048576 | tf_op jit(solution)/shard_map/all_to_all | solution.py:28
  (23 other events, 196.8 us)

commit v3 on v2

--- a/solution.py
+++ b/solution.py
@@ -18,8 +18,9 @@
     return lax.ppermute(value, axis, [((i + step) % n, i) for i in range(n)])
 
 
-def ring_blocks(value, axis):
-    one, three, two = (fetch(value, axis, step) for step in (1, 3, 2))
+def ring_blocks(value, axis, relay=True):
+    one, three = (fetch(value, axis, step) for step in (1, 3))
+    two = fetch(one, axis, 1) if relay else fetch(value, axis, 2)
     return [value, one, two, three]
 
 
@@ -53,7 +54,7 @@
     other = fetch(lax.dynamic_slice_in_dim(w_key, x * part, part), ZH, 1)
     near = ring_blocks(w_key, Y)
     quarter = jnp.zeros((4, part, features), w_key.dtype)
-    for step, piece in enumerate(ring_blocks(other, Y)):
+    for step, piece in enumerate(ring_blocks(other, Y, relay=False)):
         quarter = lax.dynamic_update_index_in_dim(quarter, piece, (y + step) & 3, 0)
     far = [block.reshape(own, features) for block in ring_blocks(quarter, X)]
 

time: 240 us -> 212 us (0.88)
  waiting for transfers between devices: 122 us -> 86.4 us
  starting transfers between devices: 69 us -> 75.6 us
    ppermute x32, waiting for transfers between devices: 80.9 us -> 52.9 us  [fetch(): return lax.ppermute(value, axis, [((i + step) % n, i) for i in range(n)])]
    all_to_all x4, waiting for transfers between devices: 26 us -> 19.4 us  [from_everyone(): return lax.all_to_all(copies, axes, split_axis=0, concat_axis=0, tiled=True)]
    all_to_all x4, starting transfers between devices: 25.3 us -> 29.3 us  [from_everyone(): return lax.all_to_all(copies, axes, split_axis=0, concat_axis=0, tiled=True)]
    unnamed x22 -> x18, local copies, waits for them, and re-layouts: 6.28 us -> 4.61 us
  transfers between devices with their start and end apart: 37 -> 37, of which waited for: 18 -> 17; matrix products, arithmetic and copies ran while one was open for 13% -> 16% of each run, Pallas kernels for 0% -> 0%
where the time goes in v3:
time: 212 us; the launch traced here: 210 us
  waiting for transfers between devices  86.4 us (41%)
  starting transfers between devices  75.6 us (36%)
  local copies, waits for them, and re-layouts  20 us (9%)
  matrix products  11.1 us (5%)
  other arithmetic  10.9 us (5%)
  between operations  5.53 us (3%)
    ppermute x32, waiting for transfers between devices, fetch(): return lax.ppermute(value, axis, [((i + step) % n, i) for i in range(n)])  52.9 us
    ppermute x32, starting transfers between devices, fetch(): return lax.ppermute(value, axis, [((i + step) % n, i) for i in range(n)])  41.2 us
    all_to_all x4, starting transfers between devices, from_everyone(): return lax.all_to_all(copies, axes, split_axis=0, concat_axis=0, tiled=True)  29.3 us
    all_to_all x4, waiting for transfers between devices, from_everyone(): return lax.all_to_all(copies, axes, split_axis=0, concat_axis=0, tiled=True)  19.4 us
    all_to_all x1, waiting for transfers between devices, body(): lax.all_to_all(pieces, (ZH, ZL), split_axis=0, concat_axis=0, tiled=True)  14.1 us
    dot_general x5, matrix products, rows_by(): lax.dot_general(left, right, (((0,), (0,)), ((), ())), preferred_element_...  7.12 us
    all_to_all x1, starting transfers between devices, body(): lax.all_to_all(pieces, (ZH, ZL), split_axis=0, concat_axis=0, tiled=True)  5.1 us
    unnamed x18, local copies, waits for them, and re-layouts  4.61 us
  transfers between devices with their start and end apart: 37, of which 17 were waited for; matrix products, arithmetic and copies ran while one was open for 16% of the time, Pallas kernels for 0%

profile of v3, /device:TPU:32, one launch (start us, length us, event | category | flops | bytes accessed | tf_op | source)
XLA Modules:
  0.0 209.5 jit_solution(7927497282121494809)
XLA Ops:
  3.3 10.3 %all-to-all-start = ((f32[16,8,128]{2,1,0:T(8,128)}), f32[16,8,128]{2,1,0:T(8,128)S(1)}, u32[]{:S(2)}, u32[]{:S(2)}) async-start(f32[16,8,128]{2,1,0:T(8,128)} %broadcast_in_dim.33), calls=%async_computation | async-start | bytes 131072 | tf_op jit(solution)/shard_map/all_to_all | solution.py:29
  13.6 3.1 %collective-permute-start.3 = (bf16[320,768]{1,0:T(8,128)(2,1)}, bf16[320,768]{1,0:T(8,128)(2,1)}, u32[]{:S(2)}, u32[]{:S(2)}) collective-permute-start(bf16[320,768]{1,0:T(8,128)(2,1)} %param.9), channel_id=1, source_target_pairs={{2,0},{4,2},{6,4},{0,6},{3,1},{5,3},{7,5},{1,7},{10,8},{12,10},{14... | collective-permute-start | bytes 1474568 | tf_op jit(solution)/shard_map/ppermute | solution.py:18
  17.7 5.5 %collective-permute-start.6 = (bf16[80,768]{1,0:T(8,128)(2,1)S(1)}, bf16[80,768]{1,0:T(8,128)(2,1)S(1)}, u32[]{:S(2)}, u32[]{:S(2)}) collective-permute-start(bf16[80,768]{1,0:T(8,128)(2,1)S(1)} %constant_dynamic-slice_fusion.6), channel_id=1, source_target_pairs={{8,0},{0,8},{9,1},{1,9},{10,2},{2,10},{11,3},{3,11},{12,4},{4,12},... | collective-permute-start | bytes 368648 | tf_op jit(solution)/shard_map/ppermute | solution.py:18
  23.1 3.0 %copy.24 = bf16[256,5120]{0,1:T(8,128)(2,1)S(1)} copy(bf16[256,5120]{1,0:T(8,128)(2,1)} %param.6) | data formatting | bytes 5242880 | tf_op args[0]
  33.3 3.9 %collective-permute-done.7 = bf16[80,768]{1,0:T(8,128)(2,1)S(1)} collective-permute-done((bf16[80,768]{1,0:T(8,128)(2,1)S(1)}, bf16[80,768]{1,0:T(8,128)(2,1)S(1)}, u32[]{:S(2)}, u32[]{:S(2)}) %collective-permute-start.7) | collective-permute-done | bytes 122912 | tf_op jit(solution)/shard_map/ppermute | solution.py:18
  41.4 2.8 %collective-permute-start.10 = (bf16[4,80,768]{2,1,0:T(8,128)(2,1)S(1)}, bf16[4,80,768]{2,1,0:T(8,128)(2,1)}, u32[]{:S(2)}, u32[]{:S(2)}) collective-permute-start(bf16[4,80,768]{2,1,0:T(8,128)(2,1)S(1)} %bitcast_dynamic-update-slice_fusion), channel_id=1, source_target_pairs={{16,0},{32,16},{48,32},{0,48},{17,1},{33,17},{49,33},{1,49},{18,2}... | collective-permute-start | bytes 1474568 | tf_op jit(solution)/shard_map/ppermute | solution.py:18
  44.3 3.2 %collective-permute-start.4 = (bf16[320,768]{1,0:T(8,128)(2,1)}, bf16[320,768]{1,0:T(8,128)(2,1)S(1)}, u32[]{:S(2)}, u32[]{:S(2)}) collective-permute-start(bf16[320,768]{1,0:T(8,128)(2,1)} %collective-permute-done.3), channel_id=1, source_target_pairs={{2,0},{4,2},{6,4},{0,6},{3,1},{5,3},{7,5},{1,7},{10,8},{12,10},{14... | collective-permute-start | bytes 1474568 | tf_op jit(solution)/shard_map/ppermute | solution.py:18
  47.5 7.4 %collective-permute-done.10 = bf16[4,80,768]{2,1,0:T(8,128)(2,1)} collective-permute-done((bf16[4,80,768]{2,1,0:T(8,128)(2,1)S(1)}, bf16[4,80,768]{2,1,0:T(8,128)(2,1)}, u32[]{:S(2)}, u32[]{:S(2)}) %collective-permute-start.10) | collective-permute-done | bytes 491552 | tf_op jit(solution)/shard_map/ppermute | solution.py:18
  55.0 3.8 %collective-permute-start.12 = (bf16[4,80,768]{2,1,0:T(8,128)(2,1)}, bf16[4,80,768]{2,1,0:T(8,128)(2,1)S(1)}, u32[]{:S(2)}, u32[]{:S(2)}) collective-permute-start(bf16[4,80,768]{2,1,0:T(8,128)(2,1)} %collective-permute-done.10), channel_id=1, source_target_pairs={{16,0},{32,16},{48,32},{0,48},{17,1},{33,17},{49,33},{1,49},{18,2}... | collective-permute-start | bytes 1474568 | tf_op jit(solution)/shard_map/ppermute | solution.py:18
  65.5 3.4 %collective-permute-done.12 = bf16[4,80,768]{2,1,0:T(8,128)(2,1)S(1)} collective-permute-done((bf16[4,80,768]{2,1,0:T(8,128)(2,1)}, bf16[4,80,768]{2,1,0:T(8,128)(2,1)S(1)}, u32[]{:S(2)}, u32[]{:S(2)}) %collective-permute-start.12) | collective-permute-done | bytes 491552 | tf_op jit(solution)/shard_map/ppermute | solution.py:18
  72.8 7.2 %all-to-all-start.1 = ((f32[16,8,128]{2,1,0:T(8,128)}), f32[16,8,128]{2,1,0:T(8,128)S(1)}, u32[]{:S(2)}, u32[]{:S(2)}) async-start(f32[16,8,128]{2,1,0:T(8,128)} %broadcast_in_dim_broadcast_in_dim.6), calls=%async_computation.1 | async-start | bytes 131072 | tf_op jit(solution)/shard_map/all_to_all | solution.py:29
  95.6 5.2 %collective-permute-done.14 = bf16[256,768]{1,0:T(8,128)(2,1)S(1)} collective-permute-done((bf16[256,768]{1,0:T(8,128)(2,1)S(1)}, bf16[256,768]{1,0:T(8,128)(2,1)S(1)}, u32[]{:S(2)}, u32[]{:S(2)}) %collective-permute-start.14) | collective-permute-done | bytes 393248 | tf_op jit(solution)/shard_map/ppermute | solution.py:18
  100.7 2.7 %collective-permute-start.17 = (bf16[256,768]{1,0:T(8,128)(2,1)S(1)}, bf16[256,768]{1,0:T(8,128)(2,1)S(1)}, u32[]{:S(2)}, u32[]{:S(2)}) collective-permute-start(bf16[256,768]{1,0:T(8,128)(2,1)S(1)} %collective-permute-done.14), channel_id=1, source_target_pairs={{2,0},{4,2},{6,4},{0,6},{3,1},{5,3},{7,5},{1,7},{10,8},{12,10},{14... | collective-permute-start | bytes 1179656 | tf_op jit(solution)/shard_map/ppermute | solution.py:18
  105.6 6.1 %collective-permute-done.23 = bf16[640,256]{1,0:T(8,128)(2,1)S(1)} collective-permute-done((bf16[640,256]{1,0:T(8,128)(2,1)S(1)}, bf16[640,256]{1,0:T(8,128)(2,1)S(1)}, u32[]{:S(2)}, u32[]{:S(2)}) %collective-permute-start.23) | collective-permute-done | bytes 327712 | tf_op jit(solution)/shard_map/ppermute | solution.py:18
  114.7 2.8 %collective-permute-done.17 = bf16[256,768]{1,0:T(8,128)(2,1)S(1)} collective-permute-done((bf16[256,768]{1,0:T(8,128)(2,1)S(1)}, bf16[256,768]{1,0:T(8,128)(2,1)S(1)}, u32[]{:S(2)}, u32[]{:S(2)}) %collective-permute-start.17) | collective-permute-done | bytes 393248 | tf_op jit(solution)/shard_map/ppermute | solution.py:18
  120.6 6.5 %collective-permute-done.27 = bf16[256,768]{1,0:T(8,128)(2,1)S(1)} collective-permute-done((bf16[256,768]{1,0:T(8,128)(2,1)S(1)}, bf16[256,768]{1,0:T(8,128)(2,1)S(1)}, u32[]{:S(2)}, u32[]{:S(2)}) %collective-permute-start.27) | collective-permute-done | bytes 393248 | tf_op jit(solution)/shard_map/ppermute | solution.py:18
  129.9 5.6 %all-to-all-start.2 = ((f32[32,8,128]{2,1,0:T(8,128)}), f32[32,8,128]{2,1,0:T(8,128)S(1)}, u32[]{:S(2)}, u32[]{:S(2)}) async-start(f32[32,8,128]{2,1,0:T(8,128)} %broadcast_in_dim_broadcast_in_dim.7), calls=%async_computation.2 | async-start | bytes 262144 | tf_op jit(solution)/shard_map/all_to_all | solution.py:29
  135.6 7.8 %all-to-all-done.2 = f32[32,8,128]{2,1,0:T(8,128)S(1)} async-done(((f32[32,8,128]{2,1,0:T(8,128)}), f32[32,8,128]{2,1,0:T(8,128)S(1)}, u32[]{:S(2)}, u32[]{:S(2)}) %all-to-all-start.2) | async-done | bytes 131104 | tf_op jit(solution)/shard_map/all_to_all | solution.py:29
  151.4 3.2 %collective-permute-done.19 = f32[80,768]{1,0:T(8,128)S(1)} collective-permute-done((f32[80,768]{1,0:T(8,128)S(1)}, f32[80,768]{1,0:T(8,128)S(1)}, u32[]{:S(2)}, u32[]{:S(2)}) %collective-permute-start.19) | collective-permute-done | bytes 245792 | tf_op jit(solution)/shard_map/ppermute | solution.py:18
  157.3 4.1 %collective-permute-done.21 = f32[80,768]{1,0:T(8,128)S(1)} collective-permute-done((f32[80,768]{1,0:T(8,128)S(1)}, f32[80,768]{1,0:T(8,128)S(1)}, u32[]{:S(2)}, u32[]{:S(2)}) %collective-permute-start.21) | collective-permute-done | bytes 245792 | tf_op jit(solution)/shard_map/ppermute | solution.py:18
  165.5 5.1 %all-to-all-start.3 = ((f32[8,128,128]{2,1,0:T(8,128)}), f32[8,128,128]{2,1,0:T(8,128)S(1)}, u32[]{:S(2)}, u32[]{:S(2)}) async-start(f32[8,128,128]{2,1,0:T(8,128)} %concatenate.41), calls=%async_computation.3 | async-start | bytes 1048576 | tf_op jit(solution)/shard_map/all_to_all | solution.py:122
  171.5 14.1 %all-to-all-done.3 = f32[8,128,128]{2,1,0:T(8,128)S(1)} async-done(((f32[8,128,128]{2,1,0:T(8,128)}), f32[8,128,128]{2,1,0:T(8,128)S(1)}, u32[]{:S(2)}, u32[]{:S(2)}) %all-to-all-start.3) | async-done | bytes 524320 | tf_op jit(solution)/shard_map/all_to_all | solution.py:122
  186.7 6.1 %all-to-all-start.4 = ((bf16[16,128,128]{2,1,0:T(8,128)(2,1)}), bf16[16,128,128]{2,1,0:T(8,128)(2,1)S(1)}, u32[]{:S(2)}, u32[]{:S(2)}) async-start(bf16[16,128,128]{2,1,0:T(8,128)(2,1)} %broadcast_in_dim.41), calls=%async_computation.4 | async-start | bytes 1048576 | tf_op jit(solution)/shard_map/all_to_all | solution.py:29
  194.7 11.6 %all-to-all-done.4 = bf16[16,128,128]{2,1,0:T(8,128)(2,1)S(1)} async-done(((bf16[16,128,128]{2,1,0:T(8,128)(2,1)}), bf16[16,128,128]{2,1,0:T(8,128)(2,1)S(1)}, u32[]{:S(2)}, u32[]{:S(2)}) %all-to-all-start.4) | async-done | bytes 524320 | tf_op jit(solution)/shard_map/all_to_all | solution.py:29
  (135 shorter events, 69.3 us)
Async XLA Ops:
  3.3 23.5 %all-to-all-start = ((f32[16,8,128]{2,1,0:T(8,128)}), f32[16,8,128]{2,1,0:T(8,128)S(1)}, u32[]{:S(2)}, u32[]{:S(2)}) async-start(f32[16,8,128]{2,1,0:T(8,128)} %broadcast_in_dim.33), calls=%async_computation | async-start | bytes 131072 | tf_op jit(solution)/shard_map/all_to_all | solution.py:29
  13.6 30.7 %collective-permute-start.3 = (bf16[320,768]{1,0:T(8,128)(2,1)}, bf16[320,768]{1,0:T(8,128)(2,1)}, u32[]{:S(2)}, u32[]{:S(2)}) collective-permute-start(bf16[320,768]{1,0:T(8,128)(2,1)} %param.9), channel_id=1, source_target_pairs={{2,0},{4,2},{6,4},{0,6},{3,1},{5,3},{7,5},{1,7},{10,8},{12,10},{14... | collective-permute-start | bytes 1474568 | tf_op jit(solution)/shard_map/ppermute | solution.py:18
  17.7 13.3 %collective-permute-start.6 = (bf16[80,768]{1,0:T(8,128)(2,1)S(1)}, bf16[80,768]{1,0:T(8,128)(2,1)S(1)}, u32[]{:S(2)}, u32[]{:S(2)}) collective-permute-start(bf16[80,768]{1,0:T(8,128)(2,1)S(1)} %constant_dynamic-slice_fusion.6), channel_id=1, source_target_pairs={{8,0},{0,8},{9,1},{1,9},{10,2},{2,10},{11,3},{3,11},{12,4},{4,12},... | collective-permute-start | bytes 368648 | tf_op jit(solution)/shard_map/ppermute | solution.py:18
  31.0 27.8 %collective-permute-start.2 = (bf16[2,4,4,80,256]{4,3,2,1,0:T(8,128)(2,1)}, bf16[2,4,4,80,256]{4,3,2,1,0:T(8,128)(2,1)S(1)}, u32[]{:S(2)}, u32[]{:S(2)}) collective-permute-start(bf16[2,4,4,80,256]{4,3,2,1,0:T(8,128)(2,1)} %get-tuple-element.21), channel_id=1, source_target_pairs={{1,0},{0,1},{3,2},{2,3},{5,4},{4,5},{7,6},{6,7},{9,8},{8,9},{11,10... | collective-permute-start | bytes 3932168 | tf_op jit(solution)/shard_map/ppermute | solution.py:18
  41.4 13.5 %collective-permute-start.10 = (bf16[4,80,768]{2,1,0:T(8,128)(2,1)S(1)}, bf16[4,80,768]{2,1,0:T(8,128)(2,1)}, u32[]{:S(2)}, u32[]{:S(2)}) collective-permute-start(bf16[4,80,768]{2,1,0:T(8,128)(2,1)S(1)} %bitcast_dynamic-update-slice_fusion), channel_id=1, source_target_pairs={{16,0},{32,16},{48,32},{0,48},{17,1},{33,17},{49,33},{1,49},{18,2}... | collective-permute-start | bytes 1474568 | tf_op jit(solution)/shard_map/ppermute | solution.py:18
  44.3 14.6 %collective-permute-start.11 = (bf16[4,80,768]{2,1,0:T(8,128)(2,1)S(1)}, bf16[4,80,768]{2,1,0:T(8,128)(2,1)}, u32[]{:S(2)}, u32[]{:S(2)}) collective-permute-start(bf16[4,80,768]{2,1,0:T(8,128)(2,1)S(1)} %bitcast_dynamic-update-slice_fusion), channel_id=1, source_target_pairs={{48,0},{0,16},{16,32},{32,48},{49,1},{1,17},{17,33},{33,49},{50,2}... | collective-permute-start | bytes 1474568 | tf_op jit(solution)/shard_map/ppermute | solution.py:18
  44.3 18.7 %collective-permute-start.5 = (bf16[320,768]{1,0:T(8,128)(2,1)}, bf16[320,768]{1,0:T(8,128)(2,1)}, u32[]{:S(2)}, u32[]{:S(2)}) collective-permute-start(bf16[320,768]{1,0:T(8,128)(2,1)} %param.9), channel_id=1, source_target_pairs={{6,0},{0,2},{2,4},{4,6},{7,1},{1,3},{3,5},{5,7},{14,8},{8,10},{10,... | collective-permute-start | bytes 1474568 | tf_op jit(solution)/shard_map/ppermute | solution.py:18
  44.3 18.7 %collective-permute-start.4 = (bf16[320,768]{1,0:T(8,128)(2,1)}, bf16[320,768]{1,0:T(8,128)(2,1)S(1)}, u32[]{:S(2)}, u32[]{:S(2)}) collective-permute-start(bf16[320,768]{1,0:T(8,128)(2,1)} %collective-permute-done.3), channel_id=1, source_target_pairs={{2,0},{4,2},{6,4},{0,6},{3,1},{5,3},{7,5},{1,7},{10,8},{12,10},{14... | collective-permute-start | bytes 1474568 | tf_op jit(solution)/shard_map/ppermute | solution.py:18
  55.0 13.9 %collective-permute-start.12 = (bf16[4,80,768]{2,1,0:T(8,128)(2,1)}, bf16[4,80,768]{2,1,0:T(8,128)(2,1)S(1)}, u32[]{:S(2)}, u32[]{:S(2)}) collective-permute-start(bf16[4,80,768]{2,1,0:T(8,128)(2,1)} %collective-permute-done.10), channel_id=1, source_target_pairs={{16,0},{32,16},{48,32},{0,48},{17,1},{33,17},{49,33},{1,49},{18,2}... | collective-permute-start | bytes 1474568 | tf_op jit(solution)/shard_map/ppermute | solution.py:18
  70.8 17.4 %collective-permute-start.13 = (f32[256,768]{1,0:T(8,128)S(1)}, f32[256,768]{1,0:T(8,128)}, u32[]{:S(2)}, u32[]{:S(2)}) collective-permute-start(f32[256,768]{1,0:T(8,128)S(1)} %slice.49), channel_id=1, source_target_pairs={{1,0},{0,1},{3,2},{2,3},{5,4},{4,5},{7,6},{6,7},{9,8},{8,9},{11,10... | collective-permute-start | bytes 2359304 | tf_op jit(solution)/shard_map/ppermute | solution.py:18
  72.8 14.1 %all-to-all-start.1 = ((f32[16,8,128]{2,1,0:T(8,128)}), f32[16,8,128]{2,1,0:T(8,128)S(1)}, u32[]{:S(2)}, u32[]{:S(2)}) async-start(f32[16,8,128]{2,1,0:T(8,128)} %broadcast_in_dim_broadcast_in_dim.6), calls=%async_computation.1 | async-start | bytes 131072 | tf_op jit(solution)/shard_map/all_to_all | solution.py:29
  81.1 12.7 %collective-permute-start.1 = (bf16[640,256]{1,0:T(8,128)(2,1)}, bf16[640,256]{1,0:T(8,128)(2,1)}, u32[]{:S(2)}, u32[]{:S(2)}) collective-permute-start(bf16[640,256]{1,0:T(8,128)(2,1)} %bitcast.8), channel_id=1, source_target_pairs={{6,0},{0,2},{2,4},{4,6},{7,1},{1,3},{3,5},{5,7},{14,8},{8,10},{10,... | collective-permute-start | bytes 983048 | tf_op jit(solution)/shard_map/ppermute | solution.py:18
  92.7 19.6 %collective-permute-start.24 = (bf16[256,768]{1,0:T(8,128)(2,1)S(1)}, bf16[256,768]{1,0:T(8,128)(2,1)S(1)}, u32[]{:S(2)}, u32[]{:S(2)}) collective-permute-start(bf16[256,768]{1,0:T(8,128)(2,1)S(1)} %get-tuple-element.4), channel_id=1, source_target_pairs={{16,0},{32,16},{48,32},{0,48},{17,1},{33,17},{49,33},{1,49},{18,2}... | collective-permute-start | bytes 1179656 | tf_op jit(solution)/shard_map/ppermute | solution.py:18
  93.8 18.5 %collective-permute-start.25 = (bf16[256,768]{1,0:T(8,128)(2,1)S(1)}, bf16[256,768]{1,0:T(8,128)(2,1)S(1)}, u32[]{:S(2)}, u32[]{:S(2)}) collective-permute-start(bf16[256,768]{1,0:T(8,128)(2,1)S(1)} %get-tuple-element.4), channel_id=1, source_target_pairs={{48,0},{0,16},{16,32},{32,48},{49,1},{1,17},{17,33},{33,49},{50,2}... | collective-permute-start | bytes 1179656 | tf_op jit(solution)/shard_map/ppermute | solution.py:18
  94.7 17.0 %collective-permute-start.23 = (bf16[640,256]{1,0:T(8,128)(2,1)S(1)}, bf16[640,256]{1,0:T(8,128)(2,1)S(1)}, u32[]{:S(2)}, u32[]{:S(2)}) collective-permute-start(bf16[640,256]{1,0:T(8,128)(2,1)S(1)} %bitcast.136), channel_id=1, source_target_pairs={{48,0},{0,16},{16,32},{32,48},{49,1},{1,17},{17,33},{33,49},{50,2}... | collective-permute-start | bytes 983048 | tf_op jit(solution)/shard_map/ppermute | solution.py:18
  100.7 16.8 %collective-permute-start.17 = (bf16[256,768]{1,0:T(8,128)(2,1)S(1)}, bf16[256,768]{1,0:T(8,128)(2,1)S(1)}, u32[]{:S(2)}, u32[]{:S(2)}) collective-permute-start(bf16[256,768]{1,0:T(8,128)(2,1)S(1)} %collective-permute-done.14), channel_id=1, source_target_pairs={{2,0},{4,2},{6,4},{0,6},{3,1},{5,3},{7,5},{1,7},{10,8},{12,10},{14... | collective-permute-start | bytes 1179656 | tf_op jit(solution)/shard_map/ppermute | solution.py:18
  113.2 13.9 %collective-permute-start.27 = (bf16[256,768]{1,0:T(8,128)(2,1)S(1)}, bf16[256,768]{1,0:T(8,128)(2,1)S(1)}, u32[]{:S(2)}, u32[]{:S(2)}) collective-permute-start(bf16[256,768]{1,0:T(8,128)(2,1)S(1)} %collective-permute-done.24), channel_id=1, source_target_pairs={{16,0},{32,16},{48,32},{0,48},{17,1},{33,17},{49,33},{1,49},{18,2}... | collective-permute-start | bytes 1179656 | tf_op jit(solution)/shard_map/ppermute | solution.py:18
  119.1 24.9 %collective-permute-start.18 = (f32[4,80,768]{2,1,0:T(8,128)}, f32[4,80,768]{2,1,0:T(8,128)}, u32[]{:S(2)}, u32[]{:S(2)}) collective-permute-start(f32[4,80,768]{2,1,0:T(8,128)} %dynamic-slice_bitcast_fusion.3), channel_id=1, source_target_pairs={{1,0},{0,1},{3,2},{2,3},{5,4},{4,5},{7,6},{6,7},{9,8},{8,9},{11,10... | collective-permute-start | bytes 2949128 | tf_op jit(solution)/shard_map/ppermute | solution.py:18
  128.6 19.9 %collective-permute-start.28 = (f32[4,80,768]{2,1,0:T(8,128)}, f32[4,80,768]{2,1,0:T(8,128)S(1)}, u32[]{:S(2)}, u32[]{:S(2)}) collective-permute-start(f32[4,80,768]{2,1,0:T(8,128)} %dynamic-slice_bitcast_fusion.2), channel_id=1, source_target_pairs={{1,0},{0,1},{3,2},{2,3},{5,4},{4,5},{7,6},{6,7},{9,8},{8,9},{11,10... | collective-permute-start | bytes 2949128 | tf_op jit(solution)/shard_map/ppermute | solution.py:18
  129.9 13.5 %all-to-all-start.2 = ((f32[32,8,128]{2,1,0:T(8,128)}), f32[32,8,128]{2,1,0:T(8,128)S(1)}, u32[]{:S(2)}, u32[]{:S(2)}) async-start(f32[32,8,128]{2,1,0:T(8,128)} %broadcast_in_dim_broadcast_in_dim.7), calls=%async_computation.2 | async-start | bytes 262144 | tf_op jit(solution)/shard_map/all_to_all | solution.py:29
  148.4 12.9 %collective-permute-start.21 = (f32[80,768]{1,0:T(8,128)S(1)}, f32[80,768]{1,0:T(8,128)S(1)}, u32[]{:S(2)}, u32[]{:S(2)}) collective-permute-start(f32[80,768]{1,0:T(8,128)S(1)} %get-tuple-element.24), channel_id=1, source_target_pairs={{48,0},{0,16},{16,32},{32,48},{49,1},{1,17},{17,33},{33,49},{50,2}... | collective-permute-start | bytes 737288 | tf_op jit(solution)/shard_map/ppermute | solution.py:18
  148.7 12.7 %collective-permute-start.29 = (f32[80,768]{1,0:T(8,128)S(1)}, f32[80,768]{1,0:T(8,128)S(1)}, u32[]{:S(2)}, u32[]{:S(2)}) collective-permute-start(f32[80,768]{1,0:T(8,128)S(1)} %get-tuple-element.28), channel_id=1, source_target_pairs={{2,0},{4,2},{6,4},{0,6},{3,1},{5,3},{7,5},{1,7},{10,8},{12,10},{14... | collective-permute-start | bytes 737288 | tf_op jit(solution)/shard_map/ppermute | solution.py:18
  165.5 20.1 %all-to-all-start.3 = ((f32[8,128,128]{2,1,0:T(8,128)}), f32[8,128,128]{2,1,0:T(8,128)S(1)}, u32[]{:S(2)}, u32[]{:S(2)}) async-start(f32[8,128,128]{2,1,0:T(8,128)} %concatenate.41), calls=%async_computation.3 | async-start | bytes 1048576 | tf_op jit(solution)/shard_map/all_to_all | solution.py:122
  186.7 19.6 %all-to-all-start.4 = ((bf16[16,128,128]{2,1,0:T(8,128)(2,1)}), bf16[16,128,128]{2,1,0:T(8,128)(2,1)S(1)}, u32[]{:S(2)}, u32[]{:S(2)}) async-start(bf16[16,128,128]{2,1,0:T(8,128)(2,1)} %broadcast_in_dim.41), calls=%async_computation.4 | async-start | bytes 1048576 | tf_op jit(solution)/shard_map/all_to_all | solution.py:29
  (21 other events, 179.5 us)

commit v4 on v3

--- a/solution.py
+++ b/solution.py
@@ -72,8 +72,8 @@
     normed = (values * inverse_rms * gains).astype(jnp.bfloat16)
 
     turned = normed.T.reshape(2, 4, 2, 4, part, rows)
-    theirs = fetch(block(turned, None, None, 1 - core), C, 1)
-    pair = jnp.concatenate([block(turned, None, None, core), theirs], axis=-1)
+    own_cols, their_cols = block(turned, None, None, core), block(turned, None, None, 1 - core)
+    pair = jnp.concatenate([own_cols, fetch(their_cols, C, 1)], axis=-1)
     near_half = [block(pair, zh, (y + s) & 3).reshape(own, -1) for s in range(4)]
     far_half = [block(pair, 1 - zh, None, (x + s) & 3).reshape(own, -1) for s in range(4)]
     near_cols = [block(turned, zh, (y + s) & 3).reshape(2 * own, rows) for s in range(4)]
@@ -116,22 +116,24 @@
     def tiled(value):
         return value.reshape(-1, 2, tall, 8, 2, wide, 128).transpose(0, 1, 4, 2, 5, 3, 6)
 
-    plane_sum = summed(own_sum, (X, Y, C))
+    near_loss = summed(own_sum, (Y, C))
     pieces = tiled(both).reshape(8, -1, 128)
-    pieces = jnp.concatenate([pieces, jnp.broadcast_to(plane_sum, (8, 8, 128))], axis=1)
+    pieces = jnp.concatenate([pieces, jnp.broadcast_to(near_loss, (8, 8, 128))], axis=1)
     pieces = lax.all_to_all(pieces, (ZH, ZL), split_axis=0, concat_axis=0, tiled=True).sum(axis=0)
-    loss = pieces[-1, 0] / (2.0 * features * total_count)
 
     piece = pieces[:-8]
     mine = tiled(block(w_key.reshape(4, part, features), x)).reshape(4, -1, 128)
     share = (piece * block(mine, lax.axis_index(ZL)).astype(jnp.float32)).sum(axis=1)
+    share = jnp.concatenate([share, pieces[-1, :8]])
     lines = []
     for _ in range(3):
         lines.append(lax.reduce_precision(share, 8, 7))
         share = share - lines[-1]
-    lines = jnp.pad(jnp.stack(lines), ((0, 5), (0, 128 - share.size)))
+    lines = jnp.pad(jnp.stack(lines), ((0, 5), (0, 0)))
     whole = from_everyone(jnp.concatenate([piece, lines]).astype(jnp.bfloat16), DP)
-    shares = whole[:, -8:-5, : share.size].astype(jnp.float32).sum(axis=1).reshape(2, 2, 4, tall, wide, 8)
+    shares = whole[:, -8:-5].astype(jnp.float32).sum(axis=1)
+    loss = shares[:4, -1].sum() / (2.0 * features * total_count)
+    shares = shares[:, :-8].reshape(2, 2, 4, tall, wide, 8)
     grad_gain = shares.sum(axis=(1, 4)).swapaxes(0, 1).reshape(own) / norm_gain.astype(jnp.float32)
     whole = whole[:, :-8].reshape(2, 2, 4, tall, wide, 8, 128)
     grad_key = whole.transpose(2, 0, 3, 5, 1, 4, 6).reshape(own, features).astype(jnp.float32)

time: 212 us -> 208 us (0.981)
  waiting for transfers between devices: 86.4 us -> 82.6 us
    all_to_all x1, waiting for transfers between devices: 14.1 us -> 10.9 us  [body(): lax.all_to_all(pieces, (ZH, ZL), split_axis=0, concat_axis=0, tiled=True)]
  transfers between devices with their start and end apart: 37 -> 37, of which waited for: 17 -> 16; matrix products, arithmetic and copies ran while one was open for 16% -> 16% of each run, Pallas kernels for 0% -> 0%
where the time goes in v4:
time: 208 us; the launch traced here: 206 us
  waiting for transfers between devices  82.6 us (40%)
  starting transfers between devices  75.3 us (36%)
  local copies, waits for them, and re-layouts  19.4 us (9%)
  other arithmetic  11.6 us (6%)
  matrix products  11 us (5%)
  between operations  5.52 us (3%)
    ppermute x32, waiting for transfers between devices, fetch(): return lax.ppermute(value, axis, [((i + step) % n, i) for i in range(n)])  54 us
    ppermute x32, starting transfers between devices, fetch(): return lax.ppermute(value, axis, [((i + step) % n, i) for i in range(n)])  42.6 us
    all_to_all x4, starting transfers between devices, from_everyone(): return lax.all_to_all(copies, axes, split_axis=0, concat_axis=0, tiled=True)  27.9 us
    all_to_all x4, waiting for transfers between devices, from_everyone(): return lax.all_to_all(copies, axes, split_axis=0, concat_axis=0, tiled=True)  17.7 us
    all_to_all x1, waiting for transfers between devices, body(): lax.all_to_all(pieces, (ZH, ZL), split_axis=0, concat_axis=0, tiled=True)  10.9 us
    dot_general x5, matrix products, rows_by(): lax.dot_general(left, right, (((0,), (0,)), ((), ())), preferred_element_...  7.1 us
    all_to_all x1, starting transfers between devices, body(): lax.all_to_all(pieces, (ZH, ZL), split_axis=0, concat_axis=0, tiled=True)  4.78 us
    unnamed x18, local copies, waits for them, and re-layouts  4.59 us
  transfers between devices with their start and end apart: 37, of which 16 were waited for; matrix products, arithmetic and copies ran while one was open for 16% of the time, Pallas kernels for 0%

profile of v4, /device:TPU:32, one launch (start us, length us, event | category | flops | bytes accessed | tf_op | source)
XLA Modules:
  0.0 205.5 jit_solution(14654227104911929887)
XLA Ops:
  3.3 10.3 %all-to-all-start = ((f32[16,8,128]{2,1,0:T(8,128)}), f32[16,8,128]{2,1,0:T(8,128)S(1)}, u32[]{:S(2)}, u32[]{:S(2)}) async-start(f32[16,8,128]{2,1,0:T(8,128)} %broadcast_in_dim.33), calls=%async_computation | async-start | bytes 131072 | tf_op jit(solution)/shard_map/all_to_all | solution.py:29
  13.6 3.1 %collective-permute-start.3 = (bf16[320,768]{1,0:T(8,128)(2,1)}, bf16[320,768]{1,0:T(8,128)(2,1)}, u32[]{:S(2)}, u32[]{:S(2)}) collective-permute-start(bf16[320,768]{1,0:T(8,128)(2,1)} %param.9), channel_id=1, source_target_pairs={{2,0},{4,2},{6,4},{0,6},{3,1},{5,3},{7,5},{1,7},{10,8},{12,10},{14... | collective-permute-start | bytes 1474568 | tf_op jit(solution)/shard_map/ppermute | solution.py:18
  17.7 5.5 %collective-permute-start.6 = (bf16[80,768]{1,0:T(8,128)(2,1)S(1)}, bf16[80,768]{1,0:T(8,128)(2,1)S(1)}, u32[]{:S(2)}, u32[]{:S(2)}) collective-permute-start(bf16[80,768]{1,0:T(8,128)(2,1)S(1)} %constant_dynamic-slice_fusion.6), channel_id=1, source_target_pairs={{8,0},{0,8},{9,1},{1,9},{10,2},{2,10},{11,3},{3,11},{12,4},{4,12},... | collective-permute-start | bytes 368648 | tf_op jit(solution)/shard_map/ppermute | solution.py:18
  23.1 3.0 %copy.24 = bf16[256,5120]{0,1:T(8,128)(2,1)S(1)} copy(bf16[256,5120]{1,0:T(8,128)(2,1)} %param.6) | data formatting | bytes 5242880 | tf_op args[0]
  33.3 3.9 %collective-permute-done.7 = bf16[80,768]{1,0:T(8,128)(2,1)S(1)} collective-permute-done((bf16[80,768]{1,0:T(8,128)(2,1)S(1)}, bf16[80,768]{1,0:T(8,128)(2,1)S(1)}, u32[]{:S(2)}, u32[]{:S(2)}) %collective-permute-start.7) | collective-permute-done | bytes 122912 | tf_op jit(solution)/shard_map/ppermute | solution.py:18
  41.4 2.8 %collective-permute-start.10 = (bf16[4,80,768]{2,1,0:T(8,128)(2,1)S(1)}, bf16[4,80,768]{2,1,0:T(8,128)(2,1)}, u32[]{:S(2)}, u32[]{:S(2)}) collective-permute-start(bf16[4,80,768]{2,1,0:T(8,128)(2,1)S(1)} %bitcast_dynamic-update-slice_fusion), channel_id=1, source_target_pairs={{16,0},{32,16},{48,32},{0,48},{17,1},{33,17},{49,33},{1,49},{18,2}... | collective-permute-start | bytes 1474568 | tf_op jit(solution)/shard_map/ppermute | solution.py:18
  44.3 3.2 %collective-permute-start.4 = (bf16[320,768]{1,0:T(8,128)(2,1)}, bf16[320,768]{1,0:T(8,128)(2,1)S(1)}, u32[]{:S(2)}, u32[]{:S(2)}) collective-permute-start(bf16[320,768]{1,0:T(8,128)(2,1)} %collective-permute-done.3), channel_id=1, source_target_pairs={{2,0},{4,2},{6,4},{0,6},{3,1},{5,3},{7,5},{1,7},{10,8},{12,10},{14... | collective-permute-start | bytes 1474568 | tf_op jit(solution)/shard_map/ppermute | solution.py:18
  47.5 7.4 %collective-permute-done.10 = bf16[4,80,768]{2,1,0:T(8,128)(2,1)} collective-permute-done((bf16[4,80,768]{2,1,0:T(8,128)(2,1)S(1)}, bf16[4,80,768]{2,1,0:T(8,128)(2,1)}, u32[]{:S(2)}, u32[]{:S(2)}) %collective-permute-start.10) | collective-permute-done | bytes 491552 | tf_op jit(solution)/shard_map/ppermute | solution.py:18
  54.9 3.8 %collective-permute-start.12 = (bf16[4,80,768]{2,1,0:T(8,128)(2,1)}, bf16[4,80,768]{2,1,0:T(8,128)(2,1)S(1)}, u32[]{:S(2)}, u32[]{:S(2)}) collective-permute-start(bf16[4,80,768]{2,1,0:T(8,128)(2,1)} %collective-permute-done.10), channel_id=1, source_target_pairs={{16,0},{32,16},{48,32},{0,48},{17,1},{33,17},{49,33},{1,49},{18,2}... | collective-permute-start | bytes 1474568 | tf_op jit(solution)/shard_map/ppermute | solution.py:18
  65.5 3.4 %collective-permute-done.12 = bf16[4,80,768]{2,1,0:T(8,128)(2,1)S(1)} collective-permute-done((bf16[4,80,768]{2,1,0:T(8,128)(2,1)}, bf16[4,80,768]{2,1,0:T(8,128)(2,1)S(1)}, u32[]{:S(2)}, u32[]{:S(2)}) %collective-permute-start.12) | collective-permute-done | bytes 491552 | tf_op jit(solution)/shard_map/ppermute | solution.py:18
  72.8 7.2 %all-to-all-start.1 = ((f32[16,8,128]{2,1,0:T(8,128)}), f32[16,8,128]{2,1,0:T(8,128)S(1)}, u32[]{:S(2)}, u32[]{:S(2)}) async-start(f32[16,8,128]{2,1,0:T(8,128)} %broadcast_in_dim_broadcast_in_dim.6), calls=%async_computation.1 | async-start | bytes 131072 | tf_op jit(solution)/shard_map/all_to_all | solution.py:29
  95.6 5.1 %collective-permute-done.14 = bf16[256,768]{1,0:T(8,128)(2,1)S(1)} collective-permute-done((bf16[256,768]{1,0:T(8,128)(2,1)S(1)}, bf16[256,768]{1,0:T(8,128)(2,1)S(1)}, u32[]{:S(2)}, u32[]{:S(2)}) %collective-permute-start.14) | collective-permute-done | bytes 393248 | tf_op jit(solution)/shard_map/ppermute | solution.py:18
  105.6 6.1 %collective-permute-done.23 = bf16[640,256]{1,0:T(8,128)(2,1)S(1)} collective-permute-done((bf16[640,256]{1,0:T(8,128)(2,1)S(1)}, bf16[640,256]{1,0:T(8,128)(2,1)S(1)}, u32[]{:S(2)}, u32[]{:S(2)}) %collective-permute-start.23) | collective-permute-done | bytes 327712 | tf_op jit(solution)/shard_map/ppermute | solution.py:18
  114.7 2.8 %collective-permute-done.17 = bf16[256,768]{1,0:T(8,128)(2,1)S(1)} collective-permute-done((bf16[256,768]{1,0:T(8,128)(2,1)S(1)}, bf16[256,768]{1,0:T(8,128)(2,1)S(1)}, u32[]{:S(2)}, u32[]{:S(2)}) %collective-permute-start.17) | collective-permute-done | bytes 393248 | tf_op jit(solution)/shard_map/ppermute | solution.py:18
  120.6 6.5 %collective-permute-done.27 = bf16[256,768]{1,0:T(8,128)(2,1)S(1)} collective-permute-done((bf16[256,768]{1,0:T(8,128)(2,1)S(1)}, bf16[256,768]{1,0:T(8,128)(2,1)S(1)}, u32[]{:S(2)}, u32[]{:S(2)}) %collective-permute-start.27) | collective-permute-done | bytes 393248 | tf_op jit(solution)/shard_map/ppermute | solution.py:18
  129.8 3.3 %all-to-all-start.2 = ((f32[8,8,128]{2,1,0:T(8,128)}), f32[8,8,128]{2,1,0:T(8,128)S(1)}, u32[]{:S(2)}, u32[]{:S(2)}) async-start(f32[8,8,128]{2,1,0:T(8,128)} %broadcast_in_dim_broadcast_in_dim.7), calls=%async_computation.2 | async-start | bytes 65536 | tf_op jit(solution)/shard_map/all_to_all | solution.py:29
  133.2 5.3 %all-to-all-done.2 = f32[8,8,128]{2,1,0:T(8,128)S(1)} async-done(((f32[8,8,128]{2,1,0:T(8,128)}), f32[8,8,128]{2,1,0:T(8,128)S(1)}, u32[]{:S(2)}, u32[]{:S(2)}) %all-to-all-start.2) | async-done | bytes 32800 | tf_op jit(solution)/shard_map/all_to_all | solution.py:29
  147.8 6.2 %collective-permute-done.19 = f32[80,768]{1,0:T(8,128)S(1)} collective-permute-done((f32[80,768]{1,0:T(8,128)S(1)}, f32[80,768]{1,0:T(8,128)S(1)}, u32[]{:S(2)}, u32[]{:S(2)}) %collective-permute-start.19) | collective-permute-done | bytes 245792 | tf_op jit(solution)/shard_map/ppermute | solution.py:18
  154.6 3.1 %collective-permute-done.21 = f32[80,768]{1,0:T(8,128)S(1)} collective-permute-done((f32[80,768]{1,0:T(8,128)S(1)}, f32[80,768]{1,0:T(8,128)S(1)}, u32[]{:S(2)}, u32[]{:S(2)}) %collective-permute-start.21) | collective-permute-done | bytes 245792 | tf_op jit(solution)/shard_map/ppermute | solution.py:18
  157.7 3.7 %collective-permute-done.31 = f32[80,768]{1,0:T(8,128)S(1)} collective-permute-done((f32[80,768]{1,0:T(8,128)S(1)}, f32[80,768]{1,0:T(8,128)S(1)}, u32[]{:S(2)}, u32[]{:S(2)}) %collective-permute-start.31) | collective-permute-done | bytes 245792 | tf_op jit(solution)/shard_map/ppermute | solution.py:18
  163.0 4.8 %all-to-all-start.3 = ((f32[8,128,128]{2,1,0:T(8,128)}), f32[8,128,128]{2,1,0:T(8,128)S(1)}, u32[]{:S(2)}, u32[]{:S(2)}) async-start(f32[8,128,128]{2,1,0:T(8,128)} %concatenate.70), calls=%async_computation.3 | async-start | bytes 1048576 | tf_op jit(solution)/shard_map/all_to_all | solution.py:122
  168.7 10.9 %all-to-all-done.3 = f32[8,128,128]{2,1,0:T(8,128)S(1)} async-done(((f32[8,128,128]{2,1,0:T(8,128)}), f32[8,128,128]{2,1,0:T(8,128)S(1)}, u32[]{:S(2)}, u32[]{:S(2)}) %all-to-all-start.3) | async-done | bytes 524320 | tf_op jit(solution)/shard_map/all_to_all | solution.py:122
  180.8 7.1 %all-to-all-start.4 = ((bf16[16,128,128]{2,1,0:T(8,128)(2,1)}), bf16[16,128,128]{2,1,0:T(8,128)(2,1)S(1)}, u32[]{:S(2)}, u32[]{:S(2)}) async-start(bf16[16,128,128]{2,1,0:T(8,128)(2,1)} %broadcast_in_dim.41), calls=%async_computation.4 | async-start | bytes 1048576 | tf_op jit(solution)/shard_map/all_to_all | solution.py:29
  188.6 12.4 %all-to-all-done.4 = bf16[16,128,128]{2,1,0:T(8,128)(2,1)S(1)} async-done(((bf16[16,128,128]{2,1,0:T(8,128)(2,1)}), bf16[16,128,128]{2,1,0:T(8,128)(2,1)S(1)}, u32[]{:S(2)}, u32[]{:S(2)}) %all-to-all-start.4) | async-done | bytes 524320 | tf_op jit(solution)/shard_map/all_to_all | solution.py:29
  (137 shorter events, 69.0 us)
Async XLA Ops:
  3.3 23.5 %all-to-all-start = ((f32[16,8,128]{2,1,0:T(8,128)}), f32[16,8,128]{2,1,0:T(8,128)S(1)}, u32[]{:S(2)}, u32[]{:S(2)}) async-start(f32[16,8,128]{2,1,0:T(8,128)} %broadcast_in_dim.33), calls=%async_computation | async-start | bytes 131072 | tf_op jit(solution)/shard_map/all_to_all | solution.py:29
  13.6 30.7 %collective-permute-start.3 = (bf16[320,768]{1,0:T(8,128)(2,1)}, bf16[320,768]{1,0:T(8,128)(2,1)}, u32[]{:S(2)}, u32[]{:S(2)}) collective-permute-start(bf16[320,768]{1,0:T(8,128)(2,1)} %param.9), channel_id=1, source_target_pairs={{2,0},{4,2},{6,4},{0,6},{3,1},{5,3},{7,5},{1,7},{10,8},{12,10},{14... | collective-permute-start | bytes 1474568 | tf_op jit(solution)/shard_map/ppermute | solution.py:18
  17.7 13.3 %collective-permute-start.6 = (bf16[80,768]{1,0:T(8,128)(2,1)S(1)}, bf16[80,768]{1,0:T(8,128)(2,1)S(1)}, u32[]{:S(2)}, u32[]{:S(2)}) collective-permute-start(bf16[80,768]{1,0:T(8,128)(2,1)S(1)} %constant_dynamic-slice_fusion.6), channel_id=1, source_target_pairs={{8,0},{0,8},{9,1},{1,9},{10,2},{2,10},{11,3},{3,11},{12,4},{4,12},... | collective-permute-start | bytes 368648 | tf_op jit(solution)/shard_map/ppermute | solution.py:18
  30.9 27.8 %collective-permute-start.2 = (bf16[2,4,4,80,256]{4,3,2,1,0:T(8,128)(2,1)}, bf16[2,4,4,80,256]{4,3,2,1,0:T(8,128)(2,1)S(1)}, u32[]{:S(2)}, u32[]{:S(2)}) collective-permute-start(bf16[2,4,4,80,256]{4,3,2,1,0:T(8,128)(2,1)} %get-tuple-element.23), channel_id=1, source_target_pairs={{1,0},{0,1},{3,2},{2,3},{5,4},{4,5},{7,6},{6,7},{9,8},{8,9},{11,10... | collective-permute-start | bytes 3932168 | tf_op jit(solution)/shard_map/ppermute | solution.py:18
  41.4 13.5 %collective-permute-start.10 = (bf16[4,80,768]{2,1,0:T(8,128)(2,1)S(1)}, bf16[4,80,768]{2,1,0:T(8,128)(2,1)}, u32[]{:S(2)}, u32[]{:S(2)}) collective-permute-start(bf16[4,80,768]{2,1,0:T(8,128)(2,1)S(1)} %bitcast_dynamic-update-slice_fusion), channel_id=1, source_target_pairs={{16,0},{32,16},{48,32},{0,48},{17,1},{33,17},{49,33},{1,49},{18,2}... | collective-permute-start | bytes 1474568 | tf_op jit(solution)/shard_map/ppermute | solution.py:18
  44.3 14.6 %collective-permute-start.11 = (bf16[4,80,768]{2,1,0:T(8,128)(2,1)S(1)}, bf16[4,80,768]{2,1,0:T(8,128)(2,1)}, u32[]{:S(2)}, u32[]{:S(2)}) collective-permute-start(bf16[4,80,768]{2,1,0:T(8,128)(2,1)S(1)} %bitcast_dynamic-update-slice_fusion), channel_id=1, source_target_pairs={{48,0},{0,16},{16,32},{32,48},{49,1},{1,17},{17,33},{33,49},{50,2}... | collective-permute-start | bytes 1474568 | tf_op jit(solution)/shard_map/ppermute | solution.py:18
  44.3 18.6 %collective-permute-start.5 = (bf16[320,768]{1,0:T(8,128)(2,1)}, bf16[320,768]{1,0:T(8,128)(2,1)}, u32[]{:S(2)}, u32[]{:S(2)}) collective-permute-start(bf16[320,768]{1,0:T(8,128)(2,1)} %param.9), channel_id=1, source_target_pairs={{6,0},{0,2},{2,4},{4,6},{7,1},{1,3},{3,5},{5,7},{14,8},{8,10},{10,... | collective-permute-start | bytes 1474568 | tf_op jit(solution)/shard_map/ppermute | solution.py:18
  44.3 18.6 %collective-permute-start.4 = (bf16[320,768]{1,0:T(8,128)(2,1)}, bf16[320,768]{1,0:T(8,128)(2,1)S(1)}, u32[]{:S(2)}, u32[]{:S(2)}) collective-permute-start(bf16[320,768]{1,0:T(8,128)(2,1)} %collective-permute-done.3), channel_id=1, source_target_pairs={{2,0},{4,2},{6,4},{0,6},{3,1},{5,3},{7,5},{1,7},{10,8},{12,10},{14... | collective-permute-start | bytes 1474568 | tf_op jit(solution)/shard_map/ppermute | solution.py:18
  54.9 13.9 %collective-permute-start.12 = (bf16[4,80,768]{2,1,0:T(8,128)(2,1)}, bf16[4,80,768]{2,1,0:T(8,128)(2,1)S(1)}, u32[]{:S(2)}, u32[]{:S(2)}) collective-permute-start(bf16[4,80,768]{2,1,0:T(8,128)(2,1)} %collective-permute-done.10), channel_id=1, source_target_pairs={{16,0},{32,16},{48,32},{0,48},{17,1},{33,17},{49,33},{1,49},{18,2}... | collective-permute-start | bytes 1474568 | tf_op jit(solution)/shard_map/ppermute | solution.py:18
  70.8 17.4 %collective-permute-start.13 = (f32[256,768]{1,0:T(8,128)S(1)}, f32[256,768]{1,0:T(8,128)}, u32[]{:S(2)}, u32[]{:S(2)}) collective-permute-start(f32[256,768]{1,0:T(8,128)S(1)} %slice.57), channel_id=1, source_target_pairs={{1,0},{0,1},{3,2},{2,3},{5,4},{4,5},{7,6},{6,7},{9,8},{8,9},{11,10... | collective-permute-start | bytes 2359304 | tf_op jit(solution)/shard_map/ppermute | solution.py:18
  72.8 14.1 %all-to-all-start.1 = ((f32[16,8,128]{2,1,0:T(8,128)}), f32[16,8,128]{2,1,0:T(8,128)S(1)}, u32[]{:S(2)}, u32[]{:S(2)}) async-start(f32[16,8,128]{2,1,0:T(8,128)} %broadcast_in_dim_broadcast_in_dim.6), calls=%async_computation.1 | async-start | bytes 131072 | tf_op jit(solution)/shard_map/all_to_all | solution.py:29
  81.1 12.7 %collective-permute-start.1 = (bf16[640,256]{1,0:T(8,128)(2,1)}, bf16[640,256]{1,0:T(8,128)(2,1)}, u32[]{:S(2)}, u32[]{:S(2)}) collective-permute-start(bf16[640,256]{1,0:T(8,128)(2,1)} %bitcast.8), channel_id=1, source_target_pairs={{6,0},{0,2},{2,4},{4,6},{7,1},{1,3},{3,5},{5,7},{14,8},{8,10},{10,... | collective-permute-start | bytes 983048 | tf_op jit(solution)/shard_map/ppermute | solution.py:18
  92.7 19.6 %collective-permute-start.24 = (bf16[256,768]{1,0:T(8,128)(2,1)S(1)}, bf16[256,768]{1,0:T(8,128)(2,1)S(1)}, u32[]{:S(2)}, u32[]{:S(2)}) collective-permute-start(bf16[256,768]{1,0:T(8,128)(2,1)S(1)} %get-tuple-element.6), channel_id=1, source_target_pairs={{16,0},{32,16},{48,32},{0,48},{17,1},{33,17},{49,33},{1,49},{18,2}... | collective-permute-start | bytes 1179656 | tf_op jit(solution)/shard_map/ppermute | solution.py:18
  93.8 18.4 %collective-permute-start.25 = (bf16[256,768]{1,0:T(8,128)(2,1)S(1)}, bf16[256,768]{1,0:T(8,128)(2,1)S(1)}, u32[]{:S(2)}, u32[]{:S(2)}) collective-permute-start(bf16[256,768]{1,0:T(8,128)(2,1)S(1)} %get-tuple-element.6), channel_id=1, source_target_pairs={{48,0},{0,16},{16,32},{32,48},{49,1},{1,17},{17,33},{33,49},{50,2}... | collective-permute-start | bytes 1179656 | tf_op jit(solution)/shard_map/ppermute | solution.py:18
  94.7 17.0 %collective-permute-start.23 = (bf16[640,256]{1,0:T(8,128)(2,1)S(1)}, bf16[640,256]{1,0:T(8,128)(2,1)S(1)}, u32[]{:S(2)}, u32[]{:S(2)}) collective-permute-start(bf16[640,256]{1,0:T(8,128)(2,1)S(1)} %bitcast.130), channel_id=1, source_target_pairs={{48,0},{0,16},{16,32},{32,48},{49,1},{1,17},{17,33},{33,49},{50,2}... | collective-permute-start | bytes 983048 | tf_op jit(solution)/shard_map/ppermute | solution.py:18
  100.7 16.8 %collective-permute-start.17 = (bf16[256,768]{1,0:T(8,128)(2,1)S(1)}, bf16[256,768]{1,0:T(8,128)(2,1)S(1)}, u32[]{:S(2)}, u32[]{:S(2)}) collective-permute-start(bf16[256,768]{1,0:T(8,128)(2,1)S(1)} %collective-permute-done.14), channel_id=1, source_target_pairs={{2,0},{4,2},{6,4},{0,6},{3,1},{5,3},{7,5},{1,7},{10,8},{12,10},{14... | collective-permute-start | bytes 1179656 | tf_op jit(solution)/shard_map/ppermute | solution.py:18
  113.2 13.9 %collective-permute-start.27 = (bf16[256,768]{1,0:T(8,128)(2,1)S(1)}, bf16[256,768]{1,0:T(8,128)(2,1)S(1)}, u32[]{:S(2)}, u32[]{:S(2)}) collective-permute-start(bf16[256,768]{1,0:T(8,128)(2,1)S(1)} %collective-permute-done.24), channel_id=1, source_target_pairs={{16,0},{32,16},{48,32},{0,48},{17,1},{33,17},{49,33},{1,49},{18,2}... | collective-permute-start | bytes 1179656 | tf_op jit(solution)/shard_map/ppermute | solution.py:18
  119.1 20.0 %collective-permute-start.18 = (f32[4,80,768]{2,1,0:T(8,128)}, f32[4,80,768]{2,1,0:T(8,128)}, u32[]{:S(2)}, u32[]{:S(2)}) collective-permute-start(f32[4,80,768]{2,1,0:T(8,128)} %dynamic-slice_bitcast_fusion.3), channel_id=1, source_target_pairs={{1,0},{0,1},{3,2},{2,3},{5,4},{4,5},{7,6},{6,7},{9,8},{8,9},{11,10... | collective-permute-start | bytes 2949128 | tf_op jit(solution)/shard_map/ppermute | solution.py:18
  128.6 16.3 %collective-permute-start.28 = (f32[4,80,768]{2,1,0:T(8,128)}, f32[4,80,768]{2,1,0:T(8,128)S(1)}, u32[]{:S(2)}, u32[]{:S(2)}) collective-permute-start(f32[4,80,768]{2,1,0:T(8,128)} %dynamic-slice_bitcast_fusion.2), channel_id=1, source_target_pairs={{1,0},{0,1},{3,2},{2,3},{5,4},{4,5},{7,6},{6,7},{9,8},{8,9},{11,10... | collective-permute-start | bytes 2949128 | tf_op jit(solution)/shard_map/ppermute | solution.py:18
  140.8 13.2 %collective-permute-start.19 = (f32[80,768]{1,0:T(8,128)S(1)}, f32[80,768]{1,0:T(8,128)S(1)}, u32[]{:S(2)}, u32[]{:S(2)}) collective-permute-start(f32[80,768]{1,0:T(8,128)S(1)} %get-tuple-element.27), channel_id=1, source_target_pairs={{16,0},{32,16},{48,32},{0,48},{17,1},{33,17},{49,33},{1,49},{18,2}... | collective-permute-start | bytes 737288 | tf_op jit(solution)/shard_map/ppermute | solution.py:18
  144.9 12.8 %collective-permute-start.21 = (f32[80,768]{1,0:T(8,128)S(1)}, f32[80,768]{1,0:T(8,128)S(1)}, u32[]{:S(2)}, u32[]{:S(2)}) collective-permute-start(f32[80,768]{1,0:T(8,128)S(1)} %get-tuple-element.26), channel_id=1, source_target_pairs={{48,0},{0,16},{16,32},{32,48},{49,1},{1,17},{17,33},{33,49},{50,2}... | collective-permute-start | bytes 737288 | tf_op jit(solution)/shard_map/ppermute | solution.py:18
  145.1 12.6 %collective-permute-start.29 = (f32[80,768]{1,0:T(8,128)S(1)}, f32[80,768]{1,0:T(8,128)S(1)}, u32[]{:S(2)}, u32[]{:S(2)}) collective-permute-start(f32[80,768]{1,0:T(8,128)S(1)} %get-tuple-element.30), channel_id=1, source_target_pairs={{2,0},{4,2},{6,4},{0,6},{3,1},{5,3},{7,5},{1,7},{10,8},{12,10},{14... | collective-permute-start | bytes 737288 | tf_op jit(solution)/shard_map/ppermute | solution.py:18
  163.0 16.6 %all-to-all-start.3 = ((f32[8,128,128]{2,1,0:T(8,128)}), f32[8,128,128]{2,1,0:T(8,128)S(1)}, u32[]{:S(2)}, u32[]{:S(2)}) async-start(f32[8,128,128]{2,1,0:T(8,128)} %concatenate.70), calls=%async_computation.3 | async-start | bytes 1048576 | tf_op jit(solution)/shard_map/all_to_all | solution.py:122
  180.8 20.1 %all-to-all-start.4 = ((bf16[16,128,128]{2,1,0:T(8,128)(2,1)}), bf16[16,128,128]{2,1,0:T(8,128)(2,1)S(1)}, u32[]{:S(2)}, u32[]{:S(2)}) async-start(bf16[16,128,128]{2,1,0:T(8,128)(2,1)} %broadcast_in_dim.41), calls=%async_computation.4 | async-start | bytes 1048576 | tf_op jit(solution)/shard_map/all_to_all | solution.py:29
  (21 other events, 178.7 us)

commit v5 on v4

--- a/solution.py
+++ b/solution.py
@@ -80,7 +80,8 @@
     far_cols = [block(turned, 1 - zh, None, None, (x + s) & 3).reshape(2 * own, rows) for s in range(4)]
 
     halves = rows_by(jnp.concatenate(near_half), jnp.concatenate(near)) + rows_by(far_half[0], far[0])
-    halves += sum(rows_by(far_half[i], far[i]) for i in (1, 3, 2))
+    halves += rows_by(jnp.concatenate([far_half[1], far_half[3]]), jnp.concatenate([far[1], far[3]]))
+    halves += rows_by(far_half[2], far[2])
     keys = halves[:rows] + fetch(halves[rows:], C, 1)
 
     position = lax.broadcasted_iota(jnp.int32, (rows, 1), 0)
@@ -94,19 +95,28 @@
     near_up = ring_blocks(upstream, Y)
     far_up = ring_blocks(upstream, X)
 
-    def pooled(left, up):
+    def pooled(left, up, halve):
         first = jnp.dot(
             jnp.concatenate([left[i] for i in (0, 1, 3)], axis=1),
             jnp.concatenate([up[i] for i in (0, 1, 3)]),
             preferred_element_type=jnp.float32,
         )
         first = lax.optimization_barrier(first)
-        return first + jnp.dot(left[2], up[2], preferred_element_type=jnp.float32)
+        return [
+            halve(first, side) + jnp.dot(halve(left[2], side), up[2], preferred_element_type=jnp.float32)
+            for side in (1 - core, core)
+        ]
 
-    near_out = pooled(near_in, near_up).reshape(2, 4, part, features)
-    near_out = block(near_out, core) + fetch(block(near_out, 1 - core), C, 1)
-    far_out = pooled(far_in, far_up).reshape(4, 2, part, features)
-    far_out = block(far_out, None, core) + fetch(block(far_out, None, 1 - core), C, 1)
+    def near_rows(value, side):
+        return block(value.reshape(2, own, -1), side)
+
+    def far_rows(value, side):
+        return block(value.reshape(4, 2, part, -1), None, side).reshape(own, -1)
+
+    near_other, near_mine = pooled(near_in, near_up, near_rows)
+    far_other, far_mine = pooled(far_in, far_up, far_rows)
+    near_out = (near_mine + fetch(near_other, C, 1)).reshape(4, part, features)
+    far_out = (far_mine + fetch(far_other, C, 1)).reshape(4, part, features)
     near_sum = block(near_out, x) + sum(fetch(block(near_out, (x - s) & 3), X, s) for s in (1, 2, 3))
     far_sum = block(far_out, y) + sum(fetch(block(far_out, (y - s) & 3), Y, s) for s in (1, 2, 3))
     both = jnp.where(zh == 0, jnp.stack([near_sum, far_sum]), jnp.stack([far_sum, near_sum]))
@@ -116,15 +126,13 @@
     def tiled(value):
         return value.reshape(-1, 2, tall, 8, 2, wide, 128).transpose(0, 1, 4, 2, 5, 3, 6)
 
-    near_loss = summed(own_sum, (Y, C))
     pieces = tiled(both).reshape(8, -1, 128)
-    pieces = jnp.concatenate([pieces, jnp.broadcast_to(near_loss, (8, 8, 128))], axis=1)
-    pieces = lax.all_to_all(pieces, (ZH, ZL), split_axis=0, concat_axis=0, tiled=True).sum(axis=0)
+    piece = lax.all_to_all(pieces, (ZH, ZL), split_axis=0, concat_axis=0, tiled=True).sum(axis=0)
+    group_sum = summed(own_sum, SHARD)
 
-    piece = pieces[:-8]
     mine = tiled(block(w_key.reshape(4, part, features), x)).reshape(4, -1, 128)
     share = (piece * block(mine, lax.axis_index(ZL)).astype(jnp.float32)).sum(axis=1)
-    share = jnp.concatenate([share, pieces[-1, :8]])
+    share = jnp.concatenate([share, jnp.broadcast_to(group_sum, (8,))])
     lines = []
     for _ in range(3):
         lines.append(lax.reduce_precision(share, 8, 7))
@@ -132,7 +140,7 @@
     lines = jnp.pad(jnp.stack(lines), ((0, 5), (0, 0)))
     whole = from_everyone(jnp.concatenate([piece, lines]).astype(jnp.bfloat16), DP)
     shares = whole[:, -8:-5].astype(jnp.float32).sum(axis=1)
-    loss = shares[:4, -1].sum() / (2.0 * features * total_count)
+    loss = shares[:, -1].sum() / (2.0 * features * total_count)
     shares = shares[:, :-8].reshape(2, 2, 4, tall, wide, 8)
     grad_gain = shares.sum(axis=(1, 4)).swapaxes(0, 1).reshape(own) / norm_gain.astype(jnp.float32)
     whole = whole[:, :-8].reshape(2, 2, 4, tall, wide, 8, 128)

time: 208 us -> 211 us (1.014)
  starting transfers between devices: 75.3 us -> 79 us
  matrix products: 11 us -> 14.4 us
  local copies, waits for them, and re-layouts: 19.4 us -> 16.8 us
    dot_general x2 -> x4, matrix products: 0.83 us -> 5.64 us  [pooled(): jnp.dot(halve(left[2], side), up[2], preferred_element_type=jnp.float32)]
    all_to_all x4, waiting for transfers between devices: 17.7 us -> 14.3 us  [from_everyone(): return lax.all_to_all(copies, axes, split_axis=0, concat_axis=0, tiled=True)]
    all_to_all x1, starting transfers between devices: 4.78 us -> 7.35 us  [body(): lax.all_to_all(pieces, (ZH, ZL), split_axis=0, concat_axis=0, tiled=True)]
    all_to_all x1, waiting for transfers between devices: 10.9 us -> 13.1 us  [body(): lax.all_to_all(pieces, (ZH, ZL), split_axis=0, concat_axis=0, tiled=True)]
    reshape x5 -> x3, local copies, waits for them, and re-layouts: 3.7 us -> 1.53 us  [block(): return lax.dynamic_slice(value, starts, sizes).reshape(kept)]
    dot_general x5 -> x4, matrix products: 7.1 us -> 5.8 us  [rows_by(): lax.dot_general(left, right, (((0,), (0,)), ((), ())), preferred_element_...]
    unnamed x18 -> x30, local copies, waits for them, and re-layouts: 4.59 us -> 4.61 us
  transfers between devices with their start and end apart: 37 -> 37, of which waited for: 16 -> 16; matrix products, arithmetic and copies ran while one was open for 16% -> 17% of each run, Pallas kernels for 0% -> 0%
where the time goes in v5:
time: 211 us; the launch traced here: 210 us
  waiting for transfers between devices  82.1 us (39%)
  starting transfers between devices  79 us (37%)
  local copies, waits for them, and re-layouts  16.8 us (8%)
  matrix products  14.4 us (7%)
  other arithmetic  12.2 us (6%)
  between operations  5.51 us (3%)
    ppermute x32, waiting for transfers between devices, fetch(): return lax.ppermute(value, axis, [((i + step) % n, i) for i in range(n)])  54.7 us
    ppermute x32, starting transfers between devices, fetch(): return lax.ppermute(value, axis, [((i + step) % n, i) for i in range(n)])  43.9 us
    all_to_all x4, starting transfers between devices, from_everyone(): return lax.all_to_all(copies, axes, split_axis=0, concat_axis=0, tiled=True)  27.7 us
    all_to_all x4, waiting for transfers between devices, from_everyone(): return lax.all_to_all(copies, axes, split_axis=0, concat_axis=0, tiled=True)  14.3 us
    all_to_all x1, waiting for transfers between devices, body(): lax.all_to_all(pieces, (ZH, ZL), split_axis=0, concat_axis=0, tiled=True)  13.1 us
    all_to_all x1, starting transfers between devices, body(): lax.all_to_all(pieces, (ZH, ZL), split_axis=0, concat_axis=0, tiled=True)  7.35 us
    dot_general x4, matrix products, rows_by(): lax.dot_general(left, right, (((0,), (0,)), ((), ())), preferred_element_...  5.8 us
    dot_general x4, matrix products, pooled(): jnp.dot(halve(left[2], side), up[2], preferred_element_type=jnp.float32)  5.64 us
  transfers between devices with their start and end apart: 37, of which 16 were waited for; matrix products, arithmetic and copies ran while one was open for 17% of the time, Pallas kernels for 0%

profile of v5, /device:TPU:32, one launch (start us, length us, event | category | flops | bytes accessed | tf_op | source)
XLA Modules:
  0.0 209.9 jit_solution(11745250046964714818)
XLA Ops:
  3.3 10.3 %all-to-all-start = ((f32[16,8,128]{2,1,0:T(8,128)}), f32[16,8,128]{2,1,0:T(8,128)S(1)}, u32[]{:S(2)}, u32[]{:S(2)}) async-start(f32[16,8,128]{2,1,0:T(8,128)} %broadcast_in_dim.33), calls=%async_computation | async-start | bytes 131072 | tf_op jit(solution)/shard_map/all_to_all | solution.py:29
  13.6 3.1 %collective-permute-start.3 = (bf16[320,768]{1,0:T(8,128)(2,1)}, bf16[320,768]{1,0:T(8,128)(2,1)}, u32[]{:S(2)}, u32[]{:S(2)}) collective-permute-start(bf16[320,768]{1,0:T(8,128)(2,1)} %param.9), channel_id=1, source_target_pairs={{2,0},{4,2},{6,4},{0,6},{3,1},{5,3},{7,5},{1,7},{10,8},{12,10},{14... | collective-permute-start | bytes 1474568 | tf_op jit(solution)/shard_map/ppermute | solution.py:18
  17.7 5.5 %collective-permute-start.6 = (bf16[80,768]{1,0:T(8,128)(2,1)S(1)}, bf16[80,768]{1,0:T(8,128)(2,1)S(1)}, u32[]{:S(2)}, u32[]{:S(2)}) collective-permute-start(bf16[80,768]{1,0:T(8,128)(2,1)S(1)} %constant_dynamic-slice_fusion.10), channel_id=1, source_target_pairs={{8,0},{0,8},{9,1},{1,9},{10,2},{2,10},{11,3},{3,11},{12,4},{4,12},... | collective-permute-start | bytes 368648 | tf_op jit(solution)/shard_map/ppermute | solution.py:18
  23.1 3.0 %copy.24 = bf16[256,5120]{0,1:T(8,128)(2,1)S(1)} copy(bf16[256,5120]{1,0:T(8,128)(2,1)} %param.6) | data formatting | bytes 5242880 | tf_op args[0]
  33.3 3.9 %collective-permute-done.7 = bf16[80,768]{1,0:T(8,128)(2,1)S(1)} collective-permute-done((bf16[80,768]{1,0:T(8,128)(2,1)S(1)}, bf16[80,768]{1,0:T(8,128)(2,1)S(1)}, u32[]{:S(2)}, u32[]{:S(2)}) %collective-permute-start.7) | collective-permute-done | bytes 122912 | tf_op jit(solution)/shard_map/ppermute | solution.py:18
  41.4 2.8 %collective-permute-start.10 = (bf16[4,80,768]{2,1,0:T(8,128)(2,1)S(1)}, bf16[4,80,768]{2,1,0:T(8,128)(2,1)}, u32[]{:S(2)}, u32[]{:S(2)}) collective-permute-start(bf16[4,80,768]{2,1,0:T(8,128)(2,1)S(1)} %bitcast_dynamic-update-slice_fusion), channel_id=1, source_target_pairs={{16,0},{32,16},{48,32},{0,48},{17,1},{33,17},{49,33},{1,49},{18,2}... | collective-permute-start | bytes 1474568 | tf_op jit(solution)/shard_map/ppermute | solution.py:18
  44.3 3.2 %collective-permute-start.4 = (bf16[320,768]{1,0:T(8,128)(2,1)}, bf16[320,768]{1,0:T(8,128)(2,1)S(1)}, u32[]{:S(2)}, u32[]{:S(2)}) collective-permute-start(bf16[320,768]{1,0:T(8,128)(2,1)} %collective-permute-done.3), channel_id=1, source_target_pairs={{2,0},{4,2},{6,4},{0,6},{3,1},{5,3},{7,5},{1,7},{10,8},{12,10},{14... | collective-permute-start | bytes 1474568 | tf_op jit(solution)/shard_map/ppermute | solution.py:18
  47.5 7.4 %collective-permute-done.10 = bf16[4,80,768]{2,1,0:T(8,128)(2,1)} collective-permute-done((bf16[4,80,768]{2,1,0:T(8,128)(2,1)S(1)}, bf16[4,80,768]{2,1,0:T(8,128)(2,1)}, u32[]{:S(2)}, u32[]{:S(2)}) %collective-permute-start.10) | collective-permute-done | bytes 491552 | tf_op jit(solution)/shard_map/ppermute | solution.py:18
  54.9 3.8 %collective-permute-start.12 = (bf16[4,80,768]{2,1,0:T(8,128)(2,1)}, bf16[4,80,768]{2,1,0:T(8,128)(2,1)S(1)}, u32[]{:S(2)}, u32[]{:S(2)}) collective-permute-start(bf16[4,80,768]{2,1,0:T(8,128)(2,1)} %collective-permute-done.10), channel_id=1, source_target_pairs={{16,0},{32,16},{48,32},{0,48},{17,1},{33,17},{49,33},{1,49},{18,2}... | collective-permute-start | bytes 1474568 | tf_op jit(solution)/shard_map/ppermute | solution.py:18
  64.2 4.7 %collective-permute-done.12 = bf16[4,80,768]{2,1,0:T(8,128)(2,1)S(1)} collective-permute-done((bf16[4,80,768]{2,1,0:T(8,128)(2,1)}, bf16[4,80,768]{2,1,0:T(8,128)(2,1)S(1)}, u32[]{:S(2)}, u32[]{:S(2)}) %collective-permute-start.12) | collective-permute-done | bytes 491552 | tf_op jit(solution)/shard_map/ppermute | solution.py:18
  72.7 7.2 %all-to-all-start.1 = ((f32[16,8,128]{2,1,0:T(8,128)}), f32[16,8,128]{2,1,0:T(8,128)}, u32[]{:S(2)}, u32[]{:S(2)}) async-start(f32[16,8,128]{2,1,0:T(8,128)} %broadcast_in_dim_broadcast_in_dim.6), calls=%async_computation.1 | async-start | bytes 131072 | tf_op jit(solution)/shard_map/all_to_all | solution.py:29
  84.2 2.8 %collective-permute-start.22 = (bf16[640,256]{1,0:T(8,128)(2,1)}, bf16[640,256]{1,0:T(8,128)(2,1)S(1)}, u32[]{:S(2)}, u32[]{:S(2)}) collective-permute-start(bf16[640,256]{1,0:T(8,128)(2,1)} %bitcast.41), channel_id=1, source_target_pairs={{16,0},{32,16},{48,32},{0,48},{17,1},{33,17},{49,33},{1,49},{18,2}... | collective-permute-start | bytes 983048 | tf_op jit(solution)/shard_map/ppermute | solution.py:18
  96.5 3.4 %collective-permute-done.22 = bf16[640,256]{1,0:T(8,128)(2,1)S(1)} collective-permute-done((bf16[640,256]{1,0:T(8,128)(2,1)}, bf16[640,256]{1,0:T(8,128)(2,1)S(1)}, u32[]{:S(2)}, u32[]{:S(2)}) %collective-permute-start.22) | collective-permute-done | bytes 327712 | tf_op jit(solution)/shard_map/ppermute | solution.py:18
  99.9 5.0 %collective-permute-done.26 = bf16[640,256]{1,0:T(8,128)(2,1)S(1)} collective-permute-done((bf16[640,256]{1,0:T(8,128)(2,1)S(1)}, bf16[640,256]{1,0:T(8,128)(2,1)S(1)}, u32[]{:S(2)}, u32[]{:S(2)}) %collective-permute-start.26) | collective-permute-done | bytes 327712 | tf_op jit(solution)/shard_map/ppermute | solution.py:18
  110.5 8.0 %collective-permute-done.23 = bf16[640,256]{1,0:T(8,128)(2,1)S(1)} collective-permute-done((bf16[640,256]{1,0:T(8,128)(2,1)S(1)}, bf16[640,256]{1,0:T(8,128)(2,1)S(1)}, u32[]{:S(2)}, u32[]{:S(2)}) %collective-permute-start.23) | collective-permute-done | bytes 327712 | tf_op jit(solution)/shard_map/ppermute | solution.py:18
  121.5 6.5 %collective-permute-done.27 = bf16[256,768]{1,0:T(8,128)(2,1)S(1)} collective-permute-done((bf16[256,768]{1,0:T(8,128)(2,1)S(1)}, bf16[256,768]{1,0:T(8,128)(2,1)S(1)}, u32[]{:S(2)}, u32[]{:S(2)}) %collective-permute-start.27) | collective-permute-done | bytes 393248 | tf_op jit(solution)/shard_map/ppermute | solution.py:18
  130.6 4.9 %all-to-all-start.3 = ((f32[16,8,128]{2,1,0:T(8,128)}), f32[16,8,128]{2,1,0:T(8,128)}, u32[]{:S(2)}, u32[]{:S(2)}) async-start(f32[16,8,128]{2,1,0:T(8,128)} %broadcast_in_dim_broadcast_in_dim.7), calls=%async_computation.3 | async-start | bytes 131072 | tf_op jit(solution)/shard_map/all_to_all | solution.py:29
  142.9 3.1 %collective-permute-start.29 = (f32[80,768]{1,0:T(8,128)S(1)}, f32[80,768]{1,0:T(8,128)S(1)}, u32[]{:S(2)}, u32[]{:S(2)}) collective-permute-start(f32[80,768]{1,0:T(8,128)S(1)} %get-tuple-element.30), channel_id=1, source_target_pairs={{2,0},{4,2},{6,4},{0,6},{3,1},{5,3},{7,5},{1,7},{10,8},{12,10},{14... | collective-permute-start | bytes 737288 | tf_op jit(solution)/shard_map/ppermute | solution.py:18
  149.1 4.3 %collective-permute-done.21 = f32[80,768]{1,0:T(8,128)S(1)} collective-permute-done((f32[80,768]{1,0:T(8,128)S(1)}, f32[80,768]{1,0:T(8,128)S(1)}, u32[]{:S(2)}, u32[]{:S(2)}) %collective-permute-start.21) | collective-permute-done | bytes 245792 | tf_op jit(solution)/shard_map/ppermute | solution.py:18
  156.3 3.3 %collective-permute-done.31 = f32[80,768]{1,0:T(8,128)S(1)} collective-permute-done((f32[80,768]{1,0:T(8,128)S(1)}, f32[80,768]{1,0:T(8,128)S(1)}, u32[]{:S(2)}, u32[]{:S(2)}) %collective-permute-start.31) | collective-permute-done | bytes 245792 | tf_op jit(solution)/shard_map/ppermute | solution.py:18
  160.5 7.4 %all-to-all-start.2 = ((f32[8,120,128]{2,1,0:T(8,128)}), f32[8,120,128]{2,1,0:T(8,128)S(1)}, u32[]{:S(2)}, u32[]{:S(2)}) async-start(f32[8,120,128]{2,1,0:T(8,128)} %bitcast.57), calls=%async_computation.2 | async-start | bytes 983040 | tf_op jit(solution)/shard_map/all_to_all | solution.py:130
  170.2 13.1 %all-to-all-done.2 = f32[8,120,128]{2,1,0:T(8,128)S(1)} async-done(((f32[8,120,128]{2,1,0:T(8,128)}), f32[8,120,128]{2,1,0:T(8,128)S(1)}, u32[]{:S(2)}, u32[]{:S(2)}) %all-to-all-start.2) | async-done | bytes 491552 | tf_op jit(solution)/shard_map/all_to_all | solution.py:130
  185.1 5.3 %all-to-all-start.4 = ((bf16[16,128,128]{2,1,0:T(8,128)(2,1)}), bf16[16,128,128]{2,1,0:T(8,128)(2,1)S(1)}, u32[]{:S(2)}, u32[]{:S(2)}) async-start(bf16[16,128,128]{2,1,0:T(8,128)(2,1)} %broadcast_in_dim.41), calls=%async_computation.4 | async-start | bytes 1048576 | tf_op jit(solution)/shard_map/all_to_all | solution.py:29
  191.1 14.3 %all-to-all-done.4 = bf16[16,128,128]{2,1,0:T(8,128)(2,1)S(1)} async-done(((bf16[16,128,128]{2,1,0:T(8,128)(2,1)}), bf16[16,128,128]{2,1,0:T(8,128)(2,1)S(1)}, u32[]{:S(2)}, u32[]{:S(2)}) %all-to-all-start.4) | async-done | bytes 524320 | tf_op jit(solution)/shard_map/all_to_all | solution.py:29
  (144 shorter events, 68.2 us)
Async XLA Ops:
  3.3 23.5 %all-to-all-start = ((f32[16,8,128]{2,1,0:T(8,128)}), f32[16,8,128]{2,1,0:T(8,128)S(1)}, u32[]{:S(2)}, u32[]{:S(2)}) async-start(f32[16,8,128]{2,1,0:T(8,128)} %broadcast_in_dim.33), calls=%async_computation | async-start | bytes 131072 | tf_op jit(solution)/shard_map/all_to_all | solution.py:29
  13.6 30.7 %collective-permute-start.3 = (bf16[320,768]{1,0:T(8,128)(2,1)}, bf16[320,768]{1,0:T(8,128)(2,1)}, u32[]{:S(2)}, u32[]{:S(2)}) collective-permute-start(bf16[320,768]{1,0:T(8,128)(2,1)} %param.9), channel_id=1, source_target_pairs={{2,0},{4,2},{6,4},{0,6},{3,1},{5,3},{7,5},{1,7},{10,8},{12,10},{14... | collective-permute-start | bytes 1474568 | tf_op jit(solution)/shard_map/ppermute | solution.py:18
  17.7 13.3 %collective-permute-start.6 = (bf16[80,768]{1,0:T(8,128)(2,1)S(1)}, bf16[80,768]{1,0:T(8,128)(2,1)S(1)}, u32[]{:S(2)}, u32[]{:S(2)}) collective-permute-start(bf16[80,768]{1,0:T(8,128)(2,1)S(1)} %constant_dynamic-slice_fusion.10), channel_id=1, source_target_pairs={{8,0},{0,8},{9,1},{1,9},{10,2},{2,10},{11,3},{3,11},{12,4},{4,12},... | collective-permute-start | bytes 368648 | tf_op jit(solution)/shard_map/ppermute | solution.py:18
  30.9 27.8 %collective-permute-start.2 = (bf16[2,4,4,80,256]{4,3,2,1,0:T(8,128)(2,1)}, bf16[2,4,4,80,256]{4,3,2,1,0:T(8,128)(2,1)S(1)}, u32[]{:S(2)}, u32[]{:S(2)}) collective-permute-start(bf16[2,4,4,80,256]{4,3,2,1,0:T(8,128)(2,1)} %get-tuple-element.21), channel_id=1, source_target_pairs={{1,0},{0,1},{3,2},{2,3},{5,4},{4,5},{7,6},{6,7},{9,8},{8,9},{11,10... | collective-permute-start | bytes 3932168 | tf_op jit(solution)/shard_map/ppermute | solution.py:18
  41.4 13.5 %collective-permute-start.10 = (bf16[4,80,768]{2,1,0:T(8,128)(2,1)S(1)}, bf16[4,80,768]{2,1,0:T(8,128)(2,1)}, u32[]{:S(2)}, u32[]{:S(2)}) collective-permute-start(bf16[4,80,768]{2,1,0:T(8,128)(2,1)S(1)} %bitcast_dynamic-update-slice_fusion), channel_id=1, source_target_pairs={{16,0},{32,16},{48,32},{0,48},{17,1},{33,17},{49,33},{1,49},{18,2}... | collective-permute-start | bytes 1474568 | tf_op jit(solution)/shard_map/ppermute | solution.py:18
  44.3 14.6 %collective-permute-start.11 = (bf16[4,80,768]{2,1,0:T(8,128)(2,1)S(1)}, bf16[4,80,768]{2,1,0:T(8,128)(2,1)}, u32[]{:S(2)}, u32[]{:S(2)}) collective-permute-start(bf16[4,80,768]{2,1,0:T(8,128)(2,1)S(1)} %bitcast_dynamic-update-slice_fusion), channel_id=1, source_target_pairs={{48,0},{0,16},{16,32},{32,48},{49,1},{1,17},{17,33},{33,49},{50,2}... | collective-permute-start | bytes 1474568 | tf_op jit(solution)/shard_map/ppermute | solution.py:18
  44.3 17.4 %collective-permute-start.5 = (bf16[320,768]{1,0:T(8,128)(2,1)}, bf16[320,768]{1,0:T(8,128)(2,1)}, u32[]{:S(2)}, u32[]{:S(2)}) collective-permute-start(bf16[320,768]{1,0:T(8,128)(2,1)} %param.9), channel_id=1, source_target_pairs={{6,0},{0,2},{2,4},{4,6},{7,1},{1,3},{3,5},{5,7},{14,8},{8,10},{10,... | collective-permute-start | bytes 1474568 | tf_op jit(solution)/shard_map/ppermute | solution.py:18
  44.3 17.4 %collective-permute-start.4 = (bf16[320,768]{1,0:T(8,128)(2,1)}, bf16[320,768]{1,0:T(8,128)(2,1)S(1)}, u32[]{:S(2)}, u32[]{:S(2)}) collective-permute-start(bf16[320,768]{1,0:T(8,128)(2,1)} %collective-permute-done.3), channel_id=1, source_target_pairs={{2,0},{4,2},{6,4},{0,6},{3,1},{5,3},{7,5},{1,7},{10,8},{12,10},{14... | collective-permute-start | bytes 1474568 | tf_op jit(solution)/shard_map/ppermute | solution.py:18
  54.9 13.9 %collective-permute-start.12 = (bf16[4,80,768]{2,1,0:T(8,128)(2,1)}, bf16[4,80,768]{2,1,0:T(8,128)(2,1)S(1)}, u32[]{:S(2)}, u32[]{:S(2)}) collective-permute-start(bf16[4,80,768]{2,1,0:T(8,128)(2,1)} %collective-permute-done.10), channel_id=1, source_target_pairs={{16,0},{32,16},{48,32},{0,48},{17,1},{33,17},{49,33},{1,49},{18,2}... | collective-permute-start | bytes 1474568 | tf_op jit(solution)/shard_map/ppermute | solution.py:18
  70.8 18.4 %collective-permute-start.13 = (f32[256,768]{1,0:T(8,128)S(1)}, f32[256,768]{1,0:T(8,128)}, u32[]{:S(2)}, u32[]{:S(2)}) collective-permute-start(f32[256,768]{1,0:T(8,128)S(1)} %slice.49), channel_id=1, source_target_pairs={{1,0},{0,1},{3,2},{2,3},{5,4},{4,5},{7,6},{6,7},{9,8},{8,9},{11,10... | collective-permute-start | bytes 2359304 | tf_op jit(solution)/shard_map/ppermute | solution.py:18
  72.7 14.2 %all-to-all-start.1 = ((f32[16,8,128]{2,1,0:T(8,128)}), f32[16,8,128]{2,1,0:T(8,128)}, u32[]{:S(2)}, u32[]{:S(2)}) async-start(f32[16,8,128]{2,1,0:T(8,128)} %broadcast_in_dim_broadcast_in_dim.6), calls=%async_computation.1 | async-start | bytes 131072 | tf_op jit(solution)/shard_map/all_to_all | solution.py:29
  81.1 13.7 %collective-permute-start.1 = (bf16[640,256]{1,0:T(8,128)(2,1)}, bf16[640,256]{1,0:T(8,128)(2,1)}, u32[]{:S(2)}, u32[]{:S(2)}) collective-permute-start(bf16[640,256]{1,0:T(8,128)(2,1)} %bitcast.8), channel_id=1, source_target_pairs={{6,0},{0,2},{2,4},{4,6},{7,1},{1,3},{3,5},{5,7},{14,8},{8,10},{10,... | collective-permute-start | bytes 983048 | tf_op jit(solution)/shard_map/ppermute | solution.py:18
  84.2 15.7 %collective-permute-start.22 = (bf16[640,256]{1,0:T(8,128)(2,1)}, bf16[640,256]{1,0:T(8,128)(2,1)S(1)}, u32[]{:S(2)}, u32[]{:S(2)}) collective-permute-start(bf16[640,256]{1,0:T(8,128)(2,1)} %bitcast.41), channel_id=1, source_target_pairs={{16,0},{32,16},{48,32},{0,48},{17,1},{33,17},{49,33},{1,49},{18,2}... | collective-permute-start | bytes 983048 | tf_op jit(solution)/shard_map/ppermute | solution.py:18
  91.6 13.4 %collective-permute-start.14 = (bf16[256,768]{1,0:T(8,128)(2,1)S(1)}, bf16[256,768]{1,0:T(8,128)(2,1)S(1)}, u32[]{:S(2)}, u32[]{:S(2)}) collective-permute-start(bf16[256,768]{1,0:T(8,128)(2,1)S(1)} %get-tuple-element.4), channel_id=1, source_target_pairs={{2,0},{4,2},{6,4},{0,6},{3,1},{5,3},{7,5},{1,7},{10,8},{12,10},{14... | collective-permute-start | bytes 1179656 | tf_op jit(solution)/shard_map/ppermute | solution.py:18
  94.8 23.7 %collective-permute-start.24 = (bf16[256,768]{1,0:T(8,128)(2,1)S(1)}, bf16[256,768]{1,0:T(8,128)(2,1)S(1)}, u32[]{:S(2)}, u32[]{:S(2)}) collective-permute-start(bf16[256,768]{1,0:T(8,128)(2,1)S(1)} %get-tuple-element.4), channel_id=1, source_target_pairs={{16,0},{32,16},{48,32},{0,48},{17,1},{33,17},{49,33},{1,49},{18,2}... | collective-permute-start | bytes 1179656 | tf_op jit(solution)/shard_map/ppermute | solution.py:18
  99.9 18.5 %collective-permute-start.25 = (bf16[256,768]{1,0:T(8,128)(2,1)S(1)}, bf16[256,768]{1,0:T(8,128)(2,1)S(1)}, u32[]{:S(2)}, u32[]{:S(2)}) collective-permute-start(bf16[256,768]{1,0:T(8,128)(2,1)S(1)} %get-tuple-element.4), channel_id=1, source_target_pairs={{48,0},{0,16},{16,32},{32,48},{49,1},{1,17},{17,33},{33,49},{50,2}... | collective-permute-start | bytes 1179656 | tf_op jit(solution)/shard_map/ppermute | solution.py:18
  104.9 13.5 %collective-permute-start.23 = (bf16[640,256]{1,0:T(8,128)(2,1)S(1)}, bf16[640,256]{1,0:T(8,128)(2,1)S(1)}, u32[]{:S(2)}, u32[]{:S(2)}) collective-permute-start(bf16[640,256]{1,0:T(8,128)(2,1)S(1)} %bitcast.148), channel_id=1, source_target_pairs={{48,0},{0,16},{16,32},{32,48},{49,1},{1,17},{17,33},{33,49},{50,2}... | collective-permute-start | bytes 983048 | tf_op jit(solution)/shard_map/ppermute | solution.py:18
  104.9 15.2 %collective-permute-start.17 = (bf16[256,768]{1,0:T(8,128)(2,1)S(1)}, bf16[256,768]{1,0:T(8,128)(2,1)S(1)}, u32[]{:S(2)}, u32[]{:S(2)}) collective-permute-start(bf16[256,768]{1,0:T(8,128)(2,1)S(1)} %collective-permute-done.14), channel_id=1, source_target_pairs={{2,0},{4,2},{6,4},{0,6},{3,1},{5,3},{7,5},{1,7},{10,8},{12,10},{14... | collective-permute-start | bytes 1179656 | tf_op jit(solution)/shard_map/ppermute | solution.py:18
  105.8 14.3 %collective-permute-start.16 = (bf16[640,256]{1,0:T(8,128)(2,1)S(1)}, bf16[640,256]{1,0:T(8,128)(2,1)S(1)}, u32[]{:S(2)}, u32[]{:S(2)}) collective-permute-start(bf16[640,256]{1,0:T(8,128)(2,1)S(1)} %bitcast.145), channel_id=1, source_target_pairs={{4,0},{6,2},{0,4},{2,6},{5,1},{7,3},{1,5},{3,7},{12,8},{14,10},{8,... | collective-permute-start | bytes 983048 | tf_op jit(solution)/shard_map/ppermute | solution.py:18
  121.4 14.1 %collective-permute-start.18 = (f32[320,768]{1,0:T(8,128)}, f32[320,768]{1,0:T(8,128)}, u32[]{:S(2)}, u32[]{:S(2)}) collective-permute-start(f32[320,768]{1,0:T(8,128)} %convolution_add_fusion.2), channel_id=1, source_target_pairs={{1,0},{0,1},{3,2},{2,3},{5,4},{4,5},{7,6},{6,7},{9,8},{8,9},{11,10... | collective-permute-start | bytes 2949128 | tf_op jit(solution)/shard_map/ppermute | solution.py:18
  130.6 29.9 %all-to-all-start.3 = ((f32[16,8,128]{2,1,0:T(8,128)}), f32[16,8,128]{2,1,0:T(8,128)}, u32[]{:S(2)}, u32[]{:S(2)}) async-start(f32[16,8,128]{2,1,0:T(8,128)} %broadcast_in_dim_broadcast_in_dim.7), calls=%async_computation.3 | async-start | bytes 131072 | tf_op jit(solution)/shard_map/all_to_all | solution.py:29
  140.1 13.3 %collective-permute-start.21 = (f32[80,768]{1,0:T(8,128)S(1)}, f32[80,768]{1,0:T(8,128)S(1)}, u32[]{:S(2)}, u32[]{:S(2)}) collective-permute-start(f32[80,768]{1,0:T(8,128)S(1)} %get-tuple-element.26), channel_id=1, source_target_pairs={{48,0},{0,16},{16,32},{32,48},{49,1},{1,17},{17,33},{33,49},{50,2}... | collective-permute-start | bytes 737288 | tf_op jit(solution)/shard_map/ppermute | solution.py:18
  160.5 22.9 %all-to-all-start.2 = ((f32[8,120,128]{2,1,0:T(8,128)}), f32[8,120,128]{2,1,0:T(8,128)S(1)}, u32[]{:S(2)}, u32[]{:S(2)}) async-start(f32[8,120,128]{2,1,0:T(8,128)} %bitcast.57), calls=%async_computation.2 | async-start | bytes 983040 | tf_op jit(solution)/shard_map/all_to_all | solution.py:130
  185.1 20.3 %all-to-all-start.4 = ((bf16[16,128,128]{2,1,0:T(8,128)(2,1)}), bf16[16,128,128]{2,1,0:T(8,128)(2,1)S(1)}, u32[]{:S(2)}, u32[]{:S(2)}) async-start(bf16[16,128,128]{2,1,0:T(8,128)(2,1)} %broadcast_in_dim.41), calls=%async_computation.4 | async-start | bytes 1048576 | tf_op jit(solution)/shard_map/all_to_all | solution.py:29
  (27 other events, 264.8 us)

commit v6 on v5

--- a/solution.py
+++ b/solution.py
@@ -127,12 +127,14 @@
         return value.reshape(-1, 2, tall, 8, 2, wide, 128).transpose(0, 1, 4, 2, 5, 3, 6)
 
     pieces = tiled(both).reshape(8, -1, 128)
-    piece = lax.all_to_all(pieces, (ZH, ZL), split_axis=0, concat_axis=0, tiled=True).sum(axis=0)
-    group_sum = summed(own_sum, SHARD)
+    near_loss = summed(own_sum, (Y, C))
+    pieces = jnp.concatenate([pieces, jnp.broadcast_to(near_loss, (8, 8, 128))], axis=1)
+    pieces = lax.all_to_all(pieces, (ZH, ZL), split_axis=0, concat_axis=0, tiled=True).sum(axis=0)
+    piece = pieces[:-8]
 
     mine = tiled(block(w_key.reshape(4, part, features), x)).reshape(4, -1, 128)
     share = (piece * block(mine, lax.axis_index(ZL)).astype(jnp.float32)).sum(axis=1)
-    share = jnp.concatenate([share, jnp.broadcast_to(group_sum, (8,))])
+    share = jnp.concatenate([share, pieces[-1, :8]])
     lines = []
     for _ in range(3):
         lines.append(lax.reduce_precision(share, 8, 7))
@@ -140,7 +142,7 @@
     lines = jnp.pad(jnp.stack(lines), ((0, 5), (0, 0)))
     whole = from_everyone(jnp.concatenate([piece, lines]).astype(jnp.bfloat16), DP)
     shares = whole[:, -8:-5].astype(jnp.float32).sum(axis=1)
-    loss = shares[:, -1].sum() / (2.0 * features * total_count)
+    loss = shares[:4, -1].sum() / (2.0 * features * total_count)
     shares = shares[:, :-8].reshape(2, 2, 4, tall, wide, 8)
     grad_gain = shares.sum(axis=(1, 4)).swapaxes(0, 1).reshape(own) / norm_gain.astype(jnp.float32)
     whole = whole[:, :-8].reshape(2, 2, 4, tall, wide, 8, 128)

time: 211 us -> 212 us (level)
  waiting for transfers between devices: 82.1 us -> 88.5 us
  starting transfers between devices: 79 us -> 74.8 us
    all_to_all x4, waiting for transfers between devices: 14.3 us -> 19.7 us  [from_everyone(): return lax.all_to_all(copies, axes, split_axis=0, concat_axis=0, tiled=True)]
    ppermute x32, starting transfers between devices: 43.9 us -> 41.4 us  [fetch(): return lax.ppermute(value, axis, [((i + step) % n, i) for i in range(n)])]
    all_to_all x1, starting transfers between devices: 7.35 us -> 5.1 us  [body(): lax.all_to_all(pieces, (ZH, ZL), split_axis=0, concat_axis=0, tiled=True)]
  transfers between devices with their start and end apart: 37 -> 37, of which waited for: 16 -> 17; matrix products, arithmetic and copies ran while one was open for 17% -> 16% of each run, Pallas kernels for 0% -> 0%
where the time goes in v6:
time: 212 us; the launch traced here: 211 us
  waiting for transfers between devices  88.5 us (42%)
  starting transfers between devices  74.8 us (35%)
  local copies, waits for them, and re-layouts  17.5 us (8%)
  matrix products  14.4 us (7%)
  other arithmetic  10.7 us (5%)
  between operations  5.51 us (3%)
    ppermute x32, waiting for transfers between devices, fetch(): return lax.ppermute(value, axis, [((i + step) % n, i) for i in range(n)])  54.3 us
    ppermute x32, starting transfers between devices, fetch(): return lax.ppermute(value, axis, [((i + step) % n, i) for i in range(n)])  41.4 us
    all_to_all x4, starting transfers between devices, from_everyone(): return lax.all_to_all(copies, axes, split_axis=0, concat_axis=0, tiled=True)  28.3 us
    all_to_all x4, waiting for transfers between devices, from_everyone(): return lax.all_to_all(copies, axes, split_axis=0, concat_axis=0, tiled=True)  19.7 us
    all_to_all x1, waiting for transfers between devices, body(): lax.all_to_all(pieces, (ZH, ZL), split_axis=0, concat_axis=0, tiled=True)  14.5 us
    dot_general x4, matrix products, rows_by(): lax.dot_general(left, right, (((0,), (0,)), ((), ())), preferred_element_...  5.8 us
    dot_general x4, matrix products, pooled(): jnp.dot(halve(left[2], side), up[2], preferred_element_type=jnp.float32)  5.63 us
    all_to_all x1, starting transfers between devices, body(): lax.all_to_all(pieces, (ZH, ZL), split_axis=0, concat_axis=0, tiled=True)  5.1 us
  transfers between devices with their start and end apart: 37, of which 17 were waited for; matrix products, arithmetic and copies ran while one was open for 16% of the time, Pallas kernels for 0%

profile of v6, /device:TPU:32, one launch (start us, length us, event | category | flops | bytes accessed | tf_op | source)
XLA Modules:
  0.0 211.4 jit_solution(10717537209128049963)
XLA Ops:
  3.3 10.3 %all-to-all-start = ((f32[16,8,128]{2,1,0:T(8,128)}), f32[16,8,128]{2,1,0:T(8,128)S(1)}, u32[]{:S(2)}, u32[]{:S(2)}) async-start(f32[16,8,128]{2,1,0:T(8,128)} %broadcast_in_dim.33), calls=%async_computation | async-start | bytes 131072 | tf_op jit(solution)/shard_map/all_to_all | solution.py:29
  13.6 3.1 %collective-permute-start.3 = (bf16[320,768]{1,0:T(8,128)(2,1)}, bf16[320,768]{1,0:T(8,128)(2,1)}, u32[]{:S(2)}, u32[]{:S(2)}) collective-permute-start(bf16[320,768]{1,0:T(8,128)(2,1)} %param.9), channel_id=1, source_target_pairs={{2,0},{4,2},{6,4},{0,6},{3,1},{5,3},{7,5},{1,7},{10,8},{12,10},{14... | collective-permute-start | bytes 1474568 | tf_op jit(solution)/shard_map/ppermute | solution.py:18
  17.7 5.5 %collective-permute-start.6 = (bf16[80,768]{1,0:T(8,128)(2,1)S(1)}, bf16[80,768]{1,0:T(8,128)(2,1)S(1)}, u32[]{:S(2)}, u32[]{:S(2)}) collective-permute-start(bf16[80,768]{1,0:T(8,128)(2,1)S(1)} %constant_dynamic-slice_fusion.10), channel_id=1, source_target_pairs={{8,0},{0,8},{9,1},{1,9},{10,2},{2,10},{11,3},{3,11},{12,4},{4,12},... | collective-permute-start | bytes 368648 | tf_op jit(solution)/shard_map/ppermute | solution.py:18
  23.1 3.0 %copy.24 = bf16[256,5120]{0,1:T(8,128)(2,1)S(1)} copy(bf16[256,5120]{1,0:T(8,128)(2,1)} %param.6) | data formatting | bytes 5242880 | tf_op args[0]
  33.3 3.9 %collective-permute-done.7 = bf16[80,768]{1,0:T(8,128)(2,1)S(1)} collective-permute-done((bf16[80,768]{1,0:T(8,128)(2,1)S(1)}, bf16[80,768]{1,0:T(8,128)(2,1)S(1)}, u32[]{:S(2)}, u32[]{:S(2)}) %collective-permute-start.7) | collective-permute-done | bytes 122912 | tf_op jit(solution)/shard_map/ppermute | solution.py:18
  41.4 2.8 %collective-permute-start.10 = (bf16[4,80,768]{2,1,0:T(8,128)(2,1)S(1)}, bf16[4,80,768]{2,1,0:T(8,128)(2,1)}, u32[]{:S(2)}, u32[]{:S(2)}) collective-permute-start(bf16[4,80,768]{2,1,0:T(8,128)(2,1)S(1)} %bitcast_dynamic-update-slice_fusion), channel_id=1, source_target_pairs={{16,0},{32,16},{48,32},{0,48},{17,1},{33,17},{49,33},{1,49},{18,2}... | collective-permute-start | bytes 1474568 | tf_op jit(solution)/shard_map/ppermute | solution.py:18
  44.3 3.2 %collective-permute-start.4 = (bf16[320,768]{1,0:T(8,128)(2,1)}, bf16[320,768]{1,0:T(8,128)(2,1)S(1)}, u32[]{:S(2)}, u32[]{:S(2)}) collective-permute-start(bf16[320,768]{1,0:T(8,128)(2,1)} %collective-permute-done.3), channel_id=1, source_target_pairs={{2,0},{4,2},{6,4},{0,6},{3,1},{5,3},{7,5},{1,7},{10,8},{12,10},{14... | collective-permute-start | bytes 1474568 | tf_op jit(solution)/shard_map/ppermute | solution.py:18
  47.5 7.4 %collective-permute-done.10 = bf16[4,80,768]{2,1,0:T(8,128)(2,1)} collective-permute-done((bf16[4,80,768]{2,1,0:T(8,128)(2,1)S(1)}, bf16[4,80,768]{2,1,0:T(8,128)(2,1)}, u32[]{:S(2)}, u32[]{:S(2)}) %collective-permute-start.10) | collective-permute-done | bytes 491552 | tf_op jit(solution)/shard_map/ppermute | solution.py:18
  54.9 3.8 %collective-permute-start.12 = (bf16[4,80,768]{2,1,0:T(8,128)(2,1)}, bf16[4,80,768]{2,1,0:T(8,128)(2,1)S(1)}, u32[]{:S(2)}, u32[]{:S(2)}) collective-permute-start(bf16[4,80,768]{2,1,0:T(8,128)(2,1)} %collective-permute-done.10), channel_id=1, source_target_pairs={{16,0},{32,16},{48,32},{0,48},{17,1},{33,17},{49,33},{1,49},{18,2}... | collective-permute-start | bytes 1474568 | tf_op jit(solution)/shard_map/ppermute | solution.py:18
  64.2 4.7 %collective-permute-done.12 = bf16[4,80,768]{2,1,0:T(8,128)(2,1)S(1)} collective-permute-done((bf16[4,80,768]{2,1,0:T(8,128)(2,1)}, bf16[4,80,768]{2,1,0:T(8,128)(2,1)S(1)}, u32[]{:S(2)}, u32[]{:S(2)}) %collective-permute-start.12) | collective-permute-done | bytes 491552 | tf_op jit(solution)/shard_map/ppermute | solution.py:18
  72.7 7.2 %all-to-all-start.1 = ((f32[16,8,128]{2,1,0:T(8,128)}), f32[16,8,128]{2,1,0:T(8,128)}, u32[]{:S(2)}, u32[]{:S(2)}) async-start(f32[16,8,128]{2,1,0:T(8,128)} %broadcast_in_dim_broadcast_in_dim.6), calls=%async_computation.1 | async-start | bytes 131072 | tf_op jit(solution)/shard_map/all_to_all | solution.py:29
  84.2 2.8 %collective-permute-start.22 = (bf16[640,256]{1,0:T(8,128)(2,1)}, bf16[640,256]{1,0:T(8,128)(2,1)S(1)}, u32[]{:S(2)}, u32[]{:S(2)}) collective-permute-start(bf16[640,256]{1,0:T(8,128)(2,1)} %bitcast.41), channel_id=1, source_target_pairs={{16,0},{32,16},{48,32},{0,48},{17,1},{33,17},{49,33},{1,49},{18,2}... | collective-permute-start | bytes 983048 | tf_op jit(solution)/shard_map/ppermute | solution.py:18
  96.5 3.4 %collective-permute-done.22 = bf16[640,256]{1,0:T(8,128)(2,1)S(1)} collective-permute-done((bf16[640,256]{1,0:T(8,128)(2,1)}, bf16[640,256]{1,0:T(8,128)(2,1)S(1)}, u32[]{:S(2)}, u32[]{:S(2)}) %collective-permute-start.22) | collective-permute-done | bytes 327712 | tf_op jit(solution)/shard_map/ppermute | solution.py:18
  99.9 5.0 %collective-permute-done.26 = bf16[640,256]{1,0:T(8,128)(2,1)S(1)} collective-permute-done((bf16[640,256]{1,0:T(8,128)(2,1)S(1)}, bf16[640,256]{1,0:T(8,128)(2,1)S(1)}, u32[]{:S(2)}, u32[]{:S(2)}) %collective-permute-start.26) | collective-permute-done | bytes 327712 | tf_op jit(solution)/shard_map/ppermute | solution.py:18
  110.5 8.0 %collective-permute-done.23 = bf16[640,256]{1,0:T(8,128)(2,1)S(1)} collective-permute-done((bf16[640,256]{1,0:T(8,128)(2,1)S(1)}, bf16[640,256]{1,0:T(8,128)(2,1)S(1)}, u32[]{:S(2)}, u32[]{:S(2)}) %collective-permute-start.23) | collective-permute-done | bytes 327712 | tf_op jit(solution)/shard_map/ppermute | solution.py:18
  121.5 6.5 %collective-permute-done.27 = bf16[256,768]{1,0:T(8,128)(2,1)S(1)} collective-permute-done((bf16[256,768]{1,0:T(8,128)(2,1)S(1)}, bf16[256,768]{1,0:T(8,128)(2,1)S(1)}, u32[]{:S(2)}, u32[]{:S(2)}) %collective-permute-start.27) | collective-permute-done | bytes 393248 | tf_op jit(solution)/shard_map/ppermute | solution.py:18
  130.5 4.7 %all-to-all-start.2 = ((f32[8,8,128]{2,1,0:T(8,128)}), f32[8,8,128]{2,1,0:T(8,128)S(1)}, u32[]{:S(2)}, u32[]{:S(2)}) async-start(f32[8,8,128]{2,1,0:T(8,128)} %broadcast_in_dim_broadcast_in_dim.7), calls=%async_computation.2 | async-start | bytes 65536 | tf_op jit(solution)/shard_map/all_to_all | solution.py:29
  135.2 5.4 %all-to-all-done.2 = f32[8,8,128]{2,1,0:T(8,128)S(1)} async-done(((f32[8,8,128]{2,1,0:T(8,128)}), f32[8,8,128]{2,1,0:T(8,128)S(1)}, u32[]{:S(2)}, u32[]{:S(2)}) %all-to-all-start.2) | async-done | bytes 32800 | tf_op jit(solution)/shard_map/all_to_all | solution.py:29
  155.0 3.8 %collective-permute-done.21 = f32[80,768]{1,0:T(8,128)S(1)} collective-permute-done((f32[80,768]{1,0:T(8,128)S(1)}, f32[80,768]{1,0:T(8,128)S(1)}, u32[]{:S(2)}, u32[]{:S(2)}) %collective-permute-start.21) | collective-permute-done | bytes 245792 | tf_op jit(solution)/shard_map/ppermute | solution.py:18
  159.5 3.0 %collective-permute-done.31 = f32[80,768]{1,0:T(8,128)S(1)} collective-permute-done((f32[80,768]{1,0:T(8,128)S(1)}, f32[80,768]{1,0:T(8,128)S(1)}, u32[]{:S(2)}, u32[]{:S(2)}) %collective-permute-start.31) | collective-permute-done | bytes 245792 | tf_op jit(solution)/shard_map/ppermute | solution.py:18
  164.1 5.1 %all-to-all-start.3 = ((f32[8,128,128]{2,1,0:T(8,128)}), f32[8,128,128]{2,1,0:T(8,128)S(1)}, u32[]{:S(2)}, u32[]{:S(2)}) async-start(f32[8,128,128]{2,1,0:T(8,128)} %concatenate.78), calls=%async_computation.3 | async-start | bytes 1048576 | tf_op jit(solution)/shard_map/all_to_all | solution.py:132
  170.2 14.5 %all-to-all-done.3 = f32[8,128,128]{2,1,0:T(8,128)S(1)} async-done(((f32[8,128,128]{2,1,0:T(8,128)}), f32[8,128,128]{2,1,0:T(8,128)S(1)}, u32[]{:S(2)}, u32[]{:S(2)}) %all-to-all-start.3) | async-done | bytes 524320 | tf_op jit(solution)/shard_map/all_to_all | solution.py:132
  185.8 6.1 %all-to-all-start.4 = ((bf16[16,128,128]{2,1,0:T(8,128)(2,1)}), bf16[16,128,128]{2,1,0:T(8,128)(2,1)S(1)}, u32[]{:S(2)}, u32[]{:S(2)}) async-start(bf16[16,128,128]{2,1,0:T(8,128)(2,1)} %broadcast_in_dim.41), calls=%async_computation.4 | async-start | bytes 1048576 | tf_op jit(solution)/shard_map/all_to_all | solution.py:29
  192.6 14.3 %all-to-all-done.4 = bf16[16,128,128]{2,1,0:T(8,128)(2,1)S(1)} async-done(((bf16[16,128,128]{2,1,0:T(8,128)(2,1)}), bf16[16,128,128]{2,1,0:T(8,128)(2,1)S(1)}, u32[]{:S(2)}, u32[]{:S(2)}) %all-to-all-start.4) | async-done | bytes 524320 | tf_op jit(solution)/shard_map/all_to_all | solution.py:29
  (148 shorter events, 68.5 us)
Async XLA Ops:
  3.3 23.5 %all-to-all-start = ((f32[16,8,128]{2,1,0:T(8,128)}), f32[16,8,128]{2,1,0:T(8,128)S(1)}, u32[]{:S(2)}, u32[]{:S(2)}) async-start(f32[16,8,128]{2,1,0:T(8,128)} %broadcast_in_dim.33), calls=%async_computation | async-start | bytes 131072 | tf_op jit(solution)/shard_map/all_to_all | solution.py:29
  13.6 30.7 %collective-permute-start.3 = (bf16[320,768]{1,0:T(8,128)(2,1)}, bf16[320,768]{1,0:T(8,128)(2,1)}, u32[]{:S(2)}, u32[]{:S(2)}) collective-permute-start(bf16[320,768]{1,0:T(8,128)(2,1)} %param.9), channel_id=1, source_target_pairs={{2,0},{4,2},{6,4},{0,6},{3,1},{5,3},{7,5},{1,7},{10,8},{12,10},{14... | collective-permute-start | bytes 1474568 | tf_op jit(solution)/shard_map/ppermute | solution.py:18
  17.7 13.3 %collective-permute-start.6 = (bf16[80,768]{1,0:T(8,128)(2,1)S(1)}, bf16[80,768]{1,0:T(8,128)(2,1)S(1)}, u32[]{:S(2)}, u32[]{:S(2)}) collective-permute-start(bf16[80,768]{1,0:T(8,128)(2,1)S(1)} %constant_dynamic-slice_fusion.10), channel_id=1, source_target_pairs={{8,0},{0,8},{9,1},{1,9},{10,2},{2,10},{11,3},{3,11},{12,4},{4,12},... | collective-permute-start | bytes 368648 | tf_op jit(solution)/shard_map/ppermute | solution.py:18
  30.9 27.8 %collective-permute-start.2 = (bf16[2,4,4,80,256]{4,3,2,1,0:T(8,128)(2,1)}, bf16[2,4,4,80,256]{4,3,2,1,0:T(8,128)(2,1)S(1)}, u32[]{:S(2)}, u32[]{:S(2)}) collective-permute-start(bf16[2,4,4,80,256]{4,3,2,1,0:T(8,128)(2,1)} %get-tuple-element.23), channel_id=1, source_target_pairs={{1,0},{0,1},{3,2},{2,3},{5,4},{4,5},{7,6},{6,7},{9,8},{8,9},{11,10... | collective-permute-start | bytes 3932168 | tf_op jit(solution)/shard_map/ppermute | solution.py:18
  41.4 13.5 %collective-permute-start.10 = (bf16[4,80,768]{2,1,0:T(8,128)(2,1)S(1)}, bf16[4,80,768]{2,1,0:T(8,128)(2,1)}, u32[]{:S(2)}, u32[]{:S(2)}) collective-permute-start(bf16[4,80,768]{2,1,0:T(8,128)(2,1)S(1)} %bitcast_dynamic-update-slice_fusion), channel_id=1, source_target_pairs={{16,0},{32,16},{48,32},{0,48},{17,1},{33,17},{49,33},{1,49},{18,2}... | collective-permute-start | bytes 1474568 | tf_op jit(solution)/shard_map/ppermute | solution.py:18
  44.3 14.6 %collective-permute-start.11 = (bf16[4,80,768]{2,1,0:T(8,128)(2,1)S(1)}, bf16[4,80,768]{2,1,0:T(8,128)(2,1)}, u32[]{:S(2)}, u32[]{:S(2)}) collective-permute-start(bf16[4,80,768]{2,1,0:T(8,128)(2,1)S(1)} %bitcast_dynamic-update-slice_fusion), channel_id=1, source_target_pairs={{48,0},{0,16},{16,32},{32,48},{49,1},{1,17},{17,33},{33,49},{50,2}... | collective-permute-start | bytes 1474568 | tf_op jit(solution)/shard_map/ppermute | solution.py:18
  44.3 17.4 %collective-permute-start.5 = (bf16[320,768]{1,0:T(8,128)(2,1)}, bf16[320,768]{1,0:T(8,128)(2,1)}, u32[]{:S(2)}, u32[]{:S(2)}) collective-permute-start(bf16[320,768]{1,0:T(8,128)(2,1)} %param.9), channel_id=1, source_target_pairs={{6,0},{0,2},{2,4},{4,6},{7,1},{1,3},{3,5},{5,7},{14,8},{8,10},{10,... | collective-permute-start | bytes 1474568 | tf_op jit(solution)/shard_map/ppermute | solution.py:18
  44.3 17.4 %collective-permute-start.4 = (bf16[320,768]{1,0:T(8,128)(2,1)}, bf16[320,768]{1,0:T(8,128)(2,1)S(1)}, u32[]{:S(2)}, u32[]{:S(2)}) collective-permute-start(bf16[320,768]{1,0:T(8,128)(2,1)} %collective-permute-done.3), channel_id=1, source_target_pairs={{2,0},{4,2},{6,4},{0,6},{3,1},{5,3},{7,5},{1,7},{10,8},{12,10},{14... | collective-permute-start | bytes 1474568 | tf_op jit(solution)/shard_map/ppermute | solution.py:18
  54.9 13.9 %collective-permute-start.12 = (bf16[4,80,768]{2,1,0:T(8,128)(2,1)}, bf16[4,80,768]{2,1,0:T(8,128)(2,1)S(1)}, u32[]{:S(2)}, u32[]{:S(2)}) collective-permute-start(bf16[4,80,768]{2,1,0:T(8,128)(2,1)} %collective-permute-done.10), channel_id=1, source_target_pairs={{16,0},{32,16},{48,32},{0,48},{17,1},{33,17},{49,33},{1,49},{18,2}... | collective-permute-start | bytes 1474568 | tf_op jit(solution)/shard_map/ppermute | solution.py:18
  70.8 18.4 %collective-permute-start.13 = (f32[256,768]{1,0:T(8,128)S(1)}, f32[256,768]{1,0:T(8,128)}, u32[]{:S(2)}, u32[]{:S(2)}) collective-permute-start(f32[256,768]{1,0:T(8,128)S(1)} %slice.57), channel_id=1, source_target_pairs={{1,0},{0,1},{3,2},{2,3},{5,4},{4,5},{7,6},{6,7},{9,8},{8,9},{11,10... | collective-permute-start | bytes 2359304 | tf_op jit(solution)/shard_map/ppermute | solution.py:18
  72.7 14.2 %all-to-all-start.1 = ((f32[16,8,128]{2,1,0:T(8,128)}), f32[16,8,128]{2,1,0:T(8,128)}, u32[]{:S(2)}, u32[]{:S(2)}) async-start(f32[16,8,128]{2,1,0:T(8,128)} %broadcast_in_dim_broadcast_in_dim.6), calls=%async_computation.1 | async-start | bytes 131072 | tf_op jit(solution)/shard_map/all_to_all | solution.py:29
  81.1 13.7 %collective-permute-start.1 = (bf16[640,256]{1,0:T(8,128)(2,1)}, bf16[640,256]{1,0:T(8,128)(2,1)}, u32[]{:S(2)}, u32[]{:S(2)}) collective-permute-start(bf16[640,256]{1,0:T(8,128)(2,1)} %bitcast.8), channel_id=1, source_target_pairs={{6,0},{0,2},{2,4},{4,6},{7,1},{1,3},{3,5},{5,7},{14,8},{8,10},{10,... | collective-permute-start | bytes 983048 | tf_op jit(solution)/shard_map/ppermute | solution.py:18
  84.2 15.7 %collective-permute-start.22 = (bf16[640,256]{1,0:T(8,128)(2,1)}, bf16[640,256]{1,0:T(8,128)(2,1)S(1)}, u32[]{:S(2)}, u32[]{:S(2)}) collective-permute-start(bf16[640,256]{1,0:T(8,128)(2,1)} %bitcast.41), channel_id=1, source_target_pairs={{16,0},{32,16},{48,32},{0,48},{17,1},{33,17},{49,33},{1,49},{18,2}... | collective-permute-start | bytes 983048 | tf_op jit(solution)/shard_map/ppermute | solution.py:18
  91.6 13.4 %collective-permute-start.14 = (bf16[256,768]{1,0:T(8,128)(2,1)S(1)}, bf16[256,768]{1,0:T(8,128)(2,1)S(1)}, u32[]{:S(2)}, u32[]{:S(2)}) collective-permute-start(bf16[256,768]{1,0:T(8,128)(2,1)S(1)} %get-tuple-element.6), channel_id=1, source_target_pairs={{2,0},{4,2},{6,4},{0,6},{3,1},{5,3},{7,5},{1,7},{10,8},{12,10},{14... | collective-permute-start | bytes 1179656 | tf_op jit(solution)/shard_map/ppermute | solution.py:18
  94.8 23.7 %collective-permute-start.24 = (bf16[256,768]{1,0:T(8,128)(2,1)S(1)}, bf16[256,768]{1,0:T(8,128)(2,1)S(1)}, u32[]{:S(2)}, u32[]{:S(2)}) collective-permute-start(bf16[256,768]{1,0:T(8,128)(2,1)S(1)} %get-tuple-element.6), channel_id=1, source_target_pairs={{16,0},{32,16},{48,32},{0,48},{17,1},{33,17},{49,33},{1,49},{18,2}... | collective-permute-start | bytes 1179656 | tf_op jit(solution)/shard_map/ppermute | solution.py:18
  99.9 18.5 %collective-permute-start.25 = (bf16[256,768]{1,0:T(8,128)(2,1)S(1)}, bf16[256,768]{1,0:T(8,128)(2,1)S(1)}, u32[]{:S(2)}, u32[]{:S(2)}) collective-permute-start(bf16[256,768]{1,0:T(8,128)(2,1)S(1)} %get-tuple-element.6), channel_id=1, source_target_pairs={{48,0},{0,16},{16,32},{32,48},{49,1},{1,17},{17,33},{33,49},{50,2}... | collective-permute-start | bytes 1179656 | tf_op jit(solution)/shard_map/ppermute | solution.py:18
  104.9 13.5 %collective-permute-start.23 = (bf16[640,256]{1,0:T(8,128)(2,1)S(1)}, bf16[640,256]{1,0:T(8,128)(2,1)S(1)}, u32[]{:S(2)}, u32[]{:S(2)}) collective-permute-start(bf16[640,256]{1,0:T(8,128)(2,1)S(1)} %bitcast.144), channel_id=1, source_target_pairs={{48,0},{0,16},{16,32},{32,48},{49,1},{1,17},{17,33},{33,49},{50,2}... | collective-permute-start | bytes 983048 | tf_op jit(solution)/shard_map/ppermute | solution.py:18
  104.9 15.2 %collective-permute-start.17 = (bf16[256,768]{1,0:T(8,128)(2,1)S(1)}, bf16[256,768]{1,0:T(8,128)(2,1)S(1)}, u32[]{:S(2)}, u32[]{:S(2)}) collective-permute-start(bf16[256,768]{1,0:T(8,128)(2,1)S(1)} %collective-permute-done.14), channel_id=1, source_target_pairs={{2,0},{4,2},{6,4},{0,6},{3,1},{5,3},{7,5},{1,7},{10,8},{12,10},{14... | collective-permute-start | bytes 1179656 | tf_op jit(solution)/shard_map/ppermute | solution.py:18
  105.8 14.3 %collective-permute-start.16 = (bf16[640,256]{1,0:T(8,128)(2,1)S(1)}, bf16[640,256]{1,0:T(8,128)(2,1)S(1)}, u32[]{:S(2)}, u32[]{:S(2)}) collective-permute-start(bf16[640,256]{1,0:T(8,128)(2,1)S(1)} %bitcast.141), channel_id=1, source_target_pairs={{4,0},{6,2},{0,4},{2,6},{5,1},{7,3},{1,5},{3,7},{12,8},{14,10},{8,... | collective-permute-start | bytes 983048 | tf_op jit(solution)/shard_map/ppermute | solution.py:18
  121.4 19.9 %collective-permute-start.18 = (f32[320,768]{1,0:T(8,128)}, f32[320,768]{1,0:T(8,128)}, u32[]{:S(2)}, u32[]{:S(2)}) collective-permute-start(f32[320,768]{1,0:T(8,128)} %convolution_add_fusion.2), channel_id=1, source_target_pairs={{1,0},{0,1},{3,2},{2,3},{5,4},{4,5},{7,6},{6,7},{9,8},{8,9},{11,10... | collective-permute-start | bytes 2949128 | tf_op jit(solution)/shard_map/ppermute | solution.py:18
  129.3 17.1 %collective-permute-start.28 = (f32[320,768]{1,0:T(8,128)}, f32[320,768]{1,0:T(8,128)}, u32[]{:S(2)}, u32[]{:S(2)}) collective-permute-start(f32[320,768]{1,0:T(8,128)} %convolution_add_fusion), channel_id=1, source_target_pairs={{1,0},{0,1},{3,2},{2,3},{5,4},{4,5},{7,6},{6,7},{9,8},{8,9},{11,10... | collective-permute-start | bytes 2949128 | tf_op jit(solution)/shard_map/ppermute | solution.py:18
  145.3 13.4 %collective-permute-start.21 = (f32[80,768]{1,0:T(8,128)S(1)}, f32[80,768]{1,0:T(8,128)S(1)}, u32[]{:S(2)}, u32[]{:S(2)}) collective-permute-start(f32[80,768]{1,0:T(8,128)S(1)} %get-tuple-element.28), channel_id=1, source_target_pairs={{48,0},{0,16},{16,32},{32,48},{49,1},{1,17},{17,33},{33,49},{50,2}... | collective-permute-start | bytes 737288 | tf_op jit(solution)/shard_map/ppermute | solution.py:18
  164.1 20.5 %all-to-all-start.3 = ((f32[8,128,128]{2,1,0:T(8,128)}), f32[8,128,128]{2,1,0:T(8,128)S(1)}, u32[]{:S(2)}, u32[]{:S(2)}) async-start(f32[8,128,128]{2,1,0:T(8,128)} %concatenate.78), calls=%async_computation.3 | async-start | bytes 1048576 | tf_op jit(solution)/shard_map/all_to_all | solution.py:132
  185.8 21.0 %all-to-all-start.4 = ((bf16[16,128,128]{2,1,0:T(8,128)(2,1)}), bf16[16,128,128]{2,1,0:T(8,128)(2,1)S(1)}, u32[]{:S(2)}, u32[]{:S(2)}) async-start(bf16[16,128,128]{2,1,0:T(8,128)(2,1)} %broadcast_in_dim.41), calls=%async_computation.4 | async-start | bytes 1048576 | tf_op jit(solution)/shard_map/all_to_all | solution.py:29
  (27 other events, 257.1 us)

commit v7 on v6

--- a/solution.py
+++ b/solution.py
@@ -102,9 +102,11 @@
             preferred_element_type=jnp.float32,
         )
         first = lax.optimization_barrier(first)
+        sides = (1 - core, core)
+        last = [halve(left[2], side) for side in sides]
         return [
-            halve(first, side) + jnp.dot(halve(left[2], side), up[2], preferred_element_type=jnp.float32)
-            for side in (1 - core, core)
+            halve(first, side) + jnp.dot(half, up[2], preferred_element_type=jnp.float32)
+            for side, half in zip(sides, last)
         ]
 
     def near_rows(value, side):

time: 212 us -> 212 us (level)
  no operation moved by 1% of the time
where the time goes in v7:
time: 212 us; the launch traced here: 211 us
  waiting for transfers between devices  88.5 us (42%)
  starting transfers between devices  74.8 us (35%)
  local copies, waits for them, and re-layouts  17.5 us (8%)
  matrix products  14.4 us (7%)
  other arithmetic  10.7 us (5%)
  between operations  5.51 us (3%)
    ppermute x32, waiting for transfers between devices, fetch(): return lax.ppermute(value, axis, [((i + step) % n, i) for i in range(n)])  54.3 us
    ppermute x32, starting transfers between devices, fetch(): return lax.ppermute(value, axis, [((i + step) % n, i) for i in range(n)])  41.4 us
    all_to_all x4, starting transfers between devices, from_everyone(): return lax.all_to_all(copies, axes, split_axis=0, concat_axis=0, tiled=True)  28.3 us
    all_to_all x4, waiting for transfers between devices, from_everyone(): return lax.all_to_all(copies, axes, split_axis=0, concat_axis=0, tiled=True)  19.7 us
    all_to_all x1, waiting for transfers between devices, body(): lax.all_to_all(pieces, (ZH, ZL), split_axis=0, concat_axis=0, tiled=True)  14.5 us
    dot_general x4, matrix products, rows_by(): lax.dot_general(left, right, (((0,), (0,)), ((), ())), preferred_element_...  5.8 us
    dot_general x4, matrix products, pooled(): jnp.dot(half, up[2], preferred_element_type=jnp.float32)  5.63 us
    all_to_all x1, starting transfers between devices, body(): lax.all_to_all(pieces, (ZH, ZL), split_axis=0, concat_axis=0, tiled=True)  5.1 us
  transfers between devices with their start and end apart: 37, of which 17 were waited for; matrix products, arithmetic and copies ran while one was open for 16% of the time, Pallas kernels for 0%

profile of v7, /device:TPU:32, one launch (start us, length us, event | category | flops | bytes accessed | tf_op | source)
XLA Modules:
  0.0 211.4 jit_solution(10717537209128049963)
XLA Ops:
  3.3 10.3 %all-to-all-start = ((f32[16,8,128]{2,1,0:T(8,128)}), f32[16,8,128]{2,1,0:T(8,128)S(1)}, u32[]{:S(2)}, u32[]{:S(2)}) async-start(f32[16,8,128]{2,1,0:T(8,128)} %broadcast_in_dim.33), calls=%async_computation | async-start | bytes 131072 | tf_op jit(solution)/shard_map/all_to_all | solution.py:29
  13.6 3.1 %collective-permute-start.3 = (bf16[320,768]{1,0:T(8,128)(2,1)}, bf16[320,768]{1,0:T(8,128)(2,1)}, u32[]{:S(2)}, u32[]{:S(2)}) collective-permute-start(bf16[320,768]{1,0:T(8,128)(2,1)} %param.9), channel_id=1, source_target_pairs={{2,0},{4,2},{6,4},{0,6},{3,1},{5,3},{7,5},{1,7},{10,8},{12,10},{14... | collective-permute-start | bytes 1474568 | tf_op jit(solution)/shard_map/ppermute | solution.py:18
  17.7 5.5 %collective-permute-start.6 = (bf16[80,768]{1,0:T(8,128)(2,1)S(1)}, bf16[80,768]{1,0:T(8,128)(2,1)S(1)}, u32[]{:S(2)}, u32[]{:S(2)}) collective-permute-start(bf16[80,768]{1,0:T(8,128)(2,1)S(1)} %constant_dynamic-slice_fusion.10), channel_id=1, source_target_pairs={{8,0},{0,8},{9,1},{1,9},{10,2},{2,10},{11,3},{3,11},{12,4},{4,12},... | collective-permute-start | bytes 368648 | tf_op jit(solution)/shard_map/ppermute | solution.py:18
  23.1 3.0 %copy.24 = bf16[256,5120]{0,1:T(8,128)(2,1)S(1)} copy(bf16[256,5120]{1,0:T(8,128)(2,1)} %param.6) | data formatting | bytes 5242880 | tf_op args[0]
  33.3 3.9 %collective-permute-done.7 = bf16[80,768]{1,0:T(8,128)(2,1)S(1)} collective-permute-done((bf16[80,768]{1,0:T(8,128)(2,1)S(1)}, bf16[80,768]{1,0:T(8,128)(2,1)S(1)}, u32[]{:S(2)}, u32[]{:S(2)}) %collective-permute-start.7) | collective-permute-done | bytes 122912 | tf_op jit(solution)/shard_map/ppermute | solution.py:18
  41.4 2.8 %collective-permute-start.10 = (bf16[4,80,768]{2,1,0:T(8,128)(2,1)S(1)}, bf16[4,80,768]{2,1,0:T(8,128)(2,1)}, u32[]{:S(2)}, u32[]{:S(2)}) collective-permute-start(bf16[4,80,768]{2,1,0:T(8,128)(2,1)S(1)} %bitcast_dynamic-update-slice_fusion), channel_id=1, source_target_pairs={{16,0},{32,16},{48,32},{0,48},{17,1},{33,17},{49,33},{1,49},{18,2}... | collective-permute-start | bytes 1474568 | tf_op jit(solution)/shard_map/ppermute | solution.py:18
  44.3 3.2 %collective-permute-start.4 = (bf16[320,768]{1,0:T(8,128)(2,1)}, bf16[320,768]{1,0:T(8,128)(2,1)S(1)}, u32[]{:S(2)}, u32[]{:S(2)}) collective-permute-start(bf16[320,768]{1,0:T(8,128)(2,1)} %collective-permute-done.3), channel_id=1, source_target_pairs={{2,0},{4,2},{6,4},{0,6},{3,1},{5,3},{7,5},{1,7},{10,8},{12,10},{14... | collective-permute-start | bytes 1474568 | tf_op jit(solution)/shard_map/ppermute | solution.py:18
  47.5 7.4 %collective-permute-done.10 = bf16[4,80,768]{2,1,0:T(8,128)(2,1)} collective-permute-done((bf16[4,80,768]{2,1,0:T(8,128)(2,1)S(1)}, bf16[4,80,768]{2,1,0:T(8,128)(2,1)}, u32[]{:S(2)}, u32[]{:S(2)}) %collective-permute-start.10) | collective-permute-done | bytes 491552 | tf_op jit(solution)/shard_map/ppermute | solution.py:18
  54.9 3.8 %collective-permute-start.12 = (bf16[4,80,768]{2,1,0:T(8,128)(2,1)}, bf16[4,80,768]{2,1,0:T(8,128)(2,1)S(1)}, u32[]{:S(2)}, u32[]{:S(2)}) collective-permute-start(bf16[4,80,768]{2,1,0:T(8,128)(2,1)} %collective-permute-done.10), channel_id=1, source_target_pairs={{16,0},{32,16},{48,32},{0,48},{17,1},{33,17},{49,33},{1,49},{18,2}... | collective-permute-start | bytes 1474568 | tf_op jit(solution)/shard_map/ppermute | solution.py:18
  64.2 4.7 %collective-permute-done.12 = bf16[4,80,768]{2,1,0:T(8,128)(2,1)S(1)} collective-permute-done((bf16[4,80,768]{2,1,0:T(8,128)(2,1)}, bf16[4,80,768]{2,1,0:T(8,128)(2,1)S(1)}, u32[]{:S(2)}, u32[]{:S(2)}) %collective-permute-start.12) | collective-permute-done | bytes 491552 | tf_op jit(solution)/shard_map/ppermute | solution.py:18
  72.7 7.2 %all-to-all-start.1 = ((f32[16,8,128]{2,1,0:T(8,128)}), f32[16,8,128]{2,1,0:T(8,128)}, u32[]{:S(2)}, u32[]{:S(2)}) async-start(f32[16,8,128]{2,1,0:T(8,128)} %broadcast_in_dim_broadcast_in_dim.6), calls=%async_computation.1 | async-start | bytes 131072 | tf_op jit(solution)/shard_map/all_to_all | solution.py:29
  84.2 2.8 %collective-permute-start.22 = (bf16[640,256]{1,0:T(8,128)(2,1)}, bf16[640,256]{1,0:T(8,128)(2,1)S(1)}, u32[]{:S(2)}, u32[]{:S(2)}) collective-permute-start(bf16[640,256]{1,0:T(8,128)(2,1)} %bitcast.41), channel_id=1, source_target_pairs={{16,0},{32,16},{48,32},{0,48},{17,1},{33,17},{49,33},{1,49},{18,2}... | collective-permute-start | bytes 983048 | tf_op jit(solution)/shard_map/ppermute | solution.py:18
  96.5 3.4 %collective-permute-done.22 = bf16[640,256]{1,0:T(8,128)(2,1)S(1)} collective-permute-done((bf16[640,256]{1,0:T(8,128)(2,1)}, bf16[640,256]{1,0:T(8,128)(2,1)S(1)}, u32[]{:S(2)}, u32[]{:S(2)}) %collective-permute-start.22) | collective-permute-done | bytes 327712 | tf_op jit(solution)/shard_map/ppermute | solution.py:18
  99.9 5.0 %collective-permute-done.26 = bf16[640,256]{1,0:T(8,128)(2,1)S(1)} collective-permute-done((bf16[640,256]{1,0:T(8,128)(2,1)S(1)}, bf16[640,256]{1,0:T(8,128)(2,1)S(1)}, u32[]{:S(2)}, u32[]{:S(2)}) %collective-permute-start.26) | collective-permute-done | bytes 327712 | tf_op jit(solution)/shard_map/ppermute | solution.py:18
  110.5 8.0 %collective-permute-done.23 = bf16[640,256]{1,0:T(8,128)(2,1)S(1)} collective-permute-done((bf16[640,256]{1,0:T(8,128)(2,1)S(1)}, bf16[640,256]{1,0:T(8,128)(2,1)S(1)}, u32[]{:S(2)}, u32[]{:S(2)}) %collective-permute-start.23) | collective-permute-done | bytes 327712 | tf_op jit(solution)/shard_map/ppermute | solution.py:18
  121.5 6.5 %collective-permute-done.27 = bf16[256,768]{1,0:T(8,128)(2,1)S(1)} collective-permute-done((bf16[256,768]{1,0:T(8,128)(2,1)S(1)}, bf16[256,768]{1,0:T(8,128)(2,1)S(1)}, u32[]{:S(2)}, u32[]{:S(2)}) %collective-permute-start.27) | collective-permute-done | bytes 393248 | tf_op jit(solution)/shard_map/ppermute | solution.py:18
  130.5 4.7 %all-to-all-start.2 = ((f32[8,8,128]{2,1,0:T(8,128)}), f32[8,8,128]{2,1,0:T(8,128)S(1)}, u32[]{:S(2)}, u32[]{:S(2)}) async-start(f32[8,8,128]{2,1,0:T(8,128)} %broadcast_in_dim_broadcast_in_dim.7), calls=%async_computation.2 | async-start | bytes 65536 | tf_op jit(solution)/shard_map/all_to_all | solution.py:29
  135.2 5.4 %all-to-all-done.2 = f32[8,8,128]{2,1,0:T(8,128)S(1)} async-done(((f32[8,8,128]{2,1,0:T(8,128)}), f32[8,8,128]{2,1,0:T(8,128)S(1)}, u32[]{:S(2)}, u32[]{:S(2)}) %all-to-all-start.2) | async-done | bytes 32800 | tf_op jit(solution)/shard_map/all_to_all | solution.py:29
  155.0 3.8 %collective-permute-done.21 = f32[80,768]{1,0:T(8,128)S(1)} collective-permute-done((f32[80,768]{1,0:T(8,128)S(1)}, f32[80,768]{1,0:T(8,128)S(1)}, u32[]{:S(2)}, u32[]{:S(2)}) %collective-permute-start.21) | collective-permute-done | bytes 245792 | tf_op jit(solution)/shard_map/ppermute | solution.py:18
  159.5 3.0 %collective-permute-done.31 = f32[80,768]{1,0:T(8,128)S(1)} collective-permute-done((f32[80,768]{1,0:T(8,128)S(1)}, f32[80,768]{1,0:T(8,128)S(1)}, u32[]{:S(2)}, u32[]{:S(2)}) %collective-permute-start.31) | collective-permute-done | bytes 245792 | tf_op jit(solution)/shard_map/ppermute | solution.py:18
  164.1 5.1 %all-to-all-start.3 = ((f32[8,128,128]{2,1,0:T(8,128)}), f32[8,128,128]{2,1,0:T(8,128)S(1)}, u32[]{:S(2)}, u32[]{:S(2)}) async-start(f32[8,128,128]{2,1,0:T(8,128)} %concatenate.78), calls=%async_computation.3 | async-start | bytes 1048576 | tf_op jit(solution)/shard_map/all_to_all | solution.py:134
  170.2 14.5 %all-to-all-done.3 = f32[8,128,128]{2,1,0:T(8,128)S(1)} async-done(((f32[8,128,128]{2,1,0:T(8,128)}), f32[8,128,128]{2,1,0:T(8,128)S(1)}, u32[]{:S(2)}, u32[]{:S(2)}) %all-to-all-start.3) | async-done | bytes 524320 | tf_op jit(solution)/shard_map/all_to_all | solution.py:134
  185.8 6.1 %all-to-all-start.4 = ((bf16[16,128,128]{2,1,0:T(8,128)(2,1)}), bf16[16,128,128]{2,1,0:T(8,128)(2,1)S(1)}, u32[]{:S(2)}, u32[]{:S(2)}) async-start(bf16[16,128,128]{2,1,0:T(8,128)(2,1)} %broadcast_in_dim.41), calls=%async_computation.4 | async-start | bytes 1048576 | tf_op jit(solution)/shard_map/all_to_all | solution.py:29
  192.6 14.3 %all-to-all-done.4 = bf16[16,128,128]{2,1,0:T(8,128)(2,1)S(1)} async-done(((bf16[16,128,128]{2,1,0:T(8,128)(2,1)}), bf16[16,128,128]{2,1,0:T(8,128)(2,1)S(1)}, u32[]{:S(2)}, u32[]{:S(2)}) %all-to-all-start.4) | async-done | bytes 524320 | tf_op jit(solution)/shard_map/all_to_all | solution.py:29
  (148 shorter events, 68.5 us)
Async XLA Ops:
  3.3 23.5 %all-to-all-start = ((f32[16,8,128]{2,1,0:T(8,128)}), f32[16,8,128]{2,1,0:T(8,128)S(1)}, u32[]{:S(2)}, u32[]{:S(2)}) async-start(f32[16,8,128]{2,1,0:T(8,128)} %broadcast_in_dim.33), calls=%async_computation | async-start | bytes 131072 | tf_op jit(solution)/shard_map/all_to_all | solution.py:29
  13.6 30.7 %collective-permute-start.3 = (bf16[320,768]{1,0:T(8,128)(2,1)}, bf16[320,768]{1,0:T(8,128)(2,1)}, u32[]{:S(2)}, u32[]{:S(2)}) collective-permute-start(bf16[320,768]{1,0:T(8,128)(2,1)} %param.9), channel_id=1, source_target_pairs={{2,0},{4,2},{6,4},{0,6},{3,1},{5,3},{7,5},{1,7},{10,8},{12,10},{14... | collective-permute-start | bytes 1474568 | tf_op jit(solution)/shard_map/ppermute | solution.py:18
  17.7 13.3 %collective-permute-start.6 = (bf16[80,768]{1,0:T(8,128)(2,1)S(1)}, bf16[80,768]{1,0:T(8,128)(2,1)S(1)}, u32[]{:S(2)}, u32[]{:S(2)}) collective-permute-start(bf16[80,768]{1,0:T(8,128)(2,1)S(1)} %constant_dynamic-slice_fusion.10), channel_id=1, source_target_pairs={{8,0},{0,8},{9,1},{1,9},{10,2},{2,10},{11,3},{3,11},{12,4},{4,12},... | collective-permute-start | bytes 368648 | tf_op jit(solution)/shard_map/ppermute | solution.py:18
  30.9 27.8 %collective-permute-start.2 = (bf16[2,4,4,80,256]{4,3,2,1,0:T(8,128)(2,1)}, bf16[2,4,4,80,256]{4,3,2,1,0:T(8,128)(2,1)S(1)}, u32[]{:S(2)}, u32[]{:S(2)}) collective-permute-start(bf16[2,4,4,80,256]{4,3,2,1,0:T(8,128)(2,1)} %get-tuple-element.23), channel_id=1, source_target_pairs={{1,0},{0,1},{3,2},{2,3},{5,4},{4,5},{7,6},{6,7},{9,8},{8,9},{11,10... | collective-permute-start | bytes 3932168 | tf_op jit(solution)/shard_map/ppermute | solution.py:18
  41.4 13.5 %collective-permute-start.10 = (bf16[4,80,768]{2,1,0:T(8,128)(2,1)S(1)}, bf16[4,80,768]{2,1,0:T(8,128)(2,1)}, u32[]{:S(2)}, u32[]{:S(2)}) collective-permute-start(bf16[4,80,768]{2,1,0:T(8,128)(2,1)S(1)} %bitcast_dynamic-update-slice_fusion), channel_id=1, source_target_pairs={{16,0},{32,16},{48,32},{0,48},{17,1},{33,17},{49,33},{1,49},{18,2}... | collective-permute-start | bytes 1474568 | tf_op jit(solution)/shard_map/ppermute | solution.py:18
  44.3 14.6 %collective-permute-start.11 = (bf16[4,80,768]{2,1,0:T(8,128)(2,1)S(1)}, bf16[4,80,768]{2,1,0:T(8,128)(2,1)}, u32[]{:S(2)}, u32[]{:S(2)}) collective-permute-start(bf16[4,80,768]{2,1,0:T(8,128)(2,1)S(1)} %bitcast_dynamic-update-slice_fusion), channel_id=1, source_target_pairs={{48,0},{0,16},{16,32},{32,48},{49,1},{1,17},{17,33},{33,49},{50,2}... | collective-permute-start | bytes 1474568 | tf_op jit(solution)/shard_map/ppermute | solution.py:18
  44.3 17.4 %collective-permute-start.5 = (bf16[320,768]{1,0:T(8,128)(2,1)}, bf16[320,768]{1,0:T(8,128)(2,1)}, u32[]{:S(2)}, u32[]{:S(2)}) collective-permute-start(bf16[320,768]{1,0:T(8,128)(2,1)} %param.9), channel_id=1, source_target_pairs={{6,0},{0,2},{2,4},{4,6},{7,1},{1,3},{3,5},{5,7},{14,8},{8,10},{10,... | collective-permute-start | bytes 1474568 | tf_op jit(solution)/shard_map/ppermute | solution.py:18
  44.3 17.4 %collective-permute-start.4 = (bf16[320,768]{1,0:T(8,128)(2,1)}, bf16[320,768]{1,0:T(8,128)(2,1)S(1)}, u32[]{:S(2)}, u32[]{:S(2)}) collective-permute-start(bf16[320,768]{1,0:T(8,128)(2,1)} %collective-permute-done.3), channel_id=1, source_target_pairs={{2,0},{4,2},{6,4},{0,6},{3,1},{5,3},{7,5},{1,7},{10,8},{12,10},{14... | collective-permute-start | bytes 1474568 | tf_op jit(solution)/shard_map/ppermute | solution.py:18
  54.9 13.9 %collective-permute-start.12 = (bf16[4,80,768]{2,1,0:T(8,128)(2,1)}, bf16[4,80,768]{2,1,0:T(8,128)(2,1)S(1)}, u32[]{:S(2)}, u32[]{:S(2)}) collective-permute-start(bf16[4,80,768]{2,1,0:T(8,128)(2,1)} %collective-permute-done.10), channel_id=1, source_target_pairs={{16,0},{32,16},{48,32},{0,48},{17,1},{33,17},{49,33},{1,49},{18,2}... | collective-permute-start | bytes 1474568 | tf_op jit(solution)/shard_map/ppermute | solution.py:18
  70.8 18.4 %collective-permute-start.13 = (f32[256,768]{1,0:T(8,128)S(1)}, f32[256,768]{1,0:T(8,128)}, u32[]{:S(2)}, u32[]{:S(2)}) collective-permute-start(f32[256,768]{1,0:T(8,128)S(1)} %slice.57), channel_id=1, source_target_pairs={{1,0},{0,1},{3,2},{2,3},{5,4},{4,5},{7,6},{6,7},{9,8},{8,9},{11,10... | collective-permute-start | bytes 2359304 | tf_op jit(solution)/shard_map/ppermute | solution.py:18
  72.7 14.2 %all-to-all-start.1 = ((f32[16,8,128]{2,1,0:T(8,128)}), f32[16,8,128]{2,1,0:T(8,128)}, u32[]{:S(2)}, u32[]{:S(2)}) async-start(f32[16,8,128]{2,1,0:T(8,128)} %broadcast_in_dim_broadcast_in_dim.6), calls=%async_computation.1 | async-start | bytes 131072 | tf_op jit(solution)/shard_map/all_to_all | solution.py:29
  81.1 13.7 %collective-permute-start.1 = (bf16[640,256]{1,0:T(8,128)(2,1)}, bf16[640,256]{1,0:T(8,128)(2,1)}, u32[]{:S(2)}, u32[]{:S(2)}) collective-permute-start(bf16[640,256]{1,0:T(8,128)(2,1)} %bitcast.8), channel_id=1, source_target_pairs={{6,0},{0,2},{2,4},{4,6},{7,1},{1,3},{3,5},{5,7},{14,8},{8,10},{10,... | collective-permute-start | bytes 983048 | tf_op jit(solution)/shard_map/ppermute | solution.py:18
  84.2 15.7 %collective-permute-start.22 = (bf16[640,256]{1,0:T(8,128)(2,1)}, bf16[640,256]{1,0:T(8,128)(2,1)S(1)}, u32[]{:S(2)}, u32[]{:S(2)}) collective-permute-start(bf16[640,256]{1,0:T(8,128)(2,1)} %bitcast.41), channel_id=1, source_target_pairs={{16,0},{32,16},{48,32},{0,48},{17,1},{33,17},{49,33},{1,49},{18,2}... | collective-permute-start | bytes 983048 | tf_op jit(solution)/shard_map/ppermute | solution.py:18
  91.6 13.4 %collective-permute-start.14 = (bf16[256,768]{1,0:T(8,128)(2,1)S(1)}, bf16[256,768]{1,0:T(8,128)(2,1)S(1)}, u32[]{:S(2)}, u32[]{:S(2)}) collective-permute-start(bf16[256,768]{1,0:T(8,128)(2,1)S(1)} %get-tuple-element.6), channel_id=1, source_target_pairs={{2,0},{4,2},{6,4},{0,6},{3,1},{5,3},{7,5},{1,7},{10,8},{12,10},{14... | collective-permute-start | bytes 1179656 | tf_op jit(solution)/shard_map/ppermute | solution.py:18
  94.8 23.7 %collective-permute-start.24 = (bf16[256,768]{1,0:T(8,128)(2,1)S(1)}, bf16[256,768]{1,0:T(8,128)(2,1)S(1)}, u32[]{:S(2)}, u32[]{:S(2)}) collective-permute-start(bf16[256,768]{1,0:T(8,128)(2,1)S(1)} %get-tuple-element.6), channel_id=1, source_target_pairs={{16,0},{32,16},{48,32},{0,48},{17,1},{33,17},{49,33},{1,49},{18,2}... | collective-permute-start | bytes 1179656 | tf_op jit(solution)/shard_map/ppermute | solution.py:18
  99.9 18.5 %collective-permute-start.25 = (bf16[256,768]{1,0:T(8,128)(2,1)S(1)}, bf16[256,768]{1,0:T(8,128)(2,1)S(1)}, u32[]{:S(2)}, u32[]{:S(2)}) collective-permute-start(bf16[256,768]{1,0:T(8,128)(2,1)S(1)} %get-tuple-element.6), channel_id=1, source_target_pairs={{48,0},{0,16},{16,32},{32,48},{49,1},{1,17},{17,33},{33,49},{50,2}... | collective-permute-start | bytes 1179656 | tf_op jit(solution)/shard_map/ppermute | solution.py:18
  104.9 13.5 %collective-permute-start.23 = (bf16[640,256]{1,0:T(8,128)(2,1)S(1)}, bf16[640,256]{1,0:T(8,128)(2,1)S(1)}, u32[]{:S(2)}, u32[]{:S(2)}) collective-permute-start(bf16[640,256]{1,0:T(8,128)(2,1)S(1)} %bitcast.144), channel_id=1, source_target_pairs={{48,0},{0,16},{16,32},{32,48},{49,1},{1,17},{17,33},{33,49},{50,2}... | collective-permute-start | bytes 983048 | tf_op jit(solution)/shard_map/ppermute | solution.py:18
  104.9 15.2 %collective-permute-start.17 = (bf16[256,768]{1,0:T(8,128)(2,1)S(1)}, bf16[256,768]{1,0:T(8,128)(2,1)S(1)}, u32[]{:S(2)}, u32[]{:S(2)}) collective-permute-start(bf16[256,768]{1,0:T(8,128)(2,1)S(1)} %collective-permute-done.14), channel_id=1, source_target_pairs={{2,0},{4,2},{6,4},{0,6},{3,1},{5,3},{7,5},{1,7},{10,8},{12,10},{14... | collective-permute-start | bytes 1179656 | tf_op jit(solution)/shard_map/ppermute | solution.py:18
  105.8 14.3 %collective-permute-start.16 = (bf16[640,256]{1,0:T(8,128)(2,1)S(1)}, bf16[640,256]{1,0:T(8,128)(2,1)S(1)}, u32[]{:S(2)}, u32[]{:S(2)}) collective-permute-start(bf16[640,256]{1,0:T(8,128)(2,1)S(1)} %bitcast.141), channel_id=1, source_target_pairs={{4,0},{6,2},{0,4},{2,6},{5,1},{7,3},{1,5},{3,7},{12,8},{14,10},{8,... | collective-permute-start | bytes 983048 | tf_op jit(solution)/shard_map/ppermute | solution.py:18
  121.4 19.9 %collective-permute-start.18 = (f32[320,768]{1,0:T(8,128)}, f32[320,768]{1,0:T(8,128)}, u32[]{:S(2)}, u32[]{:S(2)}) collective-permute-start(f32[320,768]{1,0:T(8,128)} %convolution_add_fusion.2), channel_id=1, source_target_pairs={{1,0},{0,1},{3,2},{2,3},{5,4},{4,5},{7,6},{6,7},{9,8},{8,9},{11,10... | collective-permute-start | bytes 2949128 | tf_op jit(solution)/shard_map/ppermute | solution.py:18
  129.3 17.1 %collective-permute-start.28 = (f32[320,768]{1,0:T(8,128)}, f32[320,768]{1,0:T(8,128)}, u32[]{:S(2)}, u32[]{:S(2)}) collective-permute-start(f32[320,768]{1,0:T(8,128)} %convolution_add_fusion), channel_id=1, source_target_pairs={{1,0},{0,1},{3,2},{2,3},{5,4},{4,5},{7,6},{6,7},{9,8},{8,9},{11,10... | collective-permute-start | bytes 2949128 | tf_op jit(solution)/shard_map/ppermute | solution.py:18
  145.3 13.4 %collective-permute-start.21 = (f32[80,768]{1,0:T(8,128)S(1)}, f32[80,768]{1,0:T(8,128)S(1)}, u32[]{:S(2)}, u32[]{:S(2)}) collective-permute-start(f32[80,768]{1,0:T(8,128)S(1)} %get-tuple-element.28), channel_id=1, source_target_pairs={{48,0},{0,16},{16,32},{32,48},{49,1},{1,17},{17,33},{33,49},{50,2}... | collective-permute-start | bytes 737288 | tf_op jit(solution)/shard_map/ppermute | solution.py:18
  164.1 20.5 %all-to-all-start.3 = ((f32[8,128,128]{2,1,0:T(8,128)}), f32[8,128,128]{2,1,0:T(8,128)S(1)}, u32[]{:S(2)}, u32[]{:S(2)}) async-start(f32[8,128,128]{2,1,0:T(8,128)} %concatenate.78), calls=%async_computation.3 | async-start | bytes 1048576 | tf_op jit(solution)/shard_map/all_to_all | solution.py:134
  185.8 21.0 %all-to-all-start.4 = ((bf16[16,128,128]{2,1,0:T(8,128)(2,1)}), bf16[16,128,128]{2,1,0:T(8,128)(2,1)S(1)}, u32[]{:S(2)}, u32[]{:S(2)}) async-start(bf16[16,128,128]{2,1,0:T(8,128)(2,1)} %broadcast_in_dim.41), calls=%async_computation.4 | async-start | bytes 1048576 | tf_op jit(solution)/shard_map/all_to_all | solution.py:29
  (27 other events, 257.1 us)
